TPU v7x, 128 devices: a whole 4x4x4 slice. The times are simulated.
128 devices in a mesh: mem: 8 (over x_hi, y), lat: 16 (over x_lo, z, core).
Axes of the slice: x: 4 (x_hi: 2, x_lo: 2; x = x_hi * 2 + x_lo), y: 4, z: 4, core: 2. Of those that a mesh axis runs over, the one named last changes fastest.
Arguments:
- controls: float32 [48, 16, 16, 96], P('mem', None, 'lat'), may hold values from -6 to 6
- perturbations: bfloat16 [48, 64, 64, 384], P('mem', None, 'lat'), may hold values from -0.875 to 0.875
- precision_weight: bfloat16 [64, 256, 1536], P(None, 'lat'), may hold values from 0.25 to 4
- north_coef: float32 [256, 1536], P('lat'), may hold values from 0.02 to 0.24
- east_coef: float32 [256, 1536], P('lat'), may hold values from 0.02 to 0.24
- fine_source: int32 [256], P('lat'), may hold values from 0 to 62, as said below
- fine_frac: float32 [256], P('lat'), may hold values from 0 to 1
Outputs:
- gradient: float32 [48, 16, 16, 96], P('mem', None, 'lat')
Inputs may be any that keep to these rules, and one draw needn't show every extreme that they name: Fine row f lies in band b = f // 16; its source rows fine_source[f] and fine_source[f] + 1 satisfy max(b * 4 - 4, 0) <= fine_source[f] <= min((b + 1) * 4 + 2, 62), and both ends are reached in every band.
All inputs are finite; a program needn't handle non-finite values.
Results may differ from a plain program's by a relative error of at most 0.0003.
Values sent between devices are 32-bit elements; how exact they have to be, the bound alone decides.
No kernel may reach another device: no remote copies, remote signals or barrier semaphores. Data moves between devices by JAX's collectives and lax.ppermute only.
A program may use at most 128 MiB of HBM per device.

v0:
```python
import jax
import jax.numpy as jnp
from jax import lax
from jax.sharding import PartitionSpec as P

PASSES = 5
REACH = 4


def with_halo(block, sides, width):
    for axis, dim in sides:
        count = lax.axis_size(axis)
        forward = [(i, i + 1) for i in range(count - 1)]
        backward = [(target, source) for source, target in forward]
        low = lax.ppermute(
            lax.slice_in_dim(block, block.shape[dim] - width, None, axis=dim), axis, forward
        )
        high = lax.ppermute(lax.slice_in_dim(block, 0, width, axis=dim), axis, backward)
        block = jnp.concatenate([low, block, high], axis=dim)
    return block


def in_blocks(value, dim, devices):
    before, after = (value.shape[:dim], value.shape[dim + 1 :])
    return jnp.moveaxis(value.reshape(*before, devices, -1, *after), dim, 0)


def sum_at_owner(value, axis, dim):
    parts = in_blocks(value, dim, lax.axis_size(axis))
    arrived = lax.all_to_all(parts, axis, split_axis=0, concat_axis=0, tiled=True)
    return arrived.sum(axis=0)


def copy_for_each(value, axis):
    devices = lax.axis_size(axis)
    return lax.all_to_all(
        jnp.broadcast_to(value[None], (devices, *value.shape)), axis, 0, 0, tiled=True
    )


def joined_along(parts, dim):
    shape = list(parts.shape[1:])
    shape[dim] *= parts.shape[0]
    return jnp.moveaxis(parts, 0, dim).reshape(shape)


def gathered_copies(value, axis, dim):
    parts = copy_for_each(value, axis)
    return joined_along(parts, dim)


def refine(padded, dimension):
    count = padded.shape[dimension] - 2
    previous = lax.slice_in_dim(padded, 0, count, axis=dimension)
    current = lax.slice_in_dim(padded, 1, count + 1, axis=dimension)
    following = lax.slice_in_dim(padded, 2, count + 2, axis=dimension)
    phases = [
        0.375 * previous + 0.625 * current,
        0.125 * previous + 0.875 * current,
        0.875 * current + 0.125 * following,
        0.625 * current + 0.375 * following,
    ]
    stacked = jnp.stack(phases, axis=dimension + 1)
    new_shape = list(padded.shape)
    new_shape[dimension] = 4 * count
    return stacked.reshape(new_shape)


def raise_padded(padded):
    field = refine(jnp.pad(padded, ((0, 0), (1, 1), (0, 0), (0, 0)), mode="edge"), 1)
    field = refine(jnp.pad(field, ((0, 0), (0, 0), (0, 0), (1, 1)), mode="wrap"), 3)
    return refine(field, 2)


def diffuse(padded, north_pad, east_rows):
    center = padded[:, 1:-1]
    upward = north_pad[1:-1] * (padded[:, 2:] - center)
    downward = north_pad[:-2] * (padded[:, :-2] - center)
    eastward = east_rows * (jnp.roll(center, -1, 2) - center)
    westward = jnp.roll(east_rows, 1, 1) * (jnp.roll(center, 1, 2) - center)
    return center + upward + downward + eastward + westward


def body(controls, perturbations, precision_weight, north_coef, east_coef, fine_source, fine_frac):
    lat_index = lax.axis_index("lat")
    lat_count = lax.axis_size("lat")
    band_rows = north_coef.shape[0]
    total_rows = band_rows * lat_count
    control_pad = with_halo(controls, (("lat", 2),), 1)

    def raise_local(padded):
        first = jnp.where(lat_index == 0, padded[:, :, 1:2], padded[:, :, 0:1])
        last = jnp.where(lat_index == lat_count - 1, padded[:, :, -2:-1], padded[:, :, -1:])
        fixed = jnp.concatenate([first, padded[:, :, 1:-1], last], axis=2)
        return raise_padded(fixed)

    raised, pull_up = jax.vjp(raise_local, control_pad)
    local_sum = jnp.sum(perturbations * raised, axis=0)
    level_part = local_sum.shape[0] // lax.axis_size("mem")
    increment = sum_at_owner(local_sum, "mem", 0)
    weight = lax.dynamic_slice_in_dim(
        precision_weight, lax.axis_index("mem") * level_part, level_part, 0
    )
    coef_stack = jnp.stack([north_coef, east_coef], axis=0)
    coef_pad = with_halo(coef_stack, (("lat", 1),), PASSES)

    def smooth(field):
        padded = with_halo(field, (("lat", 1),), PASSES)
        for repeat in range(PASSES):
            count = padded.shape[1]
            north_slice = coef_pad[0, repeat : repeat + count]
            east_slice = coef_pad[1, repeat + 1 : repeat + count - 1]
            padded = diffuse(padded, north_slice, east_slice)
            global_rows = (
                lat_index * band_rows - PASSES + repeat + 1 + jnp.arange(count - 2, dtype=jnp.int32)
            )
            inside = (global_rows >= 0) & (global_rows < total_rows)
            padded = jnp.where(inside[None, :, None], padded, 0.0)
        return padded

    mid_pad = with_halo(increment, (("lat", 1),), REACH)
    local_source = fine_source - (lat_index * increment.shape[1] - REACH)

    def to_fine(padded):
        lower_rows = jnp.take(padded, local_source, axis=1)
        upper_rows = jnp.take(padded, local_source + 1, axis=1)
        fraction = fine_frac[:, None]
        blended = (1.0 - fraction) * lower_rows + fraction * upper_rows
        return refine(jnp.pad(blended, ((0, 0), (0, 0), (1, 1)), mode="wrap"), 2)

    fine_grid, pull_fine = jax.vjp(to_fine, mid_pad)
    weighted = weight.astype(jnp.float32) * smooth(fine_grid)
    grad_mid = pull_fine(smooth(weighted))[0]
    mid_ghosts = jnp.concatenate([grad_mid[:, :REACH], grad_mid[:, -REACH:]], axis=1)
    mid_received = with_halo(mid_ghosts, (("lat", 1),), REACH)
    fine_adjoint = grad_mid[:, REACH:-REACH]
    fine_adjoint = fine_adjoint.at[:, :REACH].add(mid_received[:, :REACH])
    fine_adjoint = fine_adjoint.at[:, -REACH:].add(mid_received[:, -REACH:])
    fine_adjoint = gathered_copies(fine_adjoint, "mem", 0)
    member_adjoint = perturbations * fine_adjoint[None]
    grad_pad = pull_up(member_adjoint)[0]
    control_ghosts = jnp.concatenate([grad_pad[:, :, :1], grad_pad[:, :, -1:]], axis=2)
    control_received = with_halo(control_ghosts, (("lat", 2),), 1)
    owned = grad_pad[:, :, 1:-1]
    owned = owned.at[:, :, 0].add(control_received[:, :, 0])
    owned = owned.at[:, :, -1].add(control_received[:, :, -1])
    return controls + owned


def solution(mesh):
    in_specs = (
        P("mem", None, "lat", None),
        P("mem", None, "lat", None),
        P(None, "lat", None),
        P("lat", None),
        P("lat", None),
        P("lat"),
        P("lat"),
    )
    out_specs = P("mem", None, "lat", None)
    return jax.shard_map(body, mesh=mesh, in_specs=in_specs, out_specs=out_specs, check_vma=False)
```

profile of v0, /device:TPU:97, one launch (start us, length us, event | category | flops | bytes accessed | tf_op | source)
XLA Modules:
  0.0 207.7 jit_solution(9207637475503221896)
XLA Ops:
  6.3 5.5 %collective-permute-start.6 = (f32[2,5,1536]{2,1,0:T(8,128)}, f32[2,5,1536]{2,1,0:T(8,128)S(1)}, u32[]{:S(2)}, u32[]{:S(2)}) collective-permute-start(f32[2,5,1536]{2,1,0:T(8,128)} %get-tuple-element.176), channel_id=1, source_target_pairs={{0,1},{1,2},{2,3},{3,4},{4,5},{5,6},{6,7},{7,8},{8,9},{9,10},{10,1... | collective-permute-start | bytes 184328 | tf_op jit(solution)/shard_map/ppermute | solution.py:15
  21.2 2.8 %copy.427 = bf16[6,64,4,384]{1,3,0,2:T(8,128)(2,1)S(1)} copy(bf16[6,64,4,384]{3,2,1,0:T(4,128)(2,1)} %param.22) | data formatting | bytes 2359296 | tf_op args[1]
  28.1 4.6 %copy.436 = f32[6,64,3,96,4]{1,4,3,2,0:T(4,128)} copy(f32[6,64,3,96,4]{3,1,2,0,4:T(8,128)} %pad_maximum_fusion) | data formatting | bytes 3538944 | tf_op jit(solution)/shard_map/jvp()/stack | solution.py:63
  32.7 2.6 %add_bitcast_fusion.4 = (f32[6,64,1,1,384]{1,4,0,3,2:T(8,128)S(1)}, f32[6,64,1,1,384]{1,4,0,3,2:T(8,128)S(1)}, f32[6,64,1,1,384]{1,4,0,3,2:T(8,128)S(1)}) fusion(f32[6,64,3,384]{1,3,2,0:T(8,128)} %bitcast.174), kind=kLoop, calls=%fused_computation.63 | loop fusion | flops 1179648 | bytes 3538944 | tf_op jit(solution)/shard_map/jvp()/stack | solution.py:63
  40.0 6.4 %all-to-all-start = ((f32[8,8,4,384]{3,1,2,0:T(8,128)}), f32[8,8,4,384]{3,1,2,0:T(8,128)S(1)}, u32[]{:S(2)}, u32[]{:S(2)}) async-start(f32[8,8,4,384]{3,1,2,0:T(8,128)} %copy.443), calls=%async_computation | async-start | bytes 786432 | tf_op jit(solution)/shard_map/all_to_all | solution.py:30
  51.8 3.0 %all-to-all-done = f32[8,8,4,384]{3,1,2,0:T(8,128)S(1)} async-done(((f32[8,8,4,384]{3,1,2,0:T(8,128)}), f32[8,8,4,384]{3,1,2,0:T(8,128)S(1)}, u32[]{:S(2)}, u32[]{:S(2)}) %all-to-all-start) | async-done | bytes 393248 | tf_op jit(solution)/shard_map/all_to_all | solution.py:30
  54.8 6.2 %collective-permute-start.2 = (f32[8,4,384]{2,0,1:T(8,128)S(1)}, f32[8,4,384]{2,0,1:T(8,128)S(1)}, u32[]{:S(2)}, u32[]{:S(2)}) collective-permute-start(f32[8,4,384]{2,0,1:T(8,128)S(1)} %reduce_sum.22), channel_id=1, source_target_pairs={{0,1},{1,2},{2,3},{3,4},{4,5},{5,6},{6,7},{7,8},{8,9},{9,10},{10,1... | collective-permute-start | bytes 147464 | tf_op jit(solution)/shard_map/ppermute | solution.py:15
  63.8 4.8 %collective-permute-done.3 = f32[8,4,384]{2,0,1:T(8,128)S(1)} collective-permute-done((f32[8,4,384]{2,0,1:T(8,128)S(1)}, f32[8,4,384]{2,0,1:T(8,128)S(1)}, u32[]{:S(2)}, u32[]{:S(2)}) %collective-permute-start.3) | collective-permute-done | bytes 49184 | tf_op jit(solution)/shard_map/ppermute | solution.py:18
  70.3 5.9 %copy.444 = f32[8,16,384,4]{1,0,3,2:T(8,128)} copy(f32[8,16,384,4]{2,0,1,3:T(8,128)S(1)} %pad_maximum_fusion.11) | data formatting | bytes 1572864 | tf_op jit(solution)/shard_map/jvp()/stack | solution.py:63
  76.2 10.0 %fusion.120 = (f32[8,5,1536]{1,0,2:T(8,128)}, f32[8,5,1536]{1,0,2:T(8,128)}) fusion(f32[8,16,1536]{1,0,2:T(8,128)} %bitcast.171), kind=kLoop, calls=%fused_computation.279 | loop fusion | bytes 983040 | tf_op jit(solution)/shard_map/slice | solution.py:16
  86.2 4.5 %copy.445 = f32[8,5,1536]{2,0,1:T(8,128)S(1)} copy(f32[8,5,1536]{1,0,2:T(8,128)} %get-tuple-element.85) | data formatting | bytes 491520 | tf_op jit(solution)/shard_map/slice | solution.py:16
  92.6 4.5 %copy.446 = f32[8,5,1536]{2,0,1:T(8,128)S(1)} copy(f32[8,5,1536]{1,0,2:T(8,128)} %get-tuple-element.86) | data formatting | bytes 491520 | tf_op jit(solution)/shard_map/slice | solution.py:18
  97.1 2.6 %collective-permute-start.5 = (f32[8,5,1536]{2,0,1:T(8,128)S(1)}, f32[8,5,1536]{2,0,1:T(8,128)}, u32[]{:S(2)}, u32[]{:S(2)}) collective-permute-start(f32[8,5,1536]{2,0,1:T(8,128)S(1)} %copy.446), channel_id=1, source_target_pairs={{1,0},{2,1},{3,2},{4,3},{5,4},{6,5},{7,6},{8,7},{9,8},{10,9},{11,1... | collective-permute-start | bytes 737288 | tf_op jit(solution)/shard_map/ppermute | solution.py:18
  101.2 4.5 %copy.447 = f32[8,16,1536]{2,0,1:T(8,128)S(1)} copy(f32[8,16,1536]{1,0,2:T(8,128)} %bitcast.172) | data formatting | bytes 1572864 | tf_op jit(solution)/shard_map/jvp()/reshape | solution.py:66
  118.3 4.5 %collective-permute-start.8 = (f32[8,5,1536]{2,0,1:T(8,128)S(1)}, f32[8,5,1536]{2,0,1:T(8,128)S(1)}, u32[]{:S(2)}, u32[]{:S(2)}) collective-permute-start(f32[8,5,1536]{2,0,1:T(8,128)S(1)} %get-tuple-element.140), channel_id=1, source_target_pairs={{0,1},{1,2},{2,3},{3,4},{4,5},{5,6},{6,7},{7,8},{8,9},{9,10},{10,1... | collective-permute-start | bytes 737288 | tf_op jit(solution)/shard_map/ppermute | solution.py:15
  125.9 6.5 %collective-permute-done.9 = f32[8,5,1536]{2,0,1:T(8,128)S(1)} collective-permute-done((f32[8,5,1536]{2,0,1:T(8,128)S(1)}, f32[8,5,1536]{2,0,1:T(8,128)S(1)}, u32[]{:S(2)}, u32[]{:S(2)}) %collective-permute-start.9) | collective-permute-done | bytes 245792 | tf_op jit(solution)/shard_map/ppermute | solution.py:18
  139.5 4.0 %copy.448 = f32[8,16,1536]{1,0,2:T(8,128)} copy(f32[8,16,1536]{2,0,1:T(8,128)S(1)} %fusion.92) | data formatting | bytes 1572864 | tf_op jit(solution)/shard_map/jit(_where)/select_n | solution.py:118
  143.6 5.1 %fusion.119 = (f32[8,16,384,1]{1,0,3,2:T(8,128)}, f32[8,16,384,1]{1,0,3,2:T(8,128)S(1)}, f32[8,16,384,1]{1,0,3,2:T(8,128)}, f32[8,16,384,1]{1,0,3,2:T(8,128)S(1)}) fusion(f32[8,16,384,4]{1,0,3,2:T(8,128)} %bitcast.173), kind=kLoop, calls=%fused_computation.278 | loop fusion | bytes 1572864 | tf_op jit(solution)/shard_map/transpose(jvp())/unstack | solution.py:63
  162.2 5.6 %collective-permute-done.11 = f32[8,4,384]{2,0,1:T(8,128)S(1)} collective-permute-done((f32[8,4,384]{2,0,1:T(8,128)S(1)}, f32[8,4,384]{2,0,1:T(8,128)S(1)}, u32[]{:S(2)}, u32[]{:S(2)}) %collective-permute-start.11) | collective-permute-done | bytes 49184 | tf_op jit(solution)/shard_map/ppermute | solution.py:18
  167.9 11.5 %all_to_all.10 = f32[8,8,4,384]{3,1,2,0:T(8,128)S(1)} all-to-all(f32[8,8,4,384]{3,1,2,0:T(8,128)S(1)} %broadcast_in_dim.163), channel_id=1, replica_groups=mesh['mem'=8,'lat'=16] {'mem'}, dimensions={0} | all-to-all | bytes 786432 | tf_op jit(solution)/shard_map/all_to_all | solution.py:36
  181.1 3.9 %fusion.121 = (f32[6,64,3,96,1]{1,4,3,0,2:T(1,128)}, f32[6,64,3,96,1]{1,4,3,0,2:T(1,128)S(1)}, f32[6,64,3,96,1]{1,4,3,0,2:T(1,128)S(1)}, f32[6,64,3,96,1]{1,4,3,0,2:T(1,128)S(1)}) fusion(f32[6,64,3,96,4]{1,4,3,0,2:T(4,128)S(1)} %bitcast.176), kind=kLoop, calls=%fused_computation.280 | loop fusion | bytes 3538944 | tf_op jit(solution)/shard_map/transpose(jvp())/unstack | solution.py:63
  185.0 3.0 %copy.478 = f32[6,64,3,96,1]{3,1,4,2,0:T(8,128)} copy(f32[6,64,3,96,1]{1,4,3,0,2:T(1,128)} %get-tuple-element.90) | data formatting | bytes 884736
  196.7 2.8 %collective-permute-start.12 = (f32[6,16,1,96]{3,1,2,0:T(8,128)S(1)}, f32[6,16,1,96]{3,1,2,0:T(8,128)S(1)}, u32[]{:S(2)}, u32[]{:S(2)}) collective-permute-start(f32[6,16,1,96]{3,1,2,0:T(8,128)S(1)} %get-tuple-element.186), channel_id=1, source_target_pairs={{0,1},{1,2},{2,3},{3,4},{4,5},{5,6},{6,7},{7,8},{8,9},{9,10},{10,1... | collective-permute-start | bytes 110600 | tf_op jit(solution)/shard_map/ppermute | solution.py:15
  201.5 5.6 %collective-permute-done.13 = f32[6,16,1,96]{3,1,2,0:T(8,128)S(1)} collective-permute-done((f32[6,16,1,96]{3,1,2,0:T(8,128)S(1)}, f32[6,16,1,96]{3,1,2,0:T(8,128)S(1)}, u32[]{:S(2)}, u32[]{:S(2)}) %collective-permute-start.13) | collective-permute-done | bytes 36896 | tf_op jit(solution)/shard_map/ppermute | solution.py:18
  (239 shorter events, 86.1 us)
Async XLA Ops:
  0.0 19.6 %copy-start = (bf16[64,16,1536]{2,1,0:T(8,128)(2,1)S(1)}, bf16[64,16,1536]{2,1,0:T(8,128)(2,1)}, u32[]{:S(2)}) copy-start(bf16[64,16,1536]{2,1,0:T(8,128)(2,1)} %param.23) | copy-start | bytes 9437188
  0.0 20.4 %copy-start.6 = (f32[16,1536]{1,0:T(8,128)S(1)}, f32[16,1536]{1,0:T(8,128)}, u32[]{:S(2)}) copy-start(f32[16,1536]{1,0:T(8,128)} %param.25) | copy-start | bytes 294916
  0.0 24.0 %collective-permute-start = (f32[6,16,1,96]{3,1,2,0:T(8,128)}, f32[6,16,1,96]{3,1,2,0:T(8,128)}, u32[]{:S(2)}, u32[]{:S(2)}) collective-permute-start(f32[6,16,1,96]{3,1,2,0:T(8,128)} %bitcast.199), channel_id=1, source_target_pairs={{0,1},{1,2},{2,3},{3,4},{4,5},{5,6},{6,7},{7,8},{8,9},{9,10},{10,1... | collective-permute-start | bytes 110600 | tf_op jit(solution)/shard_map/ppermute | solution.py:15
  2.6 21.5 %collective-permute-start.1 = (f32[6,16,1,96]{3,1,2,0:T(8,128)}, f32[6,16,1,96]{3,1,2,0:T(8,128)}, u32[]{:S(2)}, u32[]{:S(2)}) collective-permute-start(f32[6,16,1,96]{3,1,2,0:T(8,128)} %bitcast.200), channel_id=1, source_target_pairs={{1,0},{2,1},{3,2},{4,3},{5,4},{6,5},{7,6},{8,7},{9,8},{10,9},{11,1... | collective-permute-start | bytes 110600 | tf_op jit(solution)/shard_map/ppermute | solution.py:18
  6.3 40.0 %collective-permute-start.6 = (f32[2,5,1536]{2,1,0:T(8,128)}, f32[2,5,1536]{2,1,0:T(8,128)S(1)}, u32[]{:S(2)}, u32[]{:S(2)}) collective-permute-start(f32[2,5,1536]{2,1,0:T(8,128)} %get-tuple-element.176), channel_id=1, source_target_pairs={{0,1},{1,2},{2,3},{3,4},{4,5},{5,6},{6,7},{7,8},{8,9},{9,10},{10,1... | collective-permute-start | bytes 184328 | tf_op jit(solution)/shard_map/ppermute | solution.py:15
  11.8 34.6 %collective-permute-start.7 = (f32[2,5,1536]{2,1,0:T(8,128)S(1)}, f32[2,5,1536]{2,1,0:T(8,128)S(1)}, u32[]{:S(2)}, u32[]{:S(2)}) collective-permute-start(f32[2,5,1536]{2,1,0:T(8,128)S(1)} %get-tuple-element.177), channel_id=1, source_target_pairs={{1,0},{2,1},{3,2},{4,3},{5,4},{6,5},{7,6},{8,7},{9,8},{10,9},{11,1... | collective-permute-start | bytes 184328 | tf_op jit(solution)/shard_map/ppermute | solution.py:18
  24.0 11.9 %copy-start.3 = (bf16[6,64,4,384]{1,3,0,2:T(8,128)(2,1)}, bf16[6,64,4,384]{1,3,0,2:T(8,128)(2,1)S(1)}, u32[]{:S(2)}) copy-start(bf16[6,64,4,384]{1,3,0,2:T(8,128)(2,1)S(1)} %copy.427) | copy-start | bytes 3538948
  40.0 14.8 %all-to-all-start = ((f32[8,8,4,384]{3,1,2,0:T(8,128)}), f32[8,8,4,384]{3,1,2,0:T(8,128)S(1)}, u32[]{:S(2)}, u32[]{:S(2)}) async-start(f32[8,8,4,384]{3,1,2,0:T(8,128)} %copy.443), calls=%async_computation | async-start | bytes 786432 | tf_op jit(solution)/shard_map/all_to_all | solution.py:30
  48.5 65.2 %copy-start.15 = (f32[20,1536]{1,0:T(8,128)}, f32[20,1536]{1,0:T(8,128)S(1)}, u32[]{:S(2)}) copy-start(f32[20,1536]{1,0:T(8,128)S(1)} %get-tuple-element.161) | copy-start | bytes 368644
  48.5 65.2 %copy-start.17 = (f32[20,1536]{1,0:T(8,128)}, f32[20,1536]{1,0:T(8,128)S(1)}, u32[]{:S(2)}) copy-start(f32[20,1536]{1,0:T(8,128)S(1)} %get-tuple-element.163) | copy-start | bytes 368644
  51.1 18.6 %copy-start.40 = (pred[16]{0:T(512)(128)(4,1)S(1)}, pred[16]{0:T(512)(128)(4,1)}, u32[]{:S(2)}) copy-start(pred[16]{0:T(512)(128)(4,1)} %get-tuple-element.79) | copy-start | bytes 52
  51.1 18.6 %copy-start.41 = (pred[16]{0:T(512)(128)(4,1)S(1)}, pred[16]{0:T(512)(128)(4,1)}, u32[]{:S(2)}) copy-start(pred[16]{0:T(512)(128)(4,1)} %get-tuple-element.199) | copy-start | bytes 52
  51.1 18.6 %copy-start.42 = (f32[16]{0:T(128)S(1)}, f32[16]{0:T(128)}, u32[]{:S(2)}) copy-start(f32[16]{0:T(128)} %param.27) | copy-start | bytes 196
  51.1 18.6 %copy-start.44 = (f32[16]{0:T(128)S(1)}, f32[16]{0:T(128)}, u32[]{:S(2)}) copy-start(f32[16]{0:T(128)} %broadcast_subtract_fusion) | copy-start | bytes 196
  54.8 8.9 %collective-permute-start.2 = (f32[8,4,384]{2,0,1:T(8,128)S(1)}, f32[8,4,384]{2,0,1:T(8,128)S(1)}, u32[]{:S(2)}, u32[]{:S(2)}) collective-permute-start(f32[8,4,384]{2,0,1:T(8,128)S(1)} %reduce_sum.22), channel_id=1, source_target_pairs={{0,1},{1,2},{2,3},{3,4},{4,5},{5,6},{6,7},{7,8},{8,9},{9,10},{10,1... | collective-permute-start | bytes 147464 | tf_op jit(solution)/shard_map/ppermute | solution.py:15
  61.1 7.5 %collective-permute-start.3 = (f32[8,4,384]{2,0,1:T(8,128)S(1)}, f32[8,4,384]{2,0,1:T(8,128)S(1)}, u32[]{:S(2)}, u32[]{:S(2)}) collective-permute-start(f32[8,4,384]{2,0,1:T(8,128)S(1)} %reduce_sum.22), channel_id=1, source_target_pairs={{1,0},{2,1},{3,2},{4,3},{5,4},{6,5},{7,6},{8,7},{9,8},{10,9},{11,1... | collective-permute-start | bytes 147464 | tf_op jit(solution)/shard_map/ppermute | solution.py:18
  90.7 15.1 %collective-permute-start.4 = (f32[8,5,1536]{2,0,1:T(8,128)S(1)}, f32[8,5,1536]{2,0,1:T(8,128)S(1)}, u32[]{:S(2)}, u32[]{:S(2)}) collective-permute-start(f32[8,5,1536]{2,0,1:T(8,128)S(1)} %copy.445), channel_id=1, source_target_pairs={{0,1},{1,2},{2,3},{3,4},{4,5},{5,6},{6,7},{7,8},{8,9},{9,10},{10,1... | collective-permute-start | bytes 737288 | tf_op jit(solution)/shard_map/ppermute | solution.py:15
  97.1 9.7 %collective-permute-start.5 = (f32[8,5,1536]{2,0,1:T(8,128)S(1)}, f32[8,5,1536]{2,0,1:T(8,128)}, u32[]{:S(2)}, u32[]{:S(2)}) collective-permute-start(f32[8,5,1536]{2,0,1:T(8,128)S(1)} %copy.446), channel_id=1, source_target_pairs={{1,0},{2,1},{3,2},{4,3},{5,4},{6,5},{7,6},{8,7},{9,8},{10,9},{11,1... | collective-permute-start | bytes 737288 | tf_op jit(solution)/shard_map/ppermute | solution.py:18
  118.3 7.7 %collective-permute-start.8 = (f32[8,5,1536]{2,0,1:T(8,128)S(1)}, f32[8,5,1536]{2,0,1:T(8,128)S(1)}, u32[]{:S(2)}, u32[]{:S(2)}) collective-permute-start(f32[8,5,1536]{2,0,1:T(8,128)S(1)} %get-tuple-element.140), channel_id=1, source_target_pairs={{0,1},{1,2},{2,3},{3,4},{4,5},{5,6},{6,7},{7,8},{8,9},{9,10},{10,1... | collective-permute-start | bytes 737288 | tf_op jit(solution)/shard_map/ppermute | solution.py:15
  122.8 9.6 %collective-permute-start.9 = (f32[8,5,1536]{2,0,1:T(8,128)S(1)}, f32[8,5,1536]{2,0,1:T(8,128)S(1)}, u32[]{:S(2)}, u32[]{:S(2)}) collective-permute-start(f32[8,5,1536]{2,0,1:T(8,128)S(1)} %get-tuple-element.141), channel_id=1, source_target_pairs={{1,0},{2,1},{3,2},{4,3},{5,4},{6,5},{7,6},{8,7},{9,8},{10,9},{11,1... | collective-permute-start | bytes 737288 | tf_op jit(solution)/shard_map/ppermute | solution.py:18
  157.9 4.3 %collective-permute-start.10 = (f32[8,4,384]{2,0,1:T(8,128)S(1)}, f32[8,4,384]{2,0,1:T(8,128)S(1)}, u32[]{:S(2)}, u32[]{:S(2)}) collective-permute-start(f32[8,4,384]{2,0,1:T(8,128)S(1)} %get-tuple-element.193), channel_id=1, source_target_pairs={{0,1},{1,2},{2,3},{3,4},{4,5},{5,6},{6,7},{7,8},{8,9},{9,10},{10,1... | collective-permute-start | bytes 147464 | tf_op jit(solution)/shard_map/ppermute | solution.py:15
  159.8 8.0 %collective-permute-start.11 = (f32[8,4,384]{2,0,1:T(8,128)S(1)}, f32[8,4,384]{2,0,1:T(8,128)S(1)}, u32[]{:S(2)}, u32[]{:S(2)}) collective-permute-start(f32[8,4,384]{2,0,1:T(8,128)S(1)} %get-tuple-element.194), channel_id=1, source_target_pairs={{1,0},{2,1},{3,2},{4,3},{5,4},{6,5},{7,6},{8,7},{9,8},{10,9},{11,1... | collective-permute-start | bytes 147464 | tf_op jit(solution)/shard_map/ppermute | solution.py:18
  196.7 4.8 %collective-permute-start.12 = (f32[6,16,1,96]{3,1,2,0:T(8,128)S(1)}, f32[6,16,1,96]{3,1,2,0:T(8,128)S(1)}, u32[]{:S(2)}, u32[]{:S(2)}) collective-permute-start(f32[6,16,1,96]{3,1,2,0:T(8,128)S(1)} %get-tuple-element.186), channel_id=1, source_target_pairs={{0,1},{1,2},{2,3},{3,4},{4,5},{5,6},{6,7},{7,8},{8,9},{9,10},{10,1... | collective-permute-start | bytes 110600 | tf_op jit(solution)/shard_map/ppermute | solution.py:15
  199.6 7.5 %collective-permute-start.13 = (f32[6,16,1,96]{3,1,2,0:T(8,128)S(1)}, f32[6,16,1,96]{3,1,2,0:T(8,128)S(1)}, u32[]{:S(2)}, u32[]{:S(2)}) collective-permute-start(f32[6,16,1,96]{3,1,2,0:T(8,128)S(1)} %get-tuple-element.187), channel_id=1, source_target_pairs={{1,0},{2,1},{3,2},{4,3},{5,4},{6,5},{7,6},{8,7},{9,8},{10,9},{11,1... | collective-permute-start | bytes 110600 | tf_op jit(solution)/shard_map/ppermute | solution.py:18
  (40 other events, 90.2 us)
where the time goes:
time: 209 us; the launch traced here: 208 us
  local copies, waits for them, and re-layouts  83.6 us (40%)
  starting transfers between devices  46.9 us (22%)
  other arithmetic  37 us (18%)
  waiting for transfers between devices  27.5 us (13%)
  blocking collectives  11.5 us (6%)
    ppermute x7, starting transfers between devices, with_halo(): lax.ppermute(lax.slice_in_dim(block, block.shape[dim] - width, None, axis...  25.5 us
    ppermute x7, waiting for transfers between devices, with_halo(): lax.ppermute(lax.slice_in_dim(block, 0, width, axis=dim), axis, backward)  23.5 us
    unnamed x107, local copies, waits for them, and re-layouts  22.4 us
    another operation x6, local copies, waits for them, and re-layouts, refine(): stacked = jnp.stack(phases, axis=dimension + 1)  20.3 us
    ppermute x7, starting transfers between devices, with_halo(): lax.ppermute(lax.slice_in_dim(block, 0, width, axis=dim), axis, backward)  15.1 us
    slice x3, local copies, waits for them, and re-layouts, with_halo(): lax.slice_in_dim(block, block.shape[dim] - width, None, axis=dim)  14.6 us
    all_to_all x1, blocking collectives, copy_for_each(): lax.all_to_all(jnp.broadcast_to(value[None], (devices, *value.shape)), ax...  11.5 us
    select_n x9, other arithmetic, smooth(): padded = jnp.where(inside[None, :, None], padded, 0.0)  8.74 us
  transfers between devices with their start and end apart: 15, of which 7 were waited for; matrix products, arithmetic and copies ran while one was open for 21% of the time, Pallas kernels for 0%

commit v1 on v0

v1 whole, which is shorter than its diff:
```python
import jax
import jax.numpy as jnp
import numpy as np
from jax import lax
from jax.experimental import pallas as pl
from jax.experimental.pallas import tpu as pltpu
from jax.sharding import PartitionSpec as P

PASSES = 5
REACH = 4
HALO = 2 * PASSES
F32 = jnp.float32
BF16 = jnp.bfloat16

PHASES = np.array(
    [[0.375, 0.625, 0.0], [0.125, 0.875, 0.0], [0.0, 0.875, 0.125], [0.0, 0.625, 0.375]]
)


def refine_matrix(count, periodic):
    matrix = np.zeros((4 * count, count), np.float32)
    for q in range(count):
        for r in range(4):
            for step in range(3):
                source = q + step - 1
                source = source % count if periodic else min(max(source, 0), count - 1)
                matrix[4 * q + r, source] += PHASES[r, step]
    return matrix


def split2(x):
    hi = x.astype(BF16)
    lo = (x - hi.astype(F32)).astype(BF16)
    return hi, lo


def dot(a, b):
    return jnp.dot(a, b, preferred_element_type=F32)


def prepare_kernel(place, weight, north, east, extra, select, order, coef, own_weight, buf_a, buf_b):
    odd = place[0] % 2
    levels, rows, lon = weight.shape
    stacked = jnp.concatenate([north[...], east[...]], axis=0)
    hi, rest = stacked.astype(BF16), None
    rest = stacked - hi.astype(F32)
    mid = rest.astype(BF16)
    low = (rest - mid.astype(F32)).astype(BF16)
    sel = select[...]
    values = dot(order[...], weight[...].reshape(levels * rows, lon)).astype(BF16)
    quarter = lon // 4
    for c in range(lon // 512):
        cut = slice(512 * c, 512 * c + 512)
        cpart = dot(hi[:, cut], sel) + dot(mid[:, cut], sel) + dot(low[:, cut], sel)
        wpart = dot(values[:, cut], sel)
        for r in range(4):
            to = slice(quarter * r + 128 * c, quarter * r + 128 * c + 128)
            frm = slice(128 * r, 128 * r + 128)
            coef[:, to] = cpart[:, frm]
            own_weight[:, :, to] = wpart[:, frm].reshape(rows, levels, 128)

    def fill(buf, upper):
        first = rows - PASSES if upper else 0
        for k in range(PASSES):
            buf[8 * k : 8 * k + 8, :] = own_weight[first + k]
        first = rows - HALO if upper else 0
        base = 8 * PASSES
        buf[base : base + HALO, :] = coef[first : first + HALO, :]
        buf[base + HALO : base + 2 * HALO, :] = coef[rows + first : rows + first + HALO, :]
        buf[base + 2 * HALO :, :] = extra[...]

    @pl.when(odd == 0)
    def _():
        fill(buf_a, True)
        fill(buf_b, False)

    @pl.when(odd == 1)
    def _():
        fill(buf_a, False)
        fill(buf_b, True)


def assemble_kernel(place, coef, own_weight, got_a, got_b, north, east, west, weight):
    lat = place[0]
    odd = lat % 2
    rows = own_weight.shape[0]
    quarter = coef.shape[1] // 4

    def put(i, nrow, erow):
        shape = (8, coef.shape[1])
        north[i] = jnp.broadcast_to(nrow, shape)
        spread = jnp.broadcast_to(erow, shape)
        east[i] = spread
        west[i] = pltpu.roll(spread[:, 3 * quarter :], 1, axis=1)

    for k in range(rows):
        put(HALO + k, coef[k : k + 1, :], coef[rows + k : rows + k + 1, :])
        weight[PASSES + k] = own_weight[k]

    def side(buf, start, wstart):
        base = 8 * PASSES
        for k in range(HALO):
            put(start + k, buf[base + k : base + k + 1, :], buf[base + HALO + k : base + HALO + k + 1, :])
        for k in range(PASSES):
            weight[wstart + k] = buf[8 * k : 8 * k + 8, :]

    @pl.when(odd == 0)
    def _():
        side(got_b, 0, 0)
        side(got_a, HALO + rows, PASSES + rows)

    @pl.when(odd == 1)
    def _():
        side(got_a, 0, 0)
        side(got_b, HALO + rows, PASSES + rows)

    @pl.when(lat == 0)
    def _():
        north[HALO - 1] = jnp.zeros(north.shape[1:], F32)


def raise_kernel(place, own, got_a, got_b, pert, lon_up, mix, out, x, acc):
    lat, last = place[0], place[1] - 1
    odd = lat % 2
    members = pert.shape[0]
    lev = own.shape[0] // members

    def put(step, ref):
        for m in range(members):
            at = (3 * m + step) * lev
            x[at : at + lev, :] = ref[m * lev : m * lev + lev, :]

    put(1, own)

    @pl.when(lat == 0)
    def _():
        put(0, own)

    @pl.when((lat > 0) & (odd == 0))
    def _():
        put(0, got_b)

    @pl.when(odd == 1)
    def _():
        put(0, got_a)

    @pl.when(lat == last)
    def _():
        put(2, own)

    @pl.when((lat < last) & (odd == 1))
    def _():
        put(2, got_b)

    @pl.when(odd == 0)
    def _():
        put(2, got_a)

    hi, lo = split2(x[...])
    wide = dot(hi, lon_up[...]) + dot(lo, lon_up[...])
    for m in range(members):
        hi, lo = split2(wide[3 * lev * m : 3 * lev * (m + 1), :])
        field = dot(mix[...], jnp.concatenate([hi, lo], axis=0))
        term = field * pert[m].astype(F32)
        if m == 0:
            acc[...] = term
        elif m < members - 1:
            acc[...] += term
        else:
            out[...] = (acc[...] + term).reshape(out.shape)


def total_kernel(parts, out, sums):
    count, n, lon = parts.shape
    total = parts[0]
    for k in range(1, count):
        total = total + parts[k]
    rows = n // 8
    for c in range(lon // 128):
        lanes = slice(128 * c, 128 * c + 128)
        sums[n * c : n * c + n, :] = total[:, lanes]
        for row in range(rows):
            out[8 * row : 8 * row + 8, lanes] = sums[pl.ds(n * c + row, 8, stride=rows), :]


def fine_kernel(
    place, source, frac, extra_a, extra_b, own, mate, up_pair, down_pair,
    north, east, west, weight, keep, send_a, send_b, mid, v, acc,
):
    lat, last = place[0], place[1] - 1
    odd = lat % 2
    lon = own.shape[1]
    rows = source.shape[0]
    n = rows + 2 * HALO
    band = own.shape[0] // 8

    def bring(slot, ref, start):
        for k in range(band):
            mid[slot * band + k] = ref[start + 8 * k : start + 8 * k + 8, :]

    half = own.shape[0]
    bring(2, own, 0)

    @pl.when(odd == 0)
    def _():
        bring(0, up_pair, 0)
        bring(1, up_pair, half)
        bring(3, mate, 0)
        bring(4, down_pair, 0)

    @pl.when(odd == 1)
    def _():
        bring(0, up_pair, 0)
        bring(1, mate, 0)
        bring(3, down_pair, half)
        bring(4, down_pair, 0)

    origin = (lat - 2) * band
    for i in range(n):
        k = i - HALO
        if k < 0:
            k += rows
            f = jnp.where(odd == 1, extra_a[0, k], extra_b[0, k])
            s = jnp.where(odd == 1, extra_a[0, rows + k], extra_b[0, rows + k]).astype(jnp.int32)
            valid = jnp.where(lat > 0, 1.0, 0.0)
        elif k >= rows:
            k -= rows
            f = jnp.where(odd == 0, extra_a[0, k], extra_b[0, k])
            s = jnp.where(odd == 0, extra_a[0, rows + k], extra_b[0, rows + k]).astype(jnp.int32)
            valid = jnp.where(lat < last, 1.0, 0.0)
        else:
            f, s, valid = frac[k], source[k], None
        s = jnp.clip(s - origin, 0, 5 * band - 2)
        below, above = 1.0 - f, f
        if valid is not None:
            below, above = below * valid, above * valid
        cur = below * mid[s] + above * mid[s + 1]
        prev = pltpu.roll(cur, 1, axis=1)
        nxt = pltpu.roll(cur, lon - 1, axis=1)
        v[i, :, 0:lon] = 0.375 * prev + 0.625 * cur
        v[i, :, lon : 2 * lon] = 0.125 * prev + 0.875 * cur
        v[i, :, 2 * lon : 3 * lon] = 0.875 * cur + 0.125 * nxt
        v[i, :, 3 * lon : 4 * lon] = 0.625 * cur + 0.375 * nxt

    inside_top = jnp.where(lat < last, 1.0, 0.0)

    def cut(r):
        return slice(r * lon, r * lon + lon)

    def sweep(first, stop):
        def flux(i, here, there):
            return [north[i, :, cut(r)] * (there[r] - here[r]) for r in range(4)]

        before = [v[first - 1, :, cut(r)] for r in range(4)]
        here = [v[first, :, cut(r)] for r in range(4)]
        low = flux(first - 1, before, here)
        for i in range(first, stop):
            there = [v[i + 1, :, cut(r)] for r in range(4)]
            high = flux(i, here, there)
            if i == HALO + rows:
                low = [inside_top * x for x in low]
            right = pltpu.roll(here[0], lon - 1, axis=1)
            left = pltpu.roll(here[3], 1, axis=1)
            side = [
                east[i, :, cut(r)] * ((here[r + 1] if r < 3 else right) - here[r]) for r in range(4)
            ]
            back = [west[i] * (here[0] - left)] + side[:3]
            for r in range(4):
                v[i, :, cut(r)] = here[r] + ((high[r] - low[r]) + (side[r] - back[r]))
            low, here = high, there

    def first_pass(_, carry):
        sweep(1, n - 1)
        return carry

    lax.fori_loop(0, PASSES, first_pass, 0)

    def scale(k, carry):
        v[PASSES + k] = weight[k] * v[PASSES + k]
        return carry

    lax.fori_loop(0, rows + 2 * PASSES, scale, 0)

    def second_pass(_, carry):
        sweep(PASSES + 1, n - PASSES - 1)
        return carry

    lax.fori_loop(0, PASSES, second_pass, 0)

    acc[...] = jnp.zeros(acc.shape, F32)
    base = (lat - 1) * band
    for k in range(rows):
        o = [v[HALO + k, :, cut(r)] for r in range(4)]
        ahead = pltpu.roll(0.375 * o[0] + 0.125 * o[1], lon - 1, axis=1)
        behind = pltpu.roll(0.125 * o[2] + 0.375 * o[3], 1, axis=1)
        g = 0.625 * (o[0] + o[3]) + 0.875 * (o[1] + o[2]) + (ahead + behind)
        s = jnp.clip(source[k] - base, 0, 3 * band - 2)
        f = frac[k]
        acc[s] += (1.0 - f) * g
        acc[s + 1] += f * g
    for k in range(band):
        keep[8 * k : 8 * k + 8, :] = acc[band + k]

    def give(ref, slot):
        for k in range(band):
            ref[8 * k : 8 * k + 8, :] = acc[slot * band + k]

    @pl.when(odd == 0)
    def _():
        give(send_a, 2)
        give(send_b, 0)

    @pl.when(odd == 1)
    def _():
        give(send_a, 0)
        give(send_b, 2)


def copies_kernel(keep, got_a, got_b, out, sums):
    count, n, lon = out.shape
    rows = n // 8
    total = keep[...] + got_a[...] + got_b[...]
    for c in range(lon // 128):
        lanes = slice(128 * c, 128 * c + 128)
        for row in range(rows):
            sums[pl.ds(n * c + row, 8, stride=rows), :] = total[8 * row : 8 * row + 8, lanes]
        value = sums[n * c : n * c + n, :]
        for k in range(count):
            out[k, :, lanes] = value


def lower_kernel(place, pert, adjoint, mix_t, lon_down, own, send_a, send_b, wide):
    lat, last = place[0], place[1] - 1
    odd = lat % 2
    members = pert.shape[0]
    lev = own.shape[0] // members
    field = adjoint[...].reshape(pert.shape[1], pert.shape[2])
    for m in range(members):
        hi, lo = split2(field * pert[m].astype(F32))
        wide[3 * lev * m : 3 * lev * (m + 1), :] = dot(mix_t[...], hi) + dot(mix_t[...], lo)
    hi, lo = split2(wide[...])
    narrow = dot(hi, lon_down[...]) + dot(lo, lon_down[...])
    at_first = jnp.where(lat == 0, 1.0, 0.0)
    at_last = jnp.where(lat == last, 1.0, 0.0)
    is_odd = jnp.where(odd == 1, 1.0, 0.0)
    for m in range(members):
        at = 3 * lev * m
        low = narrow[at : at + lev]
        mine = narrow[at + lev : at + 2 * lev]
        high = narrow[at + 2 * lev : at + 3 * lev]
        to = slice(m * lev, m * lev + lev)
        own[to, :] = mine + at_first * low + at_last * high
        low = (1.0 - at_first) * low
        high = (1.0 - at_last) * high
        send_a[to, :] = is_odd * low + (1.0 - is_odd) * high
        send_b[to, :] = is_odd * high + (1.0 - is_odd) * low


def vmem():
    return pl.BlockSpec(memory_space=pltpu.VMEM)


def smem():
    return pl.BlockSpec(memory_space=pltpu.SMEM)


def call(kernel, name, outs, scratch, scalars, vectors):
    many = isinstance(outs, list)
    shapes = [jax.ShapeDtypeStruct(s, F32) for s in (outs if many else [outs])]
    return pl.pallas_call(
        kernel,
        name=name,
        out_shape=shapes if many else shapes[0],
        in_specs=[smem()] * len(scalars) + [vmem()] * len(vectors),
        out_specs=[vmem()] * len(shapes) if many else vmem(),
        scratch_shapes=[pltpu.VMEM(s, F32) for s in scratch],
        compiler_params=pltpu.CompilerParams(vmem_limit_bytes=48 * 2**20),
    )(*scalars, *vectors)


def body(controls, perturbations, precision_weight, north_coef, east_coef, fine_source, fine_frac):
    lat = lax.axis_index("lat")
    count = lax.axis_size("lat")
    mem = lax.axis_index("mem")
    ranks = lax.axis_size("mem")
    members, clev, _, clon = controls.shape
    lev, band, lon = perturbations.shape[1:]
    rows, fine_lon = north_coef.shape
    part = lev // ranks

    mates = [(i, i ^ 1) for i in range(count)]
    across = [(i, (i + 1) % count if i % 2 else (i - 1) % count) for i in range(count)]
    up_two = [(i, (i + 2) % count) for i in range(count)]
    down_two = [(i, (i - 2) % count) for i in range(count)]

    place = jnp.stack([lat, jnp.int32(count), mem]).astype(jnp.int32)
    lon_refine = refine_matrix(clon, True)
    lev_refine = refine_matrix(clev, False)
    mix = np.einsum("vl,rt->vrtl", lev_refine, PHASES).reshape(lev * band, 3 * clev)
    lon_up = jnp.asarray(lon_refine.T, BF16)
    lon_down = jnp.asarray(lon_refine, BF16)
    mix_up = jnp.asarray(np.concatenate([mix, mix], axis=1), BF16)
    mix_down = jnp.asarray(mix.T, BF16)
    pick = np.zeros((512, 512), np.float32)
    for r in range(4):
        for q in range(128):
            pick[4 * q + r, 128 * r + q] = 1.0
    pick = jnp.asarray(pick, BF16)
    order = np.eye(part * rows).reshape(part, rows, part, rows).transpose(1, 0, 2, 3)
    order = jnp.asarray(order.reshape(part * rows, part * rows), BF16)

    own = controls.reshape(members * clev, clon)
    low_high = [lax.ppermute(own, "lat", across), lax.ppermute(own, "lat", mates)]
    pert = perturbations.reshape(members, lev * band, lon)

    tail = jnp.concatenate([fine_frac, fine_source.astype(F32)])
    tail = jnp.pad(tail[None], ((0, 3), (0, fine_lon - 2 * rows)))
    spots = 8 * PASSES + 2 * HALO + 4
    coef, own_weight, buf_a, buf_b = pl.pallas_call(
        prepare_kernel,
        name="prepare",
        grid_spec=pltpu.PrefetchScalarGridSpec(
            num_scalar_prefetch=1,
            grid=(1,),
            in_specs=[
                pl.BlockSpec((part, rows, fine_lon), lambda i, p: (p[2], 0, 0)),
                pl.BlockSpec((rows, fine_lon), lambda i, p: (0, 0)),
                pl.BlockSpec((rows, fine_lon), lambda i, p: (0, 0)),
                pl.BlockSpec((4, fine_lon), lambda i, p: (0, 0)),
                pl.BlockSpec((512, 512), lambda i, p: (0, 0)),
                pl.BlockSpec((part * rows, part * rows), lambda i, p: (0, 0)),
            ],
            out_specs=[
                pl.BlockSpec((2 * rows, fine_lon), lambda i, p: (0, 0)),
                pl.BlockSpec((rows, part, fine_lon), lambda i, p: (0, 0, 0)),
                pl.BlockSpec((spots, fine_lon), lambda i, p: (0, 0)),
                pl.BlockSpec((spots, fine_lon), lambda i, p: (0, 0)),
            ],
        ),
        out_shape=[
            jax.ShapeDtypeStruct((2 * rows, fine_lon), F32),
            jax.ShapeDtypeStruct((rows, part, fine_lon), F32),
            jax.ShapeDtypeStruct((spots, fine_lon), F32),
            jax.ShapeDtypeStruct((spots, fine_lon), F32),
        ],
        compiler_params=pltpu.CompilerParams(vmem_limit_bytes=48 * 2**20),
    )(place, precision_weight, north_coef, east_coef, tail, pick, order)
    far_b = lax.ppermute(buf_b, "lat", across)
    far_a = lax.ppermute(buf_a, "lat", mates)

    local_sum = call(
        raise_kernel, "raise", (ranks, part * band, lon),
        [(3 * members * clev, clon), (lev * band, lon)],
        [place], [own, low_high[1], low_high[0], pert, lon_up, mix_up],
    )
    parts = lax.all_to_all(local_sum, "mem", 0, 0, tiled=True)
    mine = call(total_kernel, "total", (band * part, lon), [(band * part * lon // 128, 128)], [], [parts])
    mate = lax.ppermute(mine, "lat", mates)
    pair = jnp.concatenate([mine, mate], axis=0)
    up_pair = lax.ppermute(pair, "lat", up_two)
    down_pair = lax.ppermute(pair, "lat", down_two)

    n = rows + 2 * HALO
    north, east, west, weight = call(
        assemble_kernel, "assemble",
        [(n, 8, fine_lon), (n, 8, fine_lon), (n, 8, lon), (rows + 2 * PASSES, 8, fine_lon)],
        [], [place], [coef, own_weight, far_a, far_b],
    )
    at = 8 * PASSES + 2 * HALO
    extra_a = far_a[at : at + 1, : 2 * rows]
    extra_b = far_b[at : at + 1, : 2 * rows]
    piece = (band * part, lon)
    keep, send_a, send_b = call(
        fine_kernel, "fine", [piece, piece, piece],
        [(5 * band, 8, lon), (n, 8, fine_lon), (3 * band, 8, lon)],
        [place, fine_source, fine_frac, extra_a, extra_b],
        [mine, mate, up_pair, down_pair, north, east, west, weight],
    )
    got_b = lax.ppermute(send_b, "lat", across)
    got_a = lax.ppermute(send_a, "lat", mates)
    copies = call(
        copies_kernel, "copies", (ranks, band * part, lon),
        [(band * part * lon // 128, 128)], [], [keep, got_a, got_b]
    )
    adjoint = lax.all_to_all(copies, "mem", 0, 0, tiled=True)
    flat = (members * clev, clon)
    result, send_a, send_b = call(
        lower_kernel, "lower", [flat, flat, flat], [(3 * members * clev, lon)],
        [place], [pert, adjoint, mix_down, lon_down],
    )
    got_b = lax.ppermute(send_b, "lat", across)
    got_a = lax.ppermute(send_a, "lat", mates)
    return controls + (result + got_a + got_b).reshape(controls.shape)


def solution(mesh):
    in_specs = (
        P("mem", None, "lat", None),
        P("mem", None, "lat", None),
        P(None, "lat", None),
        P("lat", None),
        P("lat", None),
        P("lat"),
        P("lat"),
    )
    out_specs = P("mem", None, "lat", None)
    return jax.shard_map(body, mesh=mesh, in_specs=in_specs, out_specs=out_specs, check_vma=False)
```

time: 209 us -> 71.6 us (0.34)
  the two profiles are of different devices: /device:TPU:97 before, /device:TPU:0 now
where the time goes in v1:
time: 71.6 us; the launch traced here: 71.3 us
  starting transfers between devices  24.9 us (35%)
  blocking collectives  15.3 us (21%)
  Pallas kernels  15 us (21%)
  waiting for transfers between devices  9.13 us (13%)
  local copies, waits for them, and re-layouts  5.81 us (8%)
  other arithmetic  0.85 us (1%)
    all_to_all x1, blocking collectives, body(): adjoint = lax.all_to_all(copies, 'mem', 0, 0, tiled=True)  15.3 us
    pallas_call x6, Pallas kernels, call(): pl.pallas_call(kernel, name=name, out_shape=shapes if many else shapes[0]...  12.2 us
    all_to_all x1, starting transfers between devices, body(): parts = lax.all_to_all(local_sum, 'mem', 0, 0, tiled=True)  6.64 us
    ppermute x2, starting transfers between devices, body(): got_b = lax.ppermute(send_b, 'lat', across)  6.23 us
    ppermute x2, waiting for transfers between devices, body(): got_b = lax.ppermute(send_b, 'lat', across)  5.28 us
    ppermute x1, starting transfers between devices, body(): lax.ppermute(own, 'lat', across)  5.27 us
    ppermute x1, starting transfers between devices, body(): down_pair = lax.ppermute(pair, 'lat', down_two)  4.12 us
    unnamed x26, local copies, waits for them, and re-layouts  3.42 us
  transfers between devices with their start and end apart: 12, of which 5 were waited for; matrix products, arithmetic and copies ran while one was open for 4% of the time, Pallas kernels for 7%

profile of v1, /device:TPU:0, one launch (start us, length us, event | category | flops | bytes accessed | tf_op | source)
XLA Modules:
  0.0 71.3 jit_solution(1307885623416375523)
XLA Ops:
  0.0 5.3 %collective-permute-start.3 = (f32[96,96]{1,0:T(8,128)}, f32[96,96]{1,0:T(8,128)S(1)}, u32[]{:S(2)}, u32[]{:S(2)}) collective-permute-start(f32[96,96]{1,0:T(8,128)} %bitcast.9), channel_id=1, source_target_pairs={{0,15},{1,2},{2,1},{3,4},{4,3},{5,6},{6,5},{7,8},{8,7},{9,10},{10,... | collective-permute-start | bytes 110600 | tf_op jit(solution)/shard_map/ppermute | solution.py:413
  5.4 2.4 %reshape.9.pert = bf16[6,256,384]{2,1,0:T(8,128)(2,1)S(1)} reshape(bf16[6,64,4,384]{3,2,1,0:T(4,128)(2,1)} %param.14) | data formatting | bytes 2359296 | tf_op jit(solution)/shard_map/reshape | solution.py:414
  7.9 2.0 %raise.1 = f32[8,32,384]{2,1,0:T(8,128)} custom-call(s32[3]{0:T(128)S(1)} %pad_add_fusion.place, f32[96,96]{1,0:T(8,128)S(1)} %bitcast.10, f32[96,96]{1,0:T(8,128)S(1)} %collective-permute-done.2.got_a, f32[96,96]{1,0:T(8,128)S(1)} %collective-permute-done.3.got_b, bf16[6,256,384]{2,1,0:T(8,128)(2,1)S(1)} %reshape.9.pert, bf16[96,384]{1,0:T(8,128)(2,1)S(1)} %copy-done.7, ...), custom_call_target="tpu_custom_call" | custom-call | tf_op jit(solution)/shard_map/raise/pallas_call | solution.py:370
  9.9 6.6 %all-to-all-start = ((f32[8,32,384]{2,1,0:T(8,128)}), f32[8,32,384]{2,1,0:T(8,128)S(1)}, u32[]{:S(2)}, u32[]{:S(2)}) async-start(f32[8,32,384]{2,1,0:T(8,128)} %raise.1), calls=%async_computation | async-start | bytes 786432 | tf_op jit(solution)/shard_map/all_to_all | solution.py:456
  16.6 0.1 maximum_bitcast_fusion
  16.7 1.9 %copy-done = bf16[64,16,1536]{2,1,0:T(8,128)(2,1)S(1)} copy-done((bf16[64,16,1536]{2,1,0:T(8,128)(2,1)S(1)}, bf16[64,16,1536]{2,1,0:T(8,128)(2,1)}, u32[]{:S(2)}) %copy-start) | copy-done | bytes 3145752
  18.6 2.8 %prepare.1 = (f32[32,1536]{1,0:T(8,128)S(1)}, f32[16,8,1536]{2,1,0:T(8,128)S(1)}, f32[64,1536]{1,0:T(8,128)}, f32[64,1536]{1,0:T(8,128)}) custom-call(s32[3]{0:T(128)S(1)} %pad_add_fusion.place, bf16[64,16,1536]{2,1,0:T(8,128)(2,1)S(1)} %copy-done, f32[16,1536]{1,0:T(8,128)S(1)} %copy-done.5, f32[16,1536]{1,0:T(8,128)S(1)} %copy-done.6, ...), custom_call_target="tpu_custom_call" | custom-call | tf_op jit(solution)/shard_map/prepare/pallas_call | solution.py:419
  21.4 2.4 %collective-permute-start.1 = (f32[64,1536]{1,0:T(8,128)}, f32[64,1536]{1,0:T(8,128)S(1)}, u32[]{:S(2)}, u32[]{:S(2)}) collective-permute-start(f32[64,1536]{1,0:T(8,128)} %get-tuple-element.20), channel_id=1, source_target_pairs={{0,15},{1,2},{2,1},{3,4},{4,3},{5,6},{6,5},{7,8},{8,7},{9,10},{10,... | collective-permute-start | bytes 1179656 | tf_op jit(solution)/shard_map/ppermute | solution.py:448
  23.8 2.0 %all-to-all-done.parts = f32[8,32,384]{2,1,0:T(8,128)S(1)} async-done(((f32[8,32,384]{2,1,0:T(8,128)}), f32[8,32,384]{2,1,0:T(8,128)S(1)}, u32[]{:S(2)}, u32[]{:S(2)}) %all-to-all-start) | async-done | bytes 393248 | tf_op jit(solution)/shard_map/all_to_all | solution.py:456
  25.8 0.1 collective-permute-start.4
  25.9 1.2 %collective-permute-done.4.mate = f32[32,384]{1,0:T(8,128)S(1)} collective-permute-done((f32[32,384]{1,0:T(8,128)S(1)}, f32[32,384]{1,0:T(8,128)S(1)}, u32[]{:S(2)}, u32[]{:S(2)}) %collective-permute-start.4) | collective-permute-done | bytes 49184 | tf_op jit(solution)/shard_map/ppermute | solution.py:458
  27.2 4.1 %collective-permute-start.6 = (f32[64,384]{1,0:T(8,128)S(1)}, f32[64,384]{1,0:T(8,128)S(1)}, u32[]{:S(2)}, u32[]{:S(2)}) collective-permute-start(f32[64,384]{1,0:T(8,128)S(1)} %pad_maximum_fusion), channel_id=1, source_target_pairs={{0,14},{1,15},{2,0},{3,1},{4,2},{5,3},{6,4},{7,5},{8,6},{9,7},{10,... | collective-permute-start | bytes 294920 | tf_op jit(solution)/shard_map/ppermute | solution.py:461
  31.4 2.2 %assemble.1 = (f32[36,8,1536]{2,1,0:T(8,128)S(1)}, f32[36,8,1536]{2,1,0:T(8,128)}, f32[36,8,384]{2,1,0:T(8,128)S(1)}, f32[26,8,1536]{2,1,0:T(8,128)S(1)}) custom-call(s32[3]{0:T(128)S(1)} %pad_add_fusion.place, f32[32,1536]{1,0:T(8,128)S(1)} %get-tuple-element.21.coef, f32[16,8,1536]{2,1,0:T(8,128)S(1)} %get-tuple-element.22.own_weight, ...), custom_call_target="tpu_custom_call" | custom-call | tf_op jit(solution)/shard_map/assemble/pallas_call | solution.py:370
  33.6 0.6 collective-permute-done.5.up_pair
  34.2 1.5 %copy-done.1 = f32[36,8,1536]{2,1,0:T(8,128)S(1)} copy-done((f32[36,8,1536]{2,1,0:T(8,128)S(1)}, f32[36,8,1536]{2,1,0:T(8,128)}, u32[]{:S(2)}) %copy-start.1) | copy-done | bytes 1769496
  35.6 6.6 %fine.1 = (f32[32,384]{1,0:T(8,128)S(1)}, f32[32,384]{1,0:T(8,128)S(1)}, f32[32,384]{1,0:T(8,128)S(1)}) custom-call(s32[3]{0:T(128)S(1)} %pad_add_fusion.place, s32[16]{0:T(128)S(1)} %copy-done.11, f32[16]{0:T(128)S(1)} %copy-done.12, f32[1,32]{1,0:T(1,128)S(1)} %slice.8.extra_a, f32[1,32]{1,0:T(1,128)S(1)} %slice.9.extra_b, f32[32,384]{1,0:T(8,128)S(1)} %total.1.own, ...), custom_call_target="tpu_custom_call" | custom-call | tf_op jit(solution)/shard_map/fine/pallas_call | solution.py:370
  42.2 0.1 collective-permute-start.7
  42.3 4.0 %collective-permute-start.8 = (f32[32,384]{1,0:T(8,128)S(1)}, f32[32,384]{1,0:T(8,128)S(1)}, u32[]{:S(2)}, u32[]{:S(2)}) collective-permute-start(f32[32,384]{1,0:T(8,128)S(1)} %get-tuple-element.29), channel_id=1, source_target_pairs={{0,15},{1,2},{2,1},{3,4},{4,3},{5,6},{6,5},{7,8},{8,7},{9,10},{10,... | collective-permute-start | bytes 147464 | tf_op jit(solution)/shard_map/ppermute | solution.py:479
  46.4 1.8 %collective-permute-done.8.got_b = f32[32,384]{1,0:T(8,128)S(1)} collective-permute-done((f32[32,384]{1,0:T(8,128)S(1)}, f32[32,384]{1,0:T(8,128)S(1)}, u32[]{:S(2)}, u32[]{:S(2)}) %collective-permute-start.8) | collective-permute-done | bytes 49184 | tf_op jit(solution)/shard_map/ppermute | solution.py:479
  48.2 15.3 %all_to_all.10.adjoint = f32[8,32,384]{2,1,0:T(8,128)S(1)} all-to-all(f32[8,32,384]{2,1,0:T(8,128)S(1)} %copies.1), channel_id=1, replica_groups=mesh['mem'=8,'lat'=16] {'mem'}, dimensions={0} | all-to-all | bytes 786432 | tf_op jit(solution)/shard_map/all_to_all | solution.py:485
  63.5 1.4 %lower.1 = (f32[96,96]{1,0:T(8,128)S(1)}, f32[96,96]{1,0:T(8,128)S(1)}, f32[96,96]{1,0:T(8,128)S(1)}) custom-call(s32[3]{0:T(128)S(1)} %pad_add_fusion.place, bf16[6,256,384]{2,1,0:T(8,128)(2,1)S(1)} %reshape.9.pert, f32[8,32,384]{2,1,0:T(8,128)S(1)} %all_to_all.10.adjoint, bf16[48,256]{1,0:T(8,128)(2,1)S(1)} %copy-done.10, bf16[384,96]{1,0:T(8,128)(2,1)S(1)} %copy-done.4), custom_call_target="tpu_custom_call" | custom-call | tf_op jit(solution)/shard_map/lower/pallas_call | solution.py:370
  64.9 2.2 %collective-permute-start.10 = (f32[96,96]{1,0:T(8,128)S(1)}, f32[96,96]{1,0:T(8,128)S(1)}, u32[]{:S(2)}, u32[]{:S(2)}) collective-permute-start(f32[96,96]{1,0:T(8,128)S(1)} %get-tuple-element.32), channel_id=1, source_target_pairs={{0,15},{1,2},{2,1},{3,4},{4,3},{5,6},{6,5},{7,8},{8,7},{9,10},{10,... | collective-permute-start | bytes 110600 | tf_op jit(solution)/shard_map/ppermute | solution.py:491
  67.1 3.5 %collective-permute-done.10 = f32[96,96]{1,0:T(8,128)S(1)} collective-permute-done((f32[96,96]{1,0:T(8,128)S(1)}, f32[96,96]{1,0:T(8,128)S(1)}, u32[]{:S(2)}, u32[]{:S(2)}) %collective-permute-start.10) | collective-permute-done | bytes 36896 | tf_op jit(solution)/shard_map/ppermute | solution.py:491
  70.6 0.7 add.13
  (44 shorter events, 0.3 us)
Async XLA Ops:
  0.0 7.8 %copy-start.7 = (bf16[96,384]{1,0:T(8,128)(2,1)S(1)}, bf16[96,384]{1,0:T(8,128)(2,1)}, u32[]{:S(2)}) copy-start(bf16[96,384]{1,0:T(8,128)(2,1)} %constant.26.clone.lon_up) | copy-start | bytes 221188
  0.0 7.8 %copy-start.8 = (bf16[256,96]{1,0:T(8,128)(2,1)S(1)}, bf16[256,96]{1,0:T(8,128)(2,1)}, u32[]{:S(2)}) copy-start(bf16[256,96]{1,0:T(8,128)(2,1)} %constant.28.clone.mix) | copy-start | bytes 147460
  0.0 7.9 %copy-start.3 = (f32[6,16,1,96]{3,2,1,0:T(1,128)S(1)}, f32[6,16,1,96]{3,2,1,0:T(1,128)}, u32[]{:S(2)}) copy-start(f32[6,16,1,96]{3,2,1,0:T(1,128)} %param.13) | copy-start | bytes 110596
  0.0 7.8 %collective-permute-start.2 = (f32[96,96]{1,0:T(8,128)}, f32[96,96]{1,0:T(8,128)S(1)}, u32[]{:S(2)}, u32[]{:S(2)}) collective-permute-start(f32[96,96]{1,0:T(8,128)} %bitcast.8), channel_id=1, source_target_pairs={{0,1},{1,0},{2,3},{3,2},{4,5},{5,4},{6,7},{7,6},{8,9},{9,8},{10,11... | collective-permute-start | bytes 110600 | tf_op jit(solution)/shard_map/ppermute | solution.py:413
  0.0 7.8 %collective-permute-start.3 = (f32[96,96]{1,0:T(8,128)}, f32[96,96]{1,0:T(8,128)S(1)}, u32[]{:S(2)}, u32[]{:S(2)}) collective-permute-start(f32[96,96]{1,0:T(8,128)} %bitcast.9), channel_id=1, source_target_pairs={{0,15},{1,2},{2,1},{3,4},{4,3},{5,6},{6,5},{7,8},{8,7},{9,10},{10,... | collective-permute-start | bytes 110600 | tf_op jit(solution)/shard_map/ppermute | solution.py:413
  7.7 8.8 %copy-start.11 = (s32[16]{0:T(128)S(1)}, s32[16]{0:T(128)}, u32[]{:S(2)}) copy-start(s32[16]{0:T(128)} %source.1) | copy-start | bytes 196
  7.8 8.8 %copy-start.12 = (f32[16]{0:T(128)S(1)}, f32[16]{0:T(128)}, u32[]{:S(2)}) copy-start(f32[16]{0:T(128)} %frac.1) | copy-start | bytes 196
  7.8 8.9 %copy-start.2 = (bf16[512,512]{1,0:T(8,128)(2,1)S(1)}, bf16[512,512]{1,0:T(8,128)(2,1)}, u32[]{:S(2)}) copy-start(bf16[512,512]{1,0:T(8,128)(2,1)} %constant.30.clone.select) | copy-start | bytes 1572868
  7.8 8.9 %copy-start.5 = (f32[16,1536]{1,0:T(8,128)S(1)}, f32[16,1536]{1,0:T(8,128)}, u32[]{:S(2)}) copy-start(f32[16,1536]{1,0:T(8,128)} %north.1) | copy-start | bytes 294916
  7.8 8.9 %copy-start.6 = (f32[16,1536]{1,0:T(8,128)S(1)}, f32[16,1536]{1,0:T(8,128)}, u32[]{:S(2)}) copy-start(f32[16,1536]{1,0:T(8,128)} %east.1) | copy-start | bytes 294916
  7.8 8.9 %copy-start.9 = (bf16[128,128]{1,0:T(8,128)(2,1)S(1)}, bf16[128,128]{1,0:T(8,128)(2,1)}, u32[]{:S(2)}) copy-start(bf16[128,128]{1,0:T(8,128)(2,1)} %constant.31.clone.order) | copy-start | bytes 98308
  9.9 15.9 %all-to-all-start = ((f32[8,32,384]{2,1,0:T(8,128)}), f32[8,32,384]{2,1,0:T(8,128)S(1)}, u32[]{:S(2)}, u32[]{:S(2)}) async-start(f32[8,32,384]{2,1,0:T(8,128)} %raise.1), calls=%async_computation | async-start | bytes 786432 | tf_op jit(solution)/shard_map/all_to_all | solution.py:456
  16.7 1.9 %copy-start = (bf16[64,16,1536]{2,1,0:T(8,128)(2,1)S(1)}, bf16[64,16,1536]{2,1,0:T(8,128)(2,1)}, u32[]{:S(2)}) copy-start(bf16[64,16,1536]{2,1,0:T(8,128)(2,1)} %weight.1) | copy-start | bytes 9437188
  21.4 10.0 %collective-permute-start = (f32[64,1536]{1,0:T(8,128)}, f32[64,1536]{1,0:T(8,128)S(1)}, u32[]{:S(2)}, u32[]{:S(2)}) collective-permute-start(f32[64,1536]{1,0:T(8,128)} %get-tuple-element.19), channel_id=1, source_target_pairs={{0,1},{1,0},{2,3},{3,2},{4,5},{5,4},{6,7},{7,6},{8,9},{9,8},{10,11... | collective-permute-start | bytes 1179656 | tf_op jit(solution)/shard_map/ppermute | solution.py:449
  21.4 10.0 %collective-permute-start.1 = (f32[64,1536]{1,0:T(8,128)}, f32[64,1536]{1,0:T(8,128)S(1)}, u32[]{:S(2)}, u32[]{:S(2)}) collective-permute-start(f32[64,1536]{1,0:T(8,128)} %get-tuple-element.20), channel_id=1, source_target_pairs={{0,15},{1,2},{2,1},{3,4},{4,3},{5,6},{6,5},{7,8},{8,7},{9,10},{10,... | collective-permute-start | bytes 1179656 | tf_op jit(solution)/shard_map/ppermute | solution.py:448
  25.8 1.3 %collective-permute-start.4 = (f32[32,384]{1,0:T(8,128)S(1)}, f32[32,384]{1,0:T(8,128)S(1)}, u32[]{:S(2)}, u32[]{:S(2)}) collective-permute-start(f32[32,384]{1,0:T(8,128)S(1)} %total.1.own), channel_id=1, source_target_pairs={{0,1},{1,0},{2,3},{3,2},{4,5},{5,4},{6,7},{7,6},{8,9},{9,8},{10,11... | collective-permute-start | bytes 147464 | tf_op jit(solution)/shard_map/ppermute | solution.py:458
  27.2 7.0 %collective-permute-start.5 = (f32[64,384]{1,0:T(8,128)S(1)}, f32[64,384]{1,0:T(8,128)S(1)}, u32[]{:S(2)}, u32[]{:S(2)}) collective-permute-start(f32[64,384]{1,0:T(8,128)S(1)} %pad_maximum_fusion), channel_id=1, source_target_pairs={{0,2},{1,3},{2,4},{3,5},{4,6},{5,7},{6,8},{7,9},{8,10},{9,11},{10,... | collective-permute-start | bytes 294920 | tf_op jit(solution)/shard_map/ppermute | solution.py:460
  27.2 6.9 %collective-permute-start.6 = (f32[64,384]{1,0:T(8,128)S(1)}, f32[64,384]{1,0:T(8,128)S(1)}, u32[]{:S(2)}, u32[]{:S(2)}) collective-permute-start(f32[64,384]{1,0:T(8,128)S(1)} %pad_maximum_fusion), channel_id=1, source_target_pairs={{0,14},{1,15},{2,0},{3,1},{4,2},{5,3},{6,4},{7,5},{8,6},{9,7},{10,... | collective-permute-start | bytes 294920 | tf_op jit(solution)/shard_map/ppermute | solution.py:461
  35.6 27.9 %copy-start.4 = (bf16[384,96]{1,0:T(8,128)(2,1)S(1)}, bf16[384,96]{1,0:T(8,128)(2,1)}, u32[]{:S(2)}) copy-start(bf16[384,96]{1,0:T(8,128)(2,1)} %constant.27.clone.lon_down) | copy-start | bytes 221188
  35.6 27.9 %copy-start.10 = (bf16[48,256]{1,0:T(8,128)(2,1)S(1)}, bf16[48,256]{1,0:T(8,128)(2,1)}, u32[]{:S(2)}) copy-start(bf16[48,256]{1,0:T(8,128)(2,1)} %constant.29.clone.mix_t) | copy-start | bytes 73732
  42.2 4.1 %collective-permute-start.7 = (f32[32,384]{1,0:T(8,128)S(1)}, f32[32,384]{1,0:T(8,128)S(1)}, u32[]{:S(2)}, u32[]{:S(2)}) collective-permute-start(f32[32,384]{1,0:T(8,128)S(1)} %get-tuple-element.28), channel_id=1, source_target_pairs={{0,1},{1,0},{2,3},{3,2},{4,5},{5,4},{6,7},{7,6},{8,9},{9,8},{10,11... | collective-permute-start | bytes 147464 | tf_op jit(solution)/shard_map/ppermute | solution.py:480
  42.3 5.8 %collective-permute-start.8 = (f32[32,384]{1,0:T(8,128)S(1)}, f32[32,384]{1,0:T(8,128)S(1)}, u32[]{:S(2)}, u32[]{:S(2)}) collective-permute-start(f32[32,384]{1,0:T(8,128)S(1)} %get-tuple-element.29), channel_id=1, source_target_pairs={{0,15},{1,2},{2,1},{3,4},{4,3},{5,6},{6,5},{7,8},{8,7},{9,10},{10,... | collective-permute-start | bytes 147464 | tf_op jit(solution)/shard_map/ppermute | solution.py:479
  64.9 5.7 %collective-permute-start.10 = (f32[96,96]{1,0:T(8,128)S(1)}, f32[96,96]{1,0:T(8,128)S(1)}, u32[]{:S(2)}, u32[]{:S(2)}) collective-permute-start(f32[96,96]{1,0:T(8,128)S(1)} %get-tuple-element.32), channel_id=1, source_target_pairs={{0,15},{1,2},{2,1},{3,4},{4,3},{5,6},{6,5},{7,8},{8,7},{9,10},{10,... | collective-permute-start | bytes 110600 | tf_op jit(solution)/shard_map/ppermute | solution.py:491
  67.1 3.5 %collective-permute-start.9 = (f32[96,96]{1,0:T(8,128)S(1)}, f32[96,96]{1,0:T(8,128)S(1)}, u32[]{:S(2)}, u32[]{:S(2)}) collective-permute-start(f32[96,96]{1,0:T(8,128)S(1)} %get-tuple-element.31), channel_id=1, source_target_pairs={{0,1},{1,0},{2,3},{3,2},{4,5},{5,4},{6,7},{7,6},{8,9},{9,8},{10,11... | collective-permute-start | bytes 110600 | tf_op jit(solution)/shard_map/ppermute | solution.py:492
  (1 other events, 1.5 us)

commit v2 on v1

--- a/solution.py
+++ b/solution.py
@@ -9,6 +9,7 @@
 PASSES = 5
 REACH = 4
 HALO = 2 * PASSES
+VMEM_LIMIT = 24 * 2**20
 F32 = jnp.float32
 BF16 = jnp.bfloat16
 
@@ -38,21 +39,28 @@
     return jnp.dot(a, b, preferred_element_type=F32)
 
 
-def prepare_kernel(place, weight, north, east, extra, select, order, coef, own_weight, buf_a, buf_b):
+def prepare_kernel(
+    place, weight, north, east, extra, select, order, coef, own_weight, buf_a, buf_b, level_weight, sem
+):
     odd = place[0] % 2
-    levels, rows, lon = weight.shape
+    levels, rows, lon = level_weight.shape
+    fetch = pltpu.make_async_copy(weight.at[pl.ds(place[2] * levels, levels)], level_weight, sem)
+    fetch.start()
     stacked = jnp.concatenate([north[...], east[...]], axis=0)
-    hi, rest = stacked.astype(BF16), None
+    hi = stacked.astype(BF16)
     rest = stacked - hi.astype(F32)
     mid = rest.astype(BF16)
     low = (rest - mid.astype(F32)).astype(BF16)
-    sel = select[...]
-    values = dot(order[...], weight[...].reshape(levels * rows, lon)).astype(BF16)
+    fetch.wait()
+    values = dot(order[...], level_weight[...].reshape(levels * rows, lon)).astype(BF16)
+    everything = jnp.concatenate([values, hi, mid, low], axis=0)
+    many = levels * rows
     quarter = lon // 4
     for c in range(lon // 512):
-        cut = slice(512 * c, 512 * c + 512)
-        cpart = dot(hi[:, cut], sel) + dot(mid[:, cut], sel) + dot(low[:, cut], sel)
-        wpart = dot(values[:, cut], sel)
+        moved = dot(everything[:, 512 * c : 512 * c + 512], select[...])
+        wpart = moved[:many]
+        cpart = moved[many : many + 2 * rows] + moved[many + 2 * rows : many + 4 * rows]
+        cpart = cpart + moved[many + 4 * rows :]
         for r in range(4):
             to = slice(quarter * r + 128 * c, quarter * r + 128 * c + 128)
             frm = slice(128 * r, 128 * r + 128)
@@ -119,6 +127,14 @@
         north[HALO - 1] = jnp.zeros(north.shape[1:], F32)
 
 
+def arrange_kernel(pert, out):
+    members, lev, band, _ = pert.shape
+    for m in range(members):
+        values = pert[m].astype(F32)
+        for k in range(lev):
+            out[m, band * k : band * k + band, :] = values[k]
+
+
 def raise_kernel(place, own, got_a, got_b, pert, lon_up, mix, out, x, acc):
     lat, last = place[0], place[1] - 1
     odd = lat % 2
@@ -161,7 +177,7 @@
     for m in range(members):
         hi, lo = split2(wide[3 * lev * m : 3 * lev * (m + 1), :])
         field = dot(mix[...], jnp.concatenate([hi, lo], axis=0))
-        term = field * pert[m].astype(F32)
+        term = field * pert[m]
         if m == 0:
             acc[...] = term
         elif m < members - 1:
@@ -184,7 +200,7 @@
 
 
 def fine_kernel(
-    place, source, frac, extra_a, extra_b, own, mate, up_pair, down_pair,
+    place, source, frac, extra_a, extra_b, own, mate, near_pair, far_pair,
     north, east, west, weight, keep, send_a, send_b, mid, v, acc,
 ):
     lat, last = place[0], place[1] - 1
@@ -201,19 +217,25 @@
     half = own.shape[0]
     bring(2, own, 0)
 
-    @pl.when(odd == 0)
-    def _():
+    def gather(even, up_pair, down_pair):
         bring(0, up_pair, 0)
-        bring(1, up_pair, half)
-        bring(3, mate, 0)
         bring(4, down_pair, 0)
-
-    @pl.when(odd == 1)
-    def _():
-        bring(0, up_pair, 0)
-        bring(1, mate, 0)
-        bring(3, down_pair, half)
-        bring(4, down_pair, 0)
+        if even:
+            bring(1, up_pair, half)
+            bring(3, mate, 0)
+        else:
+            bring(1, mate, 0)
+            bring(3, down_pair, half)
+
+    turn = lat % 4
+    for case in range(4):
+
+        @pl.when(turn == case)
+        def _(case=case):
+            if case < 2:
+                gather(case % 2 == 0, far_pair, near_pair)
+            else:
+                gather(case % 2 == 0, near_pair, far_pair)
 
     origin = (lat - 2) * band
     for i in range(n):
@@ -329,14 +351,14 @@
             out[k, :, lanes] = value
 
 
-def lower_kernel(place, pert, adjoint, mix_t, lon_down, own, send_a, send_b, wide):
+def lower_kernel(place, controls, pert, adjoint, mix_t, lon_down, own, send_a, send_b, wide):
     lat, last = place[0], place[1] - 1
     odd = lat % 2
     members = pert.shape[0]
     lev = own.shape[0] // members
     field = adjoint[...].reshape(pert.shape[1], pert.shape[2])
     for m in range(members):
-        hi, lo = split2(field * pert[m].astype(F32))
+        hi, lo = split2(field * pert[m])
         wide[3 * lev * m : 3 * lev * (m + 1), :] = dot(mix_t[...], hi) + dot(mix_t[...], lo)
     hi, lo = split2(wide[...])
     narrow = dot(hi, lon_down[...]) + dot(lo, lon_down[...])
@@ -349,7 +371,7 @@
         mine = narrow[at + lev : at + 2 * lev]
         high = narrow[at + 2 * lev : at + 3 * lev]
         to = slice(m * lev, m * lev + lev)
-        own[to, :] = mine + at_first * low + at_last * high
+        own[to, :] = controls[to, :] + mine + at_first * low + at_last * high
         low = (1.0 - at_first) * low
         high = (1.0 - at_last) * high
         send_a[to, :] = is_odd * low + (1.0 - is_odd) * high
@@ -374,7 +396,7 @@
         in_specs=[smem()] * len(scalars) + [vmem()] * len(vectors),
         out_specs=[vmem()] * len(shapes) if many else vmem(),
         scratch_shapes=[pltpu.VMEM(s, F32) for s in scratch],
-        compiler_params=pltpu.CompilerParams(vmem_limit_bytes=48 * 2**20),
+        compiler_params=pltpu.CompilerParams(vmem_limit_bytes=VMEM_LIMIT),
     )(*scalars, *vectors)
 
 
@@ -390,8 +412,8 @@
 
     mates = [(i, i ^ 1) for i in range(count)]
     across = [(i, (i + 1) % count if i % 2 else (i - 1) % count) for i in range(count)]
-    up_two = [(i, (i + 2) % count) for i in range(count)]
-    down_two = [(i, (i - 2) % count) for i in range(count)]
+    near_chips = [(i, i ^ 2) for i in range(count)]
+    far_chips = [(i, (i + 2) % count if i & 2 else (i - 2) % count) for i in range(count)]
 
     place = jnp.stack([lat, jnp.int32(count), mem]).astype(jnp.int32)
     lon_refine = refine_matrix(clon, True)
@@ -411,7 +433,7 @@
 
     own = controls.reshape(members * clev, clon)
     low_high = [lax.ppermute(own, "lat", across), lax.ppermute(own, "lat", mates)]
-    pert = perturbations.reshape(members, lev * band, lon)
+    pert = call(arrange_kernel, "arrange", (members, lev * band, lon), [], [], [perturbations])
 
     tail = jnp.concatenate([fine_frac, fine_source.astype(F32)])
     tail = jnp.pad(tail[None], ((0, 3), (0, fine_lon - 2 * rows)))
@@ -419,31 +441,16 @@
     coef, own_weight, buf_a, buf_b = pl.pallas_call(
         prepare_kernel,
         name="prepare",
-        grid_spec=pltpu.PrefetchScalarGridSpec(
-            num_scalar_prefetch=1,
-            grid=(1,),
-            in_specs=[
-                pl.BlockSpec((part, rows, fine_lon), lambda i, p: (p[2], 0, 0)),
-                pl.BlockSpec((rows, fine_lon), lambda i, p: (0, 0)),
-                pl.BlockSpec((rows, fine_lon), lambda i, p: (0, 0)),
-                pl.BlockSpec((4, fine_lon), lambda i, p: (0, 0)),
-                pl.BlockSpec((512, 512), lambda i, p: (0, 0)),
-                pl.BlockSpec((part * rows, part * rows), lambda i, p: (0, 0)),
-            ],
-            out_specs=[
-                pl.BlockSpec((2 * rows, fine_lon), lambda i, p: (0, 0)),
-                pl.BlockSpec((rows, part, fine_lon), lambda i, p: (0, 0, 0)),
-                pl.BlockSpec((spots, fine_lon), lambda i, p: (0, 0)),
-                pl.BlockSpec((spots, fine_lon), lambda i, p: (0, 0)),
-            ],
-        ),
         out_shape=[
             jax.ShapeDtypeStruct((2 * rows, fine_lon), F32),
             jax.ShapeDtypeStruct((rows, part, fine_lon), F32),
             jax.ShapeDtypeStruct((spots, fine_lon), F32),
             jax.ShapeDtypeStruct((spots, fine_lon), F32),
         ],
-        compiler_params=pltpu.CompilerParams(vmem_limit_bytes=48 * 2**20),
+        in_specs=[smem(), pl.BlockSpec(memory_space=pltpu.HBM)] + [vmem()] * 5,
+        out_specs=[vmem()] * 4,
+        scratch_shapes=[pltpu.VMEM((part, rows, fine_lon), BF16), pltpu.SemaphoreType.DMA(())],
+        compiler_params=pltpu.CompilerParams(vmem_limit_bytes=VMEM_LIMIT),
     )(place, precision_weight, north_coef, east_coef, tail, pick, order)
     far_b = lax.ppermute(buf_b, "lat", across)
     far_a = lax.ppermute(buf_a, "lat", mates)
@@ -457,8 +464,8 @@
     mine = call(total_kernel, "total", (band * part, lon), [(band * part * lon // 128, 128)], [], [parts])
     mate = lax.ppermute(mine, "lat", mates)
     pair = jnp.concatenate([mine, mate], axis=0)
-    up_pair = lax.ppermute(pair, "lat", up_two)
-    down_pair = lax.ppermute(pair, "lat", down_two)
+    far_pair = lax.ppermute(pair, "lat", far_chips)
+    near_pair = lax.ppermute(pair, "lat", near_chips)
 
     n = rows + 2 * HALO
     north, east, west, weight = call(
@@ -474,7 +481,7 @@
         fine_kernel, "fine", [piece, piece, piece],
         [(5 * band, 8, lon), (n, 8, fine_lon), (3 * band, 8, lon)],
         [place, fine_source, fine_frac, extra_a, extra_b],
-        [mine, mate, up_pair, down_pair, north, east, west, weight],
+        [mine, mate, near_pair, far_pair, north, east, west, weight],
     )
     got_b = lax.ppermute(send_b, "lat", across)
     got_a = lax.ppermute(send_a, "lat", mates)
@@ -486,11 +493,11 @@
     flat = (members * clev, clon)
     result, send_a, send_b = call(
         lower_kernel, "lower", [flat, flat, flat], [(3 * members * clev, lon)],
-        [place], [pert, adjoint, mix_down, lon_down],
+        [place], [own, pert, adjoint, mix_down, lon_down],
     )
     got_b = lax.ppermute(send_b, "lat", across)
     got_a = lax.ppermute(send_a, "lat", mates)
-    return controls + (result + got_a + got_b).reshape(controls.shape)
+    return (result + got_a + got_b).reshape(controls.shape)
 
 
 def solution(mesh):

time: 71.6 us -> 75.1 us (1.049)
  local copies, waits for them, and re-layouts: 5.81 us -> 9.94 us
  blocking collectives: 15.3 us -> 16.7 us
  starting transfers between devices: 24.9 us -> 23.9 us
    unnamed x26 -> x32, local copies, waits for them, and re-layouts: 3.42 us -> 8.57 us
    ppermute x1, waiting for transfers between devices: 0.01 us -> 2.63 us  [body(): far_b = lax.ppermute(buf_b, 'lat', across)]
    reshape x1 -> x0, local copies, waits for them, and re-layouts: 2.38 us -> none  [body(): pert = perturbations.reshape(members, lev * band, lon)]
    all_to_all x1, waiting for transfers between devices: 2.03 us -> 0.01 us  [body(): parts = lax.all_to_all(local_sum, 'mem', 0, 0, tiled=True)]
    ppermute x2, starting transfers between devices: 4.2 us -> 2.21 us  [the longest x1 2.12 us: body(): far_pair = lax.ppermute(pair, 'lat', far_chips)]
    all_to_all x1, blocking collectives: 15.3 us -> 16.7 us  [body(): adjoint = lax.all_to_all(copies, 'mem', 0, 0, tiled=True)]
    ppermute x2, waiting for transfers between devices: 5.28 us -> 4.49 us  [body(): got_b = lax.ppermute(send_b, 'lat', across)]
    pallas_call x6 -> x7, Pallas kernels: 12.2 us -> 11.9 us  [call(): pl.pallas_call(kernel, name=name, out_shape=shapes if many else shapes[0]...]
  transfers between devices with their start and end apart: 12 -> 12, of which waited for: 5 -> 5; matrix products, arithmetic and copies ran while one was open for 4% -> 2% of each run, Pallas kernels for 7% -> 6%
where the time goes in v2:
time: 75.1 us; the launch traced here: 74.5 us
  starting transfers between devices  23.9 us (32%)
  blocking collectives  16.7 us (22%)
  Pallas kernels  14.3 us (19%)
  local copies, waits for them, and re-layouts  9.94 us (13%)
  waiting for transfers between devices  8.72 us (12%)
  other arithmetic  0.79 us (1%)
    all_to_all x1, blocking collectives, body(): adjoint = lax.all_to_all(copies, 'mem', 0, 0, tiled=True)  16.7 us
    pallas_call x7, Pallas kernels, call(): pl.pallas_call(kernel, name=name, out_shape=shapes if many else shapes[0]...  11.9 us
    unnamed x32, local copies, waits for them, and re-layouts  8.57 us
    ppermute x2, starting transfers between devices, body(): got_b = lax.ppermute(send_b, 'lat', across)  6.91 us
    all_to_all x1, starting transfers between devices, body(): parts = lax.all_to_all(local_sum, 'mem', 0, 0, tiled=True)  6.64 us
    ppermute x1, starting transfers between devices, body(): lax.ppermute(own, 'lat', across)  5.19 us
    ppermute x2, waiting for transfers between devices, body(): got_b = lax.ppermute(send_b, 'lat', across)  4.49 us
    ppermute x1, starting transfers between devices, body(): far_b = lax.ppermute(buf_b, 'lat', across)  2.74 us
  transfers between devices with their start and end apart: 12, of which 5 were waited for; matrix products, arithmetic and copies ran while one was open for 2% of the time, Pallas kernels for 6%

profile of v2, /device:TPU:0, one launch (start us, length us, event | category | flops | bytes accessed | tf_op | source)
XLA Modules:
  0.0 74.5 jit_solution(4090545024060629656)
XLA Ops:
  0.0 5.2 %collective-permute-start.3 = (f32[96,96]{1,0:T(8,128)}, f32[96,96]{1,0:T(8,128)S(1)}, u32[]{:S(2)}, u32[]{:S(2)}) collective-permute-start(f32[96,96]{1,0:T(8,128)} %bitcast.9), channel_id=1, source_target_pairs={{0,15},{1,2},{2,1},{3,4},{4,3},{5,6},{6,5},{7,8},{8,7},{9,10},{10,... | collective-permute-start | bytes 110600 | tf_op jit(solution)/shard_map/ppermute | solution.py:435
  5.3 1.3 %copy-done.1 = bf16[6,64,4,384]{3,2,1,0:T(4,128)(2,1)S(1)} copy-done((bf16[6,64,4,384]{3,2,1,0:T(4,128)(2,1)S(1)}, bf16[6,64,4,384]{3,2,1,0:T(4,128)(2,1)}, u32[]{:S(2)}) %copy-start.1) | copy-done | bytes 1179672
  7.5 2.1 %raise.1 = f32[8,32,384]{2,1,0:T(8,128)} custom-call(s32[3]{0:T(128)S(1)} %pad_add_fusion.place, f32[96,96]{1,0:T(8,128)S(1)} %bitcast.10, f32[96,96]{1,0:T(8,128)S(1)} %collective-permute-done.2.got_a, f32[96,96]{1,0:T(8,128)S(1)} %collective-permute-done.3.got_b, f32[6,256,384]{2,1,0:T(8,128)S(1)} %arrange.1.pert, bf16[96,384]{1,0:T(8,128)(2,1)S(1)} %copy-done.10, ...), custom_call_target="tpu_custom_call" | custom-call | tf_op jit(solution)/shard_map/raise/pallas_call | solution.py:392
  9.5 6.6 %all-to-all-start = ((f32[8,32,384]{2,1,0:T(8,128)}), f32[8,32,384]{2,1,0:T(8,128)S(1)}, u32[]{:S(2)}, u32[]{:S(2)}) async-start(f32[8,32,384]{2,1,0:T(8,128)} %raise.1), calls=%async_computation | async-start | bytes 786432 | tf_op jit(solution)/shard_map/all_to_all | solution.py:463
  16.3 1.9 %copy-done = bf16[64,16,1536]{2,1,0:T(8,128)(2,1)S(1)} copy-done((bf16[64,16,1536]{2,1,0:T(8,128)(2,1)S(1)}, bf16[64,16,1536]{2,1,0:T(8,128)(2,1)}, u32[]{:S(2)}) %copy-start) | copy-done | bytes 3145752
  18.2 1.0 %copy-done.2 = bf16[512,512]{1,0:T(8,128)(2,1)S(1)} copy-done((bf16[512,512]{1,0:T(8,128)(2,1)S(1)}, bf16[512,512]{1,0:T(8,128)(2,1)}, u32[]{:S(2)}) %copy-start.2) | copy-done | bytes 524312
  19.2 0.9 %copy-done.8 = f32[16,1536]{1,0:T(8,128)S(1)} copy-done((f32[16,1536]{1,0:T(8,128)S(1)}, f32[16,1536]{1,0:T(8,128)}, u32[]{:S(2)}) %copy-start.8) | copy-done | bytes 98328
  20.1 0.9 %copy-done.9 = f32[16,1536]{1,0:T(8,128)S(1)} copy-done((f32[16,1536]{1,0:T(8,128)S(1)}, f32[16,1536]{1,0:T(8,128)}, u32[]{:S(2)}) %copy-start.9) | copy-done | bytes 98328
  21.0 0.8 %copy-done.12 = bf16[128,128]{1,0:T(8,128)(2,1)S(1)} copy-done((bf16[128,128]{1,0:T(8,128)(2,1)S(1)}, bf16[128,128]{1,0:T(8,128)(2,1)}, u32[]{:S(2)}) %copy-start.12) | copy-done | bytes 32792
  21.7 2.4 %prepare.1 = (f32[32,1536]{1,0:T(8,128)S(1)}, f32[16,8,1536]{2,1,0:T(8,128)S(1)}, f32[64,1536]{1,0:T(8,128)}, f32[64,1536]{1,0:T(8,128)}) custom-call(s32[3]{0:T(128)S(1)} %pad_add_fusion.place, bf16[64,16,1536]{2,1,0:T(8,128)(2,1)S(1)} %copy-done, f32[16,1536]{1,0:T(8,128)S(1)} %copy-done.8, f32[16,1536]{1,0:T(8,128)S(1)} %copy-done.9, ...), custom_call_target="tpu_custom_call" | custom-call | tf_op jit(solution)/shard_map/prepare/pallas_call | solution.py:441
  24.8 2.7 %collective-permute-start.1 = (f32[64,1536]{1,0:T(8,128)}, f32[64,1536]{1,0:T(8,128)}, u32[]{:S(2)}, u32[]{:S(2)}) collective-permute-start(f32[64,1536]{1,0:T(8,128)} %get-tuple-element.20), channel_id=1, source_target_pairs={{0,15},{1,2},{2,1},{3,4},{4,3},{5,6},{6,5},{7,8},{8,7},{9,10},{10,... | collective-permute-start | bytes 1179656 | tf_op jit(solution)/shard_map/ppermute | solution.py:455
  27.7 1.2 %collective-permute-done.4.mate = f32[32,384]{1,0:T(8,128)S(1)} collective-permute-done((f32[32,384]{1,0:T(8,128)S(1)}, f32[32,384]{1,0:T(8,128)S(1)}, u32[]{:S(2)}, u32[]{:S(2)}) %collective-permute-start.4) | collective-permute-done | bytes 49184 | tf_op jit(solution)/shard_map/ppermute | solution.py:465
  29.0 2.1 %collective-permute-start.6 = (f32[64,384]{1,0:T(8,128)S(1)}, f32[64,384]{1,0:T(8,128)S(1)}, u32[]{:S(2)}, u32[]{:S(2)}) collective-permute-start(f32[64,384]{1,0:T(8,128)S(1)} %pad_maximum_fusion), channel_id=1, source_target_pairs={{0,14},{1,15},{2,4},{3,5},{4,2},{5,3},{6,8},{7,9},{8,6},{9,7},{10,... | collective-permute-start | bytes 294920 | tf_op jit(solution)/shard_map/ppermute | solution.py:467
  31.1 0.7 slice.8.extra_a
  31.8 2.6 %collective-permute-done.1.got_b = f32[64,1536]{1,0:T(8,128)} collective-permute-done((f32[64,1536]{1,0:T(8,128)}, f32[64,1536]{1,0:T(8,128)}, u32[]{:S(2)}, u32[]{:S(2)}) %collective-permute-start.1) | collective-permute-done | bytes 393248 | tf_op jit(solution)/shard_map/ppermute | solution.py:455
  35.1 0.9 %copy-done.4 = f32[32,1536]{1,0:T(8,128)S(1)} copy-done((f32[32,1536]{1,0:T(8,128)S(1)}, f32[32,1536]{1,0:T(8,128)}, u32[]{:S(2)}) %copy-start.4) | copy-done | bytes 196632
  36.1 1.5 %assemble.1 = (f32[36,8,1536]{2,1,0:T(8,128)S(1)}, f32[36,8,1536]{2,1,0:T(8,128)S(1)}, f32[36,8,384]{2,1,0:T(8,128)S(1)}, f32[26,8,1536]{2,1,0:T(8,128)S(1)}) custom-call(s32[3]{0:T(128)S(1)} %pad_add_fusion.place, f32[32,1536]{1,0:T(8,128)S(1)} %copy-done.4, f32[16,8,1536]{2,1,0:T(8,128)S(1)} %get-tuple-element.22.own_weight, ...), custom_call_target="tpu_custom_call" | custom-call | tf_op jit(solution)/shard_map/assemble/pallas_call | solution.py:392
  37.6 6.6 %fine.1 = (f32[32,384]{1,0:T(8,128)S(1)}, f32[32,384]{1,0:T(8,128)S(1)}, f32[32,384]{1,0:T(8,128)S(1)}) custom-call(s32[3]{0:T(128)S(1)} %pad_add_fusion.place, s32[16]{0:T(128)S(1)} %copy-done.14, f32[16]{0:T(128)S(1)} %copy-done.15, f32[1,32]{1,0:T(1,128)S(1)} %slice.8.extra_a, f32[1,32]{1,0:T(1,128)S(1)} %slice.9.extra_b, f32[32,384]{1,0:T(8,128)S(1)} %total.1.own, ...), custom_call_target="tpu_custom_call" | custom-call | tf_op jit(solution)/shard_map/fine/pallas_call | solution.py:392
  44.3 3.9 %collective-permute-start.8 = (f32[32,384]{1,0:T(8,128)S(1)}, f32[32,384]{1,0:T(8,128)S(1)}, u32[]{:S(2)}, u32[]{:S(2)}) collective-permute-start(f32[32,384]{1,0:T(8,128)S(1)} %get-tuple-element.29), channel_id=1, source_target_pairs={{0,15},{1,2},{2,1},{3,4},{4,3},{5,6},{6,5},{7,8},{8,7},{9,10},{10,... | collective-permute-start | bytes 147464 | tf_op jit(solution)/shard_map/ppermute | solution.py:486
  48.2 1.8 %collective-permute-done.8.got_b = f32[32,384]{1,0:T(8,128)S(1)} collective-permute-done((f32[32,384]{1,0:T(8,128)S(1)}, f32[32,384]{1,0:T(8,128)S(1)}, u32[]{:S(2)}, u32[]{:S(2)}) %collective-permute-start.8) | collective-permute-done | bytes 49184 | tf_op jit(solution)/shard_map/ppermute | solution.py:486
  50.1 16.7 %all_to_all.10.adjoint = f32[8,32,384]{2,1,0:T(8,128)S(1)} all-to-all(f32[8,32,384]{2,1,0:T(8,128)S(1)} %copies.1), channel_id=1, replica_groups=mesh['mem'=8,'lat'=16] {'mem'}, dimensions={0} | all-to-all | bytes 786432 | tf_op jit(solution)/shard_map/all_to_all | solution.py:492
  66.8 1.3 %lower.1 = (f32[96,96]{1,0:T(8,128)S(1)}, f32[96,96]{1,0:T(8,128)S(1)}, f32[96,96]{1,0:T(8,128)S(1)}) custom-call(s32[3]{0:T(128)S(1)} %pad_add_fusion.place, f32[96,96]{1,0:T(8,128)S(1)} %bitcast.11, f32[6,256,384]{2,1,0:T(8,128)S(1)} %arrange.1.pert, f32[8,32,384]{2,1,0:T(8,128)S(1)} %all_to_all.10.adjoint, bf16[48,256]{1,0:T(8,128)(2,1)S(1)} %copy-done.13, ...), custom_call_target="tpu_custom_call" | custom-call | tf_op jit(solution)/shard_map/lower/pallas_call | solution.py:392
  68.2 3.0 %collective-permute-start.10 = (f32[96,96]{1,0:T(8,128)S(1)}, f32[96,96]{1,0:T(8,128)S(1)}, u32[]{:S(2)}, u32[]{:S(2)}) collective-permute-start(f32[96,96]{1,0:T(8,128)S(1)} %get-tuple-element.32), channel_id=1, source_target_pairs={{0,15},{1,2},{2,1},{3,4},{4,3},{5,6},{6,5},{7,8},{8,7},{9,10},{10,... | collective-permute-start | bytes 110600 | tf_op jit(solution)/shard_map/ppermute | solution.py:498
  71.2 2.7 %collective-permute-done.10 = f32[96,96]{1,0:T(8,128)S(1)} collective-permute-done((f32[96,96]{1,0:T(8,128)S(1)}, f32[96,96]{1,0:T(8,128)S(1)}, u32[]{:S(2)}, u32[]{:S(2)}) %collective-permute-start.10) | collective-permute-done | bytes 36896 | tf_op jit(solution)/shard_map/ppermute | solution.py:498
  (49 shorter events, 3.4 us)
Async XLA Ops:
  0.0 6.9 %collective-permute-start.2 = (f32[96,96]{1,0:T(8,128)}, f32[96,96]{1,0:T(8,128)S(1)}, u32[]{:S(2)}, u32[]{:S(2)}) collective-permute-start(f32[96,96]{1,0:T(8,128)} %bitcast.8), channel_id=1, source_target_pairs={{0,1},{1,0},{2,3},{3,2},{4,5},{5,4},{6,7},{7,6},{8,9},{9,8},{10,11... | collective-permute-start | bytes 110600 | tf_op jit(solution)/shard_map/ppermute | solution.py:435
  0.0 7.3 %collective-permute-start.3 = (f32[96,96]{1,0:T(8,128)}, f32[96,96]{1,0:T(8,128)S(1)}, u32[]{:S(2)}, u32[]{:S(2)}) collective-permute-start(f32[96,96]{1,0:T(8,128)} %bitcast.9), channel_id=1, source_target_pairs={{0,15},{1,2},{2,1},{3,4},{4,3},{5,6},{6,5},{7,8},{8,7},{9,10},{10,... | collective-permute-start | bytes 110600 | tf_op jit(solution)/shard_map/ppermute | solution.py:435
  5.3 1.3 %copy-start.1 = (bf16[6,64,4,384]{3,2,1,0:T(4,128)(2,1)S(1)}, bf16[6,64,4,384]{3,2,1,0:T(4,128)(2,1)}, u32[]{:S(2)}) copy-start(bf16[6,64,4,384]{3,2,1,0:T(4,128)(2,1)} %pert.1) | copy-start | bytes 3538948
  6.5 0.9 %copy-start.10 = (bf16[96,384]{1,0:T(8,128)(2,1)S(1)}, bf16[96,384]{1,0:T(8,128)(2,1)}, u32[]{:S(2)}) copy-start(bf16[96,384]{1,0:T(8,128)(2,1)} %constant.26.clone.lon_up) | copy-start | bytes 221188
  6.5 0.9 %copy-start.11 = (bf16[256,96]{1,0:T(8,128)(2,1)S(1)}, bf16[256,96]{1,0:T(8,128)(2,1)}, u32[]{:S(2)}) copy-start(bf16[256,96]{1,0:T(8,128)(2,1)} %constant.28.clone.mix) | copy-start | bytes 147460
  6.9 9.3 %copy-start.14 = (s32[16]{0:T(128)S(1)}, s32[16]{0:T(128)}, u32[]{:S(2)}) copy-start(s32[16]{0:T(128)} %source.1) | copy-start | bytes 196
  6.9 9.3 %copy-start.15 = (f32[16]{0:T(128)S(1)}, f32[16]{0:T(128)}, u32[]{:S(2)}) copy-start(f32[16]{0:T(128)} %frac.1) | copy-start | bytes 196
  9.5 18.0 %all-to-all-start = ((f32[8,32,384]{2,1,0:T(8,128)}), f32[8,32,384]{2,1,0:T(8,128)S(1)}, u32[]{:S(2)}, u32[]{:S(2)}) async-start(f32[8,32,384]{2,1,0:T(8,128)} %raise.1), calls=%async_computation | async-start | bytes 786432 | tf_op jit(solution)/shard_map/all_to_all | solution.py:463
  16.3 1.9 %copy-start = (bf16[64,16,1536]{2,1,0:T(8,128)(2,1)S(1)}, bf16[64,16,1536]{2,1,0:T(8,128)(2,1)}, u32[]{:S(2)}) copy-start(bf16[64,16,1536]{2,1,0:T(8,128)(2,1)} %weight.1) | copy-start | bytes 9437188
  18.2 1.0 %copy-start.2 = (bf16[512,512]{1,0:T(8,128)(2,1)S(1)}, bf16[512,512]{1,0:T(8,128)(2,1)}, u32[]{:S(2)}) copy-start(bf16[512,512]{1,0:T(8,128)(2,1)} %constant.30.clone.select) | copy-start | bytes 1572868
  20.1 0.9 %copy-start.9 = (f32[16,1536]{1,0:T(8,128)S(1)}, f32[16,1536]{1,0:T(8,128)}, u32[]{:S(2)}) copy-start(f32[16,1536]{1,0:T(8,128)} %east.1) | copy-start | bytes 294916
  24.8 6.3 %collective-permute-start = (f32[64,1536]{1,0:T(8,128)}, f32[64,1536]{1,0:T(8,128)}, u32[]{:S(2)}, u32[]{:S(2)}) collective-permute-start(f32[64,1536]{1,0:T(8,128)} %get-tuple-element.19), channel_id=1, source_target_pairs={{0,1},{1,0},{2,3},{3,2},{4,5},{5,4},{6,7},{7,6},{8,9},{9,8},{10,11... | collective-permute-start | bytes 1179656 | tf_op jit(solution)/shard_map/ppermute | solution.py:456
  24.8 9.6 %collective-permute-start.1 = (f32[64,1536]{1,0:T(8,128)}, f32[64,1536]{1,0:T(8,128)}, u32[]{:S(2)}, u32[]{:S(2)}) collective-permute-start(f32[64,1536]{1,0:T(8,128)} %get-tuple-element.20), channel_id=1, source_target_pairs={{0,15},{1,2},{2,1},{3,4},{4,3},{5,6},{6,5},{7,8},{8,7},{9,10},{10,... | collective-permute-start | bytes 1179656 | tf_op jit(solution)/shard_map/ppermute | solution.py:455
  27.6 1.3 %collective-permute-start.4 = (f32[32,384]{1,0:T(8,128)S(1)}, f32[32,384]{1,0:T(8,128)S(1)}, u32[]{:S(2)}, u32[]{:S(2)}) collective-permute-start(f32[32,384]{1,0:T(8,128)S(1)} %total.1.own), channel_id=1, source_target_pairs={{0,1},{1,0},{2,3},{3,2},{4,5},{5,4},{6,7},{7,6},{8,9},{9,8},{10,11... | collective-permute-start | bytes 147464 | tf_op jit(solution)/shard_map/ppermute | solution.py:465
  28.9 8.7 %collective-permute-start.5 = (f32[64,384]{1,0:T(8,128)S(1)}, f32[64,384]{1,0:T(8,128)S(1)}, u32[]{:S(2)}, u32[]{:S(2)}) collective-permute-start(f32[64,384]{1,0:T(8,128)S(1)} %pad_maximum_fusion), channel_id=1, source_target_pairs={{0,2},{1,3},{2,0},{3,1},{4,6},{5,7},{6,4},{7,5},{8,10},{9,11},{10,... | collective-permute-start | bytes 294920 | tf_op jit(solution)/shard_map/ppermute | solution.py:468
  29.0 8.6 %collective-permute-start.6 = (f32[64,384]{1,0:T(8,128)S(1)}, f32[64,384]{1,0:T(8,128)S(1)}, u32[]{:S(2)}, u32[]{:S(2)}) collective-permute-start(f32[64,384]{1,0:T(8,128)S(1)} %pad_maximum_fusion), channel_id=1, source_target_pairs={{0,14},{1,15},{2,4},{3,5},{4,2},{5,3},{6,8},{7,9},{8,6},{9,7},{10,... | collective-permute-start | bytes 294920 | tf_op jit(solution)/shard_map/ppermute | solution.py:467
  35.1 0.9 %copy-start.4 = (f32[32,1536]{1,0:T(8,128)S(1)}, f32[32,1536]{1,0:T(8,128)}, u32[]{:S(2)}) copy-start(f32[32,1536]{1,0:T(8,128)} %copy-done.3) | copy-start | bytes 589828
  37.6 29.2 %copy-start.6 = (f32[6,16,1,96]{3,2,1,0:T(1,128)S(1)}, f32[6,16,1,96]{3,2,1,0:T(1,128)}, u32[]{:S(2)}) copy-start(f32[6,16,1,96]{3,2,1,0:T(1,128)} %param.13) | copy-start | bytes 110596
  37.6 29.2 %copy-start.7 = (bf16[384,96]{1,0:T(8,128)(2,1)S(1)}, bf16[384,96]{1,0:T(8,128)(2,1)}, u32[]{:S(2)}) copy-start(bf16[384,96]{1,0:T(8,128)(2,1)} %constant.27.clone.lon_down) | copy-start | bytes 221188
  37.6 29.2 %copy-start.13 = (bf16[48,256]{1,0:T(8,128)(2,1)S(1)}, bf16[48,256]{1,0:T(8,128)(2,1)}, u32[]{:S(2)}) copy-start(bf16[48,256]{1,0:T(8,128)(2,1)} %constant.29.clone.mix_t) | copy-start | bytes 73732
  44.2 4.0 %collective-permute-start.7 = (f32[32,384]{1,0:T(8,128)S(1)}, f32[32,384]{1,0:T(8,128)S(1)}, u32[]{:S(2)}, u32[]{:S(2)}) collective-permute-start(f32[32,384]{1,0:T(8,128)S(1)} %get-tuple-element.28), channel_id=1, source_target_pairs={{0,1},{1,0},{2,3},{3,2},{4,5},{5,4},{6,7},{7,6},{8,9},{9,8},{10,11... | collective-permute-start | bytes 147464 | tf_op jit(solution)/shard_map/ppermute | solution.py:487
  44.3 5.7 %collective-permute-start.8 = (f32[32,384]{1,0:T(8,128)S(1)}, f32[32,384]{1,0:T(8,128)S(1)}, u32[]{:S(2)}, u32[]{:S(2)}) collective-permute-start(f32[32,384]{1,0:T(8,128)S(1)} %get-tuple-element.29), channel_id=1, source_target_pairs={{0,15},{1,2},{2,1},{3,4},{4,3},{5,6},{6,5},{7,8},{8,7},{9,10},{10,... | collective-permute-start | bytes 147464 | tf_op jit(solution)/shard_map/ppermute | solution.py:486
  68.2 5.7 %collective-permute-start.10 = (f32[96,96]{1,0:T(8,128)S(1)}, f32[96,96]{1,0:T(8,128)S(1)}, u32[]{:S(2)}, u32[]{:S(2)}) collective-permute-start(f32[96,96]{1,0:T(8,128)S(1)} %get-tuple-element.32), channel_id=1, source_target_pairs={{0,15},{1,2},{2,1},{3,4},{4,3},{5,6},{6,5},{7,8},{8,7},{9,10},{10,... | collective-permute-start | bytes 110600 | tf_op jit(solution)/shard_map/ppermute | solution.py:498
  71.2 2.7 %collective-permute-start.9 = (f32[96,96]{1,0:T(8,128)S(1)}, f32[96,96]{1,0:T(8,128)S(1)}, u32[]{:S(2)}, u32[]{:S(2)}) collective-permute-start(f32[96,96]{1,0:T(8,128)S(1)} %get-tuple-element.31), channel_id=1, source_target_pairs={{0,1},{1,0},{2,3},{3,2},{4,5},{5,4},{6,7},{7,6},{8,9},{9,8},{10,11... | collective-permute-start | bytes 110600 | tf_op jit(solution)/shard_map/ppermute | solution.py:499
  (4 other events, 3.1 us)

commit v3 on v2

--- a/solution.py
+++ b/solution.py
@@ -40,20 +40,41 @@
 
 
 def prepare_kernel(
-    place, weight, north, east, extra, select, order, coef, own_weight, buf_a, buf_b, level_weight, sem
+    place, source, frac, weight, north_all, east_all, select_all, order_all,
+    coef, own_weight, buf_a, buf_b, level_weight, north, east, select, order, extra, sems,
 ):
     odd = place[0] % 2
     levels, rows, lon = level_weight.shape
-    fetch = pltpu.make_async_copy(weight.at[pl.ds(place[2] * levels, levels)], level_weight, sem)
-    fetch.start()
+    copies = [
+        pltpu.make_async_copy(north_all, north, sems.at[0]),
+        pltpu.make_async_copy(east_all, east, sems.at[1]),
+        pltpu.make_async_copy(
+            weight.at[pl.ds(place[2] * levels, levels)], level_weight, sems.at[2]
+        ),
+        pltpu.make_async_copy(order_all, order, sems.at[3]),
+        pltpu.make_async_copy(select_all, select, sems.at[4]),
+    ]
+    for copy in copies:
+        copy.start()
+    lane = lax.broadcasted_iota(jnp.int32, (4, 128), 1)
+    tail = jnp.zeros((4, 128), F32)
+    for k in range(rows):
+        tail = jnp.where(lane == k, frac[k], tail)
+        tail = jnp.where(lane == rows + k, source[k].astype(F32), tail)
+    extra[...] = jnp.zeros(extra.shape, F32)
+    extra[:, 0:128] = tail
+    copies[0].wait()
+    copies[1].wait()
     stacked = jnp.concatenate([north[...], east[...]], axis=0)
     hi = stacked.astype(BF16)
     rest = stacked - hi.astype(F32)
     mid = rest.astype(BF16)
     low = (rest - mid.astype(F32)).astype(BF16)
-    fetch.wait()
+    copies[2].wait()
+    copies[3].wait()
     values = dot(order[...], level_weight[...].reshape(levels * rows, lon)).astype(BF16)
     everything = jnp.concatenate([values, hi, mid, low], axis=0)
+    copies[4].wait()
     many = levels * rows
     quarter = lon // 4
     for c in range(lon // 512):
@@ -65,12 +86,12 @@
             to = slice(quarter * r + 128 * c, quarter * r + 128 * c + 128)
             frm = slice(128 * r, 128 * r + 128)
             coef[:, to] = cpart[:, frm]
-            own_weight[:, :, to] = wpart[:, frm].reshape(rows, levels, 128)
+            own_weight[:, :, to] = wpart[:, frm].reshape(rows, levels, 128).astype(BF16)
 
     def fill(buf, upper):
         first = rows - PASSES if upper else 0
         for k in range(PASSES):
-            buf[8 * k : 8 * k + 8, :] = own_weight[first + k]
+            buf[8 * k : 8 * k + 8, :] = own_weight[first + k].astype(F32)
         first = rows - HALO if upper else 0
         base = 8 * PASSES
         buf[base : base + HALO, :] = coef[first : first + HALO, :]
@@ -103,7 +124,7 @@
 
     for k in range(rows):
         put(HALO + k, coef[k : k + 1, :], coef[rows + k : rows + k + 1, :])
-        weight[PASSES + k] = own_weight[k]
+        weight[PASSES + k] = own_weight[k].astype(F32)
 
     def side(buf, start, wstart):
         base = 8 * PASSES
@@ -127,19 +148,24 @@
         north[HALO - 1] = jnp.zeros(north.shape[1:], F32)
 
 
-def arrange_kernel(pert, out):
-    members, lev, band, _ = pert.shape
-    for m in range(members):
-        values = pert[m].astype(F32)
-        for k in range(lev):
-            out[m, band * k : band * k + band, :] = values[k]
-
-
-def raise_kernel(place, own, got_a, got_b, pert, lon_up, mix, out, x, acc):
+def raise_kernel(
+    place, got_a, got_b, own_all, lon_all, mix_all, stored, out, pert, x, acc, raw, flat, own, lon_up,
+    mix, sems,
+):
     lat, last = place[0], place[1] - 1
     odd = lat % 2
-    members = pert.shape[0]
+    members, levels, band, _ = raw.shape
     lev = own.shape[0] // members
+    small = [
+        pltpu.make_async_copy(own_all, own, sems.at[members]),
+        pltpu.make_async_copy(lon_all, lon_up, sems.at[members + 1]),
+        pltpu.make_async_copy(mix_all, mix, sems.at[members + 2]),
+    ]
+    copies = [pltpu.make_async_copy(stored.at[m], raw.at[m], sems.at[m]) for m in range(members)]
+    for copy in small + copies:
+        copy.start()
+    for copy in small:
+        copy.wait()
 
     def put(step, ref):
         for m in range(members):
@@ -175,9 +201,15 @@
     hi, lo = split2(x[...])
     wide = dot(hi, lon_up[...]) + dot(lo, lon_up[...])
     for m in range(members):
+        copies[m].wait()
+        values = raw[m].astype(F32)
+        for k in range(levels):
+            flat[band * k : band * k + band, :] = values[k]
+        spread = flat[...]
+        pert[m] = spread.astype(BF16)
         hi, lo = split2(wide[3 * lev * m : 3 * lev * (m + 1), :])
         field = dot(mix[...], jnp.concatenate([hi, lo], axis=0))
-        term = field * pert[m]
+        term = field * spread
         if m == 0:
             acc[...] = term
         elif m < members - 1:
@@ -199,10 +231,23 @@
             out[8 * row : 8 * row + 8, lanes] = sums[pl.ds(n * c + row, 8, stride=rows), :]
 
 
+def join_kernel(mine, mate, out):
+    half = mine.shape[0]
+    out[:half] = mine[...]
+    out[half:] = mate[...]
+
+
 def fine_kernel(
-    place, source, frac, extra_a, extra_b, own, mate, near_pair, far_pair,
-    north, east, west, weight, keep, send_a, send_b, mid, v, acc,
+    place, source, frac, far_a, far_b, own, mate, near_pair, far_pair,
+    north, east, west, weight, keep, send_a, send_b, mid, v, acc, extra_a, extra_b, sems,
 ):
+    at = 8 * PASSES + 2 * HALO
+    copies = [
+        pltpu.make_async_copy(far_a.at[at : at + 1, 0:128], extra_a, sems.at[0]),
+        pltpu.make_async_copy(far_b.at[at : at + 1, 0:128], extra_b, sems.at[1]),
+    ]
+    for copy in copies:
+        copy.start()
     lat, last = place[0], place[1] - 1
     odd = lat % 2
     lon = own.shape[1]
@@ -237,6 +282,8 @@
             else:
                 gather(case % 2 == 0, near_pair, far_pair)
 
+    for copy in copies:
+        copy.wait()
     origin = (lat - 2) * band
     for i in range(n):
         k = i - HALO
@@ -358,7 +405,7 @@
     lev = own.shape[0] // members
     field = adjoint[...].reshape(pert.shape[1], pert.shape[2])
     for m in range(members):
-        hi, lo = split2(field * pert[m])
+        hi, lo = split2(field * pert[m].astype(F32))
         wide[3 * lev * m : 3 * lev * (m + 1), :] = dot(mix_t[...], hi) + dot(mix_t[...], lo)
     hi, lo = split2(wide[...])
     narrow = dot(hi, lon_down[...]) + dot(lo, lon_down[...])
@@ -382,6 +429,14 @@
     return pl.BlockSpec(memory_space=pltpu.VMEM)
 
 
+def anywhere():
+    return pl.BlockSpec(memory_space=pl.ANY)
+
+
+def in_hbm(x):
+    return pltpu.with_memory_space_constraint(x, pltpu.HBM)
+
+
 def smem():
     return pl.BlockSpec(memory_space=pltpu.SMEM)
 
@@ -433,37 +488,64 @@
 
     own = controls.reshape(members * clev, clon)
     low_high = [lax.ppermute(own, "lat", across), lax.ppermute(own, "lat", mates)]
-    pert = call(arrange_kernel, "arrange", (members, lev * band, lon), [], [], [perturbations])
-
-    tail = jnp.concatenate([fine_frac, fine_source.astype(F32)])
-    tail = jnp.pad(tail[None], ((0, 3), (0, fine_lon - 2 * rows)))
+
     spots = 8 * PASSES + 2 * HALO + 4
     coef, own_weight, buf_a, buf_b = pl.pallas_call(
         prepare_kernel,
         name="prepare",
         out_shape=[
             jax.ShapeDtypeStruct((2 * rows, fine_lon), F32),
-            jax.ShapeDtypeStruct((rows, part, fine_lon), F32),
+            jax.ShapeDtypeStruct((rows, part, fine_lon), BF16),
             jax.ShapeDtypeStruct((spots, fine_lon), F32),
             jax.ShapeDtypeStruct((spots, fine_lon), F32),
         ],
-        in_specs=[smem(), pl.BlockSpec(memory_space=pltpu.HBM)] + [vmem()] * 5,
+        in_specs=[smem()] * 3 + [anywhere()] * 5,
         out_specs=[vmem()] * 4,
-        scratch_shapes=[pltpu.VMEM((part, rows, fine_lon), BF16), pltpu.SemaphoreType.DMA(())],
+        scratch_shapes=[
+            pltpu.VMEM((part, rows, fine_lon), BF16),
+            pltpu.VMEM((rows, fine_lon), F32),
+            pltpu.VMEM((rows, fine_lon), F32),
+            pltpu.VMEM((512, 512), BF16),
+            pltpu.VMEM((part * rows, part * rows), BF16),
+            pltpu.VMEM((4, fine_lon), F32),
+            pltpu.SemaphoreType.DMA((5,)),
+        ],
         compiler_params=pltpu.CompilerParams(vmem_limit_bytes=VMEM_LIMIT),
-    )(place, precision_weight, north_coef, east_coef, tail, pick, order)
+    )(
+        place, fine_source, fine_frac,
+        *[in_hbm(x) for x in (precision_weight, north_coef, east_coef, pick, order)],
+    )
     far_b = lax.ppermute(buf_b, "lat", across)
     far_a = lax.ppermute(buf_a, "lat", mates)
 
-    local_sum = call(
-        raise_kernel, "raise", (ranks, part * band, lon),
-        [(3 * members * clev, clon), (lev * band, lon)],
-        [place], [own, low_high[1], low_high[0], pert, lon_up, mix_up],
+    local_sum, pert = pl.pallas_call(
+        raise_kernel,
+        name="raise",
+        out_shape=[
+            jax.ShapeDtypeStruct((ranks, part * band, lon), F32),
+            jax.ShapeDtypeStruct((members, lev * band, lon), BF16),
+        ],
+        in_specs=[smem()] + [vmem()] * 2 + [anywhere()] * 4,
+        out_specs=[vmem()] * 2,
+        scratch_shapes=[
+            pltpu.VMEM((3 * members * clev, clon), F32),
+            pltpu.VMEM((lev * band, lon), F32),
+            pltpu.VMEM((members, lev, band, lon), BF16),
+            pltpu.VMEM((lev * band, lon), F32),
+            pltpu.VMEM((members * clev, clon), F32),
+            pltpu.VMEM(lon_up.shape, BF16),
+            pltpu.VMEM(mix_up.shape, BF16),
+            pltpu.SemaphoreType.DMA((members + 3,)),
+        ],
+        compiler_params=pltpu.CompilerParams(vmem_limit_bytes=VMEM_LIMIT),
+    )(
+        place, low_high[1], low_high[0],
+        *[in_hbm(x) for x in (own, lon_up, mix_up, perturbations)],
     )
     parts = lax.all_to_all(local_sum, "mem", 0, 0, tiled=True)
     mine = call(total_kernel, "total", (band * part, lon), [(band * part * lon // 128, 128)], [], [parts])
     mate = lax.ppermute(mine, "lat", mates)
-    pair = jnp.concatenate([mine, mate], axis=0)
+    pair = call(join_kernel, "join", (2 * band * part, lon), [], [], [mine, mate])
     far_pair = lax.ppermute(pair, "lat", far_chips)
     near_pair = lax.ppermute(pair, "lat", near_chips)
 
@@ -473,15 +555,25 @@
         [(n, 8, fine_lon), (n, 8, fine_lon), (n, 8, lon), (rows + 2 * PASSES, 8, fine_lon)],
         [], [place], [coef, own_weight, far_a, far_b],
     )
-    at = 8 * PASSES + 2 * HALO
-    extra_a = far_a[at : at + 1, : 2 * rows]
-    extra_b = far_b[at : at + 1, : 2 * rows]
-    piece = (band * part, lon)
-    keep, send_a, send_b = call(
-        fine_kernel, "fine", [piece, piece, piece],
-        [(5 * band, 8, lon), (n, 8, fine_lon), (3 * band, 8, lon)],
-        [place, fine_source, fine_frac, extra_a, extra_b],
-        [mine, mate, near_pair, far_pair, north, east, west, weight],
+    piece = jax.ShapeDtypeStruct((band * part, lon), F32)
+    keep, send_a, send_b = pl.pallas_call(
+        fine_kernel,
+        name="fine",
+        out_shape=[piece] * 3,
+        in_specs=[smem()] * 3 + [anywhere()] * 2 + [vmem()] * 8,
+        out_specs=[vmem()] * 3,
+        scratch_shapes=[
+            pltpu.VMEM((5 * band, 8, lon), F32),
+            pltpu.VMEM((n, 8, fine_lon), F32),
+            pltpu.VMEM((3 * band, 8, lon), F32),
+            pltpu.SMEM((1, 128), F32),
+            pltpu.SMEM((1, 128), F32),
+            pltpu.SemaphoreType.DMA((2,)),
+        ],
+        compiler_params=pltpu.CompilerParams(vmem_limit_bytes=VMEM_LIMIT),
+    )(
+        place, fine_source, fine_frac, far_a, far_b, mine, mate, near_pair, far_pair,
+        north, east, west, weight,
     )
     got_b = lax.ppermute(send_b, "lat", across)
     got_a = lax.ppermute(send_a, "lat", mates)

time: 75.1 us -> 70.6 us (0.940)
  local copies, waits for them, and re-layouts: 9.94 us -> 0.02 us
  waiting for transfers between devices: 8.72 us -> 15.6 us
  blocking collectives: 16.7 us -> 14 us
  Pallas kernels: 14.3 us -> 16.8 us
  starting transfers between devices: 23.9 us -> 23.1 us
    pallas_call x0 -> x2, Pallas kernels: none -> 11.1 us  [the longest x1 7.11 us: body(): pl.pallas_call(fine_kernel, name='fine', out_shape=[piece] * 3, in_specs=...]
    pallas_call x7 -> x5, Pallas kernels: 11.9 us -> 2.38 us  [call(): pl.pallas_call(kernel, name=name, out_shape=shapes if many else shapes[0]...]
    unnamed x32 -> x10, local copies, waits for them, and re-layouts: 8.57 us -> 0.02 us
    all_to_all x1, waiting for transfers between devices: 0.01 us -> 2.86 us  [body(): parts = lax.all_to_all(local_sum, 'mem', 0, 0, tiled=True)]
    all_to_all x1, blocking collectives: 16.7 us -> 14 us  [body(): adjoint = lax.all_to_all(copies, 'mem', 0, 0, tiled=True)]
    ppermute x1, waiting for transfers between devices: 2.63 us -> 0.01 us  [body(): far_b = lax.ppermute(buf_b, 'lat', across)]
    ppermute x1, waiting for transfers between devices: 0.01 us -> 2.2 us  [body(): far_pair = lax.ppermute(pair, 'lat', far_chips)]
    ppermute x1, waiting for transfers between devices: 0.37 us -> 1.99 us  [body(): lax.ppermute(own, 'lat', across)]
  transfers between devices with their start and end apart: 12 -> 12, of which waited for: 5 -> 7; matrix products, arithmetic and copies ran while one was open for 2% -> 0% of each run, Pallas kernels for 6% -> 6%
where the time goes in v3:
time: 70.6 us; the launch traced here: 70.3 us
  starting transfers between devices  23.1 us (33%)
  Pallas kernels  16.8 us (24%)
  waiting for transfers between devices  15.6 us (22%)
  blocking collectives  14 us (20%)
  other arithmetic  0.71 us (1%)
    all_to_all x1, blocking collectives, body(): adjoint = lax.all_to_all(copies, 'mem', 0, 0, tiled=True)  14 us
    pallas_call x1, Pallas kernels, body(): pl.pallas_call(fine_kernel, name='fine', out_shape=[piece] * 3, in_specs=...  7.11 us
    all_to_all x1, starting transfers between devices, body(): parts = lax.all_to_all(local_sum, 'mem', 0, 0, tiled=True)  6.65 us
    ppermute x2, waiting for transfers between devices, body(): got_b = lax.ppermute(send_b, 'lat', across)  6.06 us
    ppermute x2, starting transfers between devices, body(): got_b = lax.ppermute(send_b, 'lat', across)  5.34 us
    ppermute x1, starting transfers between devices, body(): lax.ppermute(own, 'lat', across)  5.19 us
    pallas_call x1, Pallas kernels, body(): pl.pallas_call(raise_kernel, name='raise', out_shape=[jax.ShapeDtypeStruc...  4.03 us
    pallas_call x1, Pallas kernels, body(): pl.pallas_call(prepare_kernel, name='prepare', out_shape=[jax.ShapeDtypeS...  3.3 us
  transfers between devices with their start and end apart: 12, of which 7 were waited for; matrix products, arithmetic and copies ran while one was open for 0% of the time, Pallas kernels for 6%

profile of v3, /device:TPU:0, one launch (start us, length us, event | category | flops | bytes accessed | tf_op | source)
XLA Modules:
  0.0 70.3 jit_solution(12861927405968650487)
XLA Ops:
  0.0 5.2 %collective-permute-start.1 = (f32[96,96]{1,0:T(8,128)}, f32[96,96]{1,0:T(8,128)S(1)}, u32[]{:S(2)}, u32[]{:S(2)}) collective-permute-start(f32[96,96]{1,0:T(8,128)} %bitcast.7), channel_id=1, source_target_pairs={{0,15},{1,2},{2,1},{3,4},{4,3},{5,6},{6,5},{7,8},{8,7},{9,10},{10,... | collective-permute-start | bytes 110600 | tf_op jit(solution)/shard_map/ppermute | solution.py:490
  5.3 2.0 %collective-permute-done.1.got_b = f32[96,96]{1,0:T(8,128)S(1)} collective-permute-done((f32[96,96]{1,0:T(8,128)}, f32[96,96]{1,0:T(8,128)S(1)}, u32[]{:S(2)}, u32[]{:S(2)}) %collective-permute-start.1) | collective-permute-done | bytes 36896 | tf_op jit(solution)/shard_map/ppermute | solution.py:490
  7.3 4.0 %raise.1 = (f32[8,32,384]{2,1,0:T(8,128)}, bf16[6,256,384]{2,1,0:T(8,128)(2,1)S(1)}) custom-call(s32[3]{0:T(128)S(1)} %pad_add_fusion.place, f32[96,96]{1,0:T(8,128)S(1)} %collective-permute-done.got_a, f32[96,96]{1,0:T(8,128)S(1)} %collective-permute-done.1.got_b, f32[96,96]{1,0:T(8,128)} %bitcast.8, bf16[96,384]{1,0:T(8,128)(2,1)} %constant.23.clone.lon_all, ...), custom_call_target="tpu_custom_call" | custom-call | tf_op jit(solution)/shard_map/raise/pallas_call | solution.py:521
  11.3 6.7 %all-to-all-start = ((f32[8,32,384]{2,1,0:T(8,128)}), f32[8,32,384]{2,1,0:T(8,128)S(1)}, u32[]{:S(2)}, u32[]{:S(2)}) async-start(f32[8,32,384]{2,1,0:T(8,128)} %get-tuple-element.24), calls=%async_computation | async-start | bytes 786432 | tf_op jit(solution)/shard_map/all_to_all | solution.py:545
  18.0 3.3 %prepare.1 = (f32[32,1536]{1,0:T(8,128)S(1)}, bf16[16,8,1536]{2,1,0:T(8,128)(2,1)S(1)}, f32[64,1536]{1,0:T(8,128)}, f32[64,1536]{1,0:T(8,128)S(1)}) custom-call(s32[3]{0:T(128)S(1)} %pad_add_fusion.place, s32[16]{0:T(128)S(1)} %copy-done.3, f32[16]{0:T(128)S(1)} %copy-done.4, bf16[64,16,1536]{2,1,0:T(8,128)(2,1)} %weight.1, f32[16,1536]{1,0:T(8,128)} %north_all.1, ...), custom_call_target="tpu_custom_call" | custom-call | tf_op jit(solution)/shard_map/prepare/pallas_call | solution.py:493
  21.3 0.1 collective-permute-start.2
  21.4 3.0 %collective-permute-start.3 = (f32[64,1536]{1,0:T(8,128)S(1)}, f32[64,1536]{1,0:T(8,128)S(1)}, u32[]{:S(2)}, u32[]{:S(2)}) collective-permute-start(f32[64,1536]{1,0:T(8,128)S(1)} %get-tuple-element.23), channel_id=1, source_target_pairs={{0,15},{1,2},{2,1},{3,4},{4,3},{5,6},{6,5},{7,8},{8,7},{9,10},{10,... | collective-permute-start | bytes 1179656 | tf_op jit(solution)/shard_map/ppermute | solution.py:518
  24.4 2.9 %all-to-all-done.parts = f32[8,32,384]{2,1,0:T(8,128)S(1)} async-done(((f32[8,32,384]{2,1,0:T(8,128)}), f32[8,32,384]{2,1,0:T(8,128)S(1)}, u32[]{:S(2)}, u32[]{:S(2)}) %all-to-all-start) | async-done | bytes 393248 | tf_op jit(solution)/shard_map/all_to_all | solution.py:545
  27.2 0.1 collective-permute-start.4
  27.3 1.2 %collective-permute-done.4.mate = f32[32,384]{1,0:T(8,128)S(1)} collective-permute-done((f32[32,384]{1,0:T(8,128)S(1)}, f32[32,384]{1,0:T(8,128)S(1)}, u32[]{:S(2)}, u32[]{:S(2)}) %collective-permute-start.4) | collective-permute-done | bytes 49184 | tf_op jit(solution)/shard_map/ppermute | solution.py:547
  28.6 0.1 collective-permute-start.5
  28.7 2.6 %collective-permute-start.6 = (f32[64,384]{1,0:T(8,128)S(1)}, f32[64,384]{1,0:T(8,128)S(1)}, u32[]{:S(2)}, u32[]{:S(2)}) collective-permute-start(f32[64,384]{1,0:T(8,128)S(1)} %join.1), channel_id=1, source_target_pairs={{0,14},{1,15},{2,4},{3,5},{4,2},{5,3},{6,8},{7,9},{8,6},{9,7},{10,... | collective-permute-start | bytes 294920 | tf_op jit(solution)/shard_map/ppermute | solution.py:549
  31.3 0.9 %assemble.1 = (f32[36,8,1536]{2,1,0:T(8,128)S(1)}, f32[36,8,1536]{2,1,0:T(8,128)S(1)}, f32[36,8,384]{2,1,0:T(8,128)S(1)}, f32[26,8,1536]{2,1,0:T(8,128)S(1)}) custom-call(s32[3]{0:T(128)S(1)} %pad_add_fusion.place, f32[32,1536]{1,0:T(8,128)S(1)} %get-tuple-element.25.coef, bf16[16,8,1536]{2,1,0:T(8,128)(2,1)S(1)} %get-tuple-element.26.own_weight, ...), custom_call_target="tpu_custom_call" | custom-call | tf_op jit(solution)/shard_map/assemble/pallas_call | solution.py:447
  32.2 1.3 %collective-permute-done.5.near_pair = f32[64,384]{1,0:T(8,128)S(1)} collective-permute-done((f32[64,384]{1,0:T(8,128)S(1)}, f32[64,384]{1,0:T(8,128)S(1)}, u32[]{:S(2)}, u32[]{:S(2)}) %collective-permute-start.5) | collective-permute-done | bytes 98336 | tf_op jit(solution)/shard_map/ppermute | solution.py:550
  33.5 2.2 %collective-permute-done.6.far_pair = f32[64,384]{1,0:T(8,128)S(1)} collective-permute-done((f32[64,384]{1,0:T(8,128)S(1)}, f32[64,384]{1,0:T(8,128)S(1)}, u32[]{:S(2)}, u32[]{:S(2)}) %collective-permute-start.6) | collective-permute-done | bytes 98336 | tf_op jit(solution)/shard_map/ppermute | solution.py:549
  35.7 7.1 %fine.1 = (f32[32,384]{1,0:T(8,128)S(1)}, f32[32,384]{1,0:T(8,128)S(1)}, f32[32,384]{1,0:T(8,128)S(1)}) custom-call(s32[3]{0:T(128)S(1)} %pad_add_fusion.place, s32[16]{0:T(128)S(1)} %copy-done.3, f32[16]{0:T(128)S(1)} %copy-done.4, f32[64,1536]{1,0:T(8,128)S(1)} %collective-permute-done.2.got_a.far_a, f32[64,1536]{1,0:T(8,128)S(1)} %collective-permute-done.3.got_b.far_b, ...), custom_call_target="tpu_custom_call" | custom-call | tf_op jit(solution)/shard_map/fine/pallas_call | solution.py:559
  42.8 0.1 collective-permute-start.7
  42.9 2.9 %collective-permute-start.8 = (f32[32,384]{1,0:T(8,128)S(1)}, f32[32,384]{1,0:T(8,128)S(1)}, u32[]{:S(2)}, u32[]{:S(2)}) collective-permute-start(f32[32,384]{1,0:T(8,128)S(1)} %get-tuple-element.33), channel_id=1, source_target_pairs={{0,15},{1,2},{2,1},{3,4},{4,3},{5,6},{6,5},{7,8},{8,7},{9,10},{10,... | collective-permute-start | bytes 147464 | tf_op jit(solution)/shard_map/ppermute | solution.py:578
  45.8 2.8 %collective-permute-done.8.got_b = f32[32,384]{1,0:T(8,128)S(1)} collective-permute-done((f32[32,384]{1,0:T(8,128)S(1)}, f32[32,384]{1,0:T(8,128)S(1)}, u32[]{:S(2)}, u32[]{:S(2)}) %collective-permute-start.8) | collective-permute-done | bytes 49184 | tf_op jit(solution)/shard_map/ppermute | solution.py:578
  48.6 14.0 %all_to_all.10.adjoint = f32[8,32,384]{2,1,0:T(8,128)S(1)} all-to-all(f32[8,32,384]{2,1,0:T(8,128)S(1)} %copies.1), channel_id=1, replica_groups=mesh['mem'=8,'lat'=16] {'mem'}, dimensions={0} | all-to-all | bytes 786432 | tf_op jit(solution)/shard_map/all_to_all | solution.py:584
  62.6 1.4 %lower.1 = (f32[96,96]{1,0:T(8,128)S(1)}, f32[96,96]{1,0:T(8,128)S(1)}, f32[96,96]{1,0:T(8,128)S(1)}) custom-call(s32[3]{0:T(128)S(1)} %pad_add_fusion.place, f32[96,96]{1,0:T(8,128)S(1)} %bitcast.9, bf16[6,256,384]{2,1,0:T(8,128)(2,1)S(1)} %get-tuple-element.21.pert, f32[8,32,384]{2,1,0:T(8,128)S(1)} %all_to_all.10.adjoint, bf16[48,256]{1,0:T(8,128)(2,1)S(1)} %copy-done.2, ...), custom_call_target="tpu_custom_call" | custom-call | tf_op jit(solution)/shard_map/lower/pallas_call | solution.py:447
  64.0 2.4 %collective-permute-start.10 = (f32[96,96]{1,0:T(8,128)S(1)}, f32[96,96]{1,0:T(8,128)S(1)}, u32[]{:S(2)}, u32[]{:S(2)}) collective-permute-start(f32[96,96]{1,0:T(8,128)S(1)} %get-tuple-element.36), channel_id=1, source_target_pairs={{0,15},{1,2},{2,1},{3,4},{4,3},{5,6},{6,5},{7,8},{8,7},{9,10},{10,... | collective-permute-start | bytes 110600 | tf_op jit(solution)/shard_map/ppermute | solution.py:590
  66.4 3.3 %collective-permute-done.10 = f32[96,96]{1,0:T(8,128)S(1)} collective-permute-done((f32[96,96]{1,0:T(8,128)S(1)}, f32[96,96]{1,0:T(8,128)S(1)}, u32[]{:S(2)}, u32[]{:S(2)}) %collective-permute-start.10) | collective-permute-done | bytes 36896 | tf_op jit(solution)/shard_map/ppermute | solution.py:590
  69.7 0.6 add_add_fusion
  (21 shorter events, 0.2 us)
Async XLA Ops:
  0.0 18.0 %copy-start.3 = (s32[16]{0:T(128)S(1)}, s32[16]{0:T(128)}, u32[]{:S(2)}) copy-start(s32[16]{0:T(128)} %source.3) | copy-start | bytes 196
  0.0 18.0 %copy-start.4 = (f32[16]{0:T(128)S(1)}, f32[16]{0:T(128)}, u32[]{:S(2)}) copy-start(f32[16]{0:T(128)} %frac.3) | copy-start | bytes 196
  0.0 5.3 %collective-permute-start = (f32[96,96]{1,0:T(8,128)}, f32[96,96]{1,0:T(8,128)S(1)}, u32[]{:S(2)}, u32[]{:S(2)}) collective-permute-start(f32[96,96]{1,0:T(8,128)} %bitcast.6), channel_id=1, source_target_pairs={{0,1},{1,0},{2,3},{3,2},{4,5},{5,4},{6,7},{7,6},{8,9},{9,8},{10,11... | collective-permute-start | bytes 110600 | tf_op jit(solution)/shard_map/ppermute | solution.py:490
  0.0 7.3 %collective-permute-start.1 = (f32[96,96]{1,0:T(8,128)}, f32[96,96]{1,0:T(8,128)S(1)}, u32[]{:S(2)}, u32[]{:S(2)}) collective-permute-start(f32[96,96]{1,0:T(8,128)} %bitcast.7), channel_id=1, source_target_pairs={{0,15},{1,2},{2,1},{3,4},{4,3},{5,6},{6,5},{7,8},{8,7},{9,10},{10,... | collective-permute-start | bytes 110600 | tf_op jit(solution)/shard_map/ppermute | solution.py:490
  11.3 15.9 %all-to-all-start = ((f32[8,32,384]{2,1,0:T(8,128)}), f32[8,32,384]{2,1,0:T(8,128)S(1)}, u32[]{:S(2)}, u32[]{:S(2)}) async-start(f32[8,32,384]{2,1,0:T(8,128)} %get-tuple-element.24), calls=%async_computation | async-start | bytes 786432 | tf_op jit(solution)/shard_map/all_to_all | solution.py:545
  21.3 10.0 %collective-permute-start.2 = (f32[64,1536]{1,0:T(8,128)}, f32[64,1536]{1,0:T(8,128)S(1)}, u32[]{:S(2)}, u32[]{:S(2)}) collective-permute-start(f32[64,1536]{1,0:T(8,128)} %get-tuple-element.22), channel_id=1, source_target_pairs={{0,1},{1,0},{2,3},{3,2},{4,5},{5,4},{6,7},{7,6},{8,9},{9,8},{10,11... | collective-permute-start | bytes 1179656 | tf_op jit(solution)/shard_map/ppermute | solution.py:519
  21.4 9.9 %collective-permute-start.3 = (f32[64,1536]{1,0:T(8,128)S(1)}, f32[64,1536]{1,0:T(8,128)S(1)}, u32[]{:S(2)}, u32[]{:S(2)}) collective-permute-start(f32[64,1536]{1,0:T(8,128)S(1)} %get-tuple-element.23), channel_id=1, source_target_pairs={{0,15},{1,2},{2,1},{3,4},{4,3},{5,6},{6,5},{7,8},{8,7},{9,10},{10,... | collective-permute-start | bytes 1179656 | tf_op jit(solution)/shard_map/ppermute | solution.py:518
  27.2 1.3 %collective-permute-start.4 = (f32[32,384]{1,0:T(8,128)S(1)}, f32[32,384]{1,0:T(8,128)S(1)}, u32[]{:S(2)}, u32[]{:S(2)}) collective-permute-start(f32[32,384]{1,0:T(8,128)S(1)} %total.1.mine.own), channel_id=1, source_target_pairs={{0,1},{1,0},{2,3},{3,2},{4,5},{5,4},{6,7},{7,6},{8,9},{9,8},{10,11... | collective-permute-start | bytes 147464 | tf_op jit(solution)/shard_map/ppermute | solution.py:547
  28.6 4.9 %collective-permute-start.5 = (f32[64,384]{1,0:T(8,128)S(1)}, f32[64,384]{1,0:T(8,128)S(1)}, u32[]{:S(2)}, u32[]{:S(2)}) collective-permute-start(f32[64,384]{1,0:T(8,128)S(1)} %join.1), channel_id=1, source_target_pairs={{0,2},{1,3},{2,0},{3,1},{4,6},{5,7},{6,4},{7,5},{8,10},{9,11},{10,... | collective-permute-start | bytes 294920 | tf_op jit(solution)/shard_map/ppermute | solution.py:550
  28.7 7.0 %collective-permute-start.6 = (f32[64,384]{1,0:T(8,128)S(1)}, f32[64,384]{1,0:T(8,128)S(1)}, u32[]{:S(2)}, u32[]{:S(2)}) collective-permute-start(f32[64,384]{1,0:T(8,128)S(1)} %join.1), channel_id=1, source_target_pairs={{0,14},{1,15},{2,4},{3,5},{4,2},{5,3},{6,8},{7,9},{8,6},{9,7},{10,... | collective-permute-start | bytes 294920 | tf_op jit(solution)/shard_map/ppermute | solution.py:549
  35.7 26.9 %copy-start = (f32[6,16,1,96]{3,2,1,0:T(1,128)S(1)}, f32[6,16,1,96]{3,2,1,0:T(1,128)}, u32[]{:S(2)}) copy-start(f32[6,16,1,96]{3,2,1,0:T(1,128)} %param.13) | copy-start | bytes 110596
  35.7 26.9 %copy-start.1 = (bf16[384,96]{1,0:T(8,128)(2,1)S(1)}, bf16[384,96]{1,0:T(8,128)(2,1)}, u32[]{:S(2)}) copy-start(bf16[384,96]{1,0:T(8,128)(2,1)} %constant.24.clone.lon_down) | copy-start | bytes 221188
  35.7 26.9 %copy-start.2 = (bf16[48,256]{1,0:T(8,128)(2,1)S(1)}, bf16[48,256]{1,0:T(8,128)(2,1)}, u32[]{:S(2)}) copy-start(bf16[48,256]{1,0:T(8,128)(2,1)} %constant.26.clone.mix_t) | copy-start | bytes 73732
  42.8 3.0 %collective-permute-start.7 = (f32[32,384]{1,0:T(8,128)S(1)}, f32[32,384]{1,0:T(8,128)S(1)}, u32[]{:S(2)}, u32[]{:S(2)}) collective-permute-start(f32[32,384]{1,0:T(8,128)S(1)} %get-tuple-element.32), channel_id=1, source_target_pairs={{0,1},{1,0},{2,3},{3,2},{4,5},{5,4},{6,7},{7,6},{8,9},{9,8},{10,11... | collective-permute-start | bytes 147464 | tf_op jit(solution)/shard_map/ppermute | solution.py:579
  42.9 5.7 %collective-permute-start.8 = (f32[32,384]{1,0:T(8,128)S(1)}, f32[32,384]{1,0:T(8,128)S(1)}, u32[]{:S(2)}, u32[]{:S(2)}) collective-permute-start(f32[32,384]{1,0:T(8,128)S(1)} %get-tuple-element.33), channel_id=1, source_target_pairs={{0,15},{1,2},{2,1},{3,4},{4,3},{5,6},{6,5},{7,8},{8,7},{9,10},{10,... | collective-permute-start | bytes 147464 | tf_op jit(solution)/shard_map/ppermute | solution.py:578
  64.0 5.7 %collective-permute-start.10 = (f32[96,96]{1,0:T(8,128)S(1)}, f32[96,96]{1,0:T(8,128)S(1)}, u32[]{:S(2)}, u32[]{:S(2)}) collective-permute-start(f32[96,96]{1,0:T(8,128)S(1)} %get-tuple-element.36), channel_id=1, source_target_pairs={{0,15},{1,2},{2,1},{3,4},{4,3},{5,6},{6,5},{7,8},{8,7},{9,10},{10,... | collective-permute-start | bytes 110600 | tf_op jit(solution)/shard_map/ppermute | solution.py:590
  66.4 3.3 %collective-permute-start.9 = (f32[96,96]{1,0:T(8,128)S(1)}, f32[96,96]{1,0:T(8,128)S(1)}, u32[]{:S(2)}, u32[]{:S(2)}) collective-permute-start(f32[96,96]{1,0:T(8,128)S(1)} %get-tuple-element.35), channel_id=1, source_target_pairs={{0,1},{1,0},{2,3},{3,2},{4,5},{5,4},{6,7},{7,6},{8,9},{9,8},{10,11... | collective-permute-start | bytes 110600 | tf_op jit(solution)/shard_map/ppermute | solution.py:591

commit v4 on v3

--- a/solution.py
+++ b/solution.py
@@ -35,21 +35,26 @@
     return hi, lo
 
 
+def position():
+    lat = lax.axis_index("lat")
+    return lat, lat % 2, lax.axis_size("lat") - 1
+
+
 def dot(a, b):
     return jnp.dot(a, b, preferred_element_type=F32)
 
 
 def prepare_kernel(
-    place, source, frac, weight, north_all, east_all, select_all, order_all,
+    source, frac, weight, north_all, east_all, select_all, order_all,
     coef, own_weight, buf_a, buf_b, level_weight, north, east, select, order, extra, sems,
 ):
-    odd = place[0] % 2
+    _, odd, _ = position()
     levels, rows, lon = level_weight.shape
     copies = [
         pltpu.make_async_copy(north_all, north, sems.at[0]),
         pltpu.make_async_copy(east_all, east, sems.at[1]),
         pltpu.make_async_copy(
-            weight.at[pl.ds(place[2] * levels, levels)], level_weight, sems.at[2]
+            weight.at[pl.ds(lax.axis_index("mem") * levels, levels)], level_weight, sems.at[2]
         ),
         pltpu.make_async_copy(order_all, order, sems.at[3]),
         pltpu.make_async_copy(select_all, select, sems.at[4]),
@@ -109,9 +114,8 @@
         fill(buf_b, True)
 
 
-def assemble_kernel(place, coef, own_weight, got_a, got_b, north, east, west, weight):
-    lat = place[0]
-    odd = lat % 2
+def assemble_kernel(coef, own_weight, got_a, got_b, north, east, west, weight):
+    lat, odd, _ = position()
     rows = own_weight.shape[0]
     quarter = coef.shape[1] // 4
 
@@ -148,24 +152,30 @@
         north[HALO - 1] = jnp.zeros(north.shape[1:], F32)
 
 
-def raise_kernel(
-    place, got_a, got_b, own_all, lon_all, mix_all, stored, out, pert, x, acc, raw, flat, own, lon_up,
-    mix, sems,
-):
-    lat, last = place[0], place[1] - 1
-    odd = lat % 2
+def arrange_kernel(own_all, lon_all, mix_all, stored, own, lon_up, mix, pert, raw, flat, sems):
     members, levels, band, _ = raw.shape
-    lev = own.shape[0] // members
     small = [
         pltpu.make_async_copy(own_all, own, sems.at[members]),
         pltpu.make_async_copy(lon_all, lon_up, sems.at[members + 1]),
         pltpu.make_async_copy(mix_all, mix, sems.at[members + 2]),
     ]
     copies = [pltpu.make_async_copy(stored.at[m], raw.at[m], sems.at[m]) for m in range(members)]
-    for copy in small + copies:
+    for copy in copies + small:
         copy.start()
+    for m in range(members):
+        copies[m].wait()
+        values = raw[m].astype(F32)
+        for k in range(levels):
+            flat[m, band * k : band * k + band, :] = values[k]
+        pert[m] = flat[m].astype(BF16)
     for copy in small:
         copy.wait()
+
+
+def raise_kernel(got_a, got_b, own, lon_up, mix, pert, out, x, acc):
+    lat, odd, last = position()
+    members = pert.shape[0]
+    lev = own.shape[0] // members
 
     def put(step, ref):
         for m in range(members):
@@ -201,15 +211,9 @@
     hi, lo = split2(x[...])
     wide = dot(hi, lon_up[...]) + dot(lo, lon_up[...])
     for m in range(members):
-        copies[m].wait()
-        values = raw[m].astype(F32)
-        for k in range(levels):
-            flat[band * k : band * k + band, :] = values[k]
-        spread = flat[...]
-        pert[m] = spread.astype(BF16)
         hi, lo = split2(wide[3 * lev * m : 3 * lev * (m + 1), :])
         field = dot(mix[...], jnp.concatenate([hi, lo], axis=0))
-        term = field * spread
+        term = field * pert[m].astype(F32)
         if m == 0:
             acc[...] = term
         elif m < members - 1:
@@ -238,18 +242,19 @@
 
 
 def fine_kernel(
-    place, source, frac, far_a, far_b, own, mate, near_pair, far_pair,
-    north, east, west, weight, keep, send_a, send_b, mid, v, acc, extra_a, extra_b, sems,
+    source_all, frac_all, far_a, far_b, own, mate, near_pair, far_pair,
+    north, east, west, weight, keep, send_a, send_b, mid, v, acc, extra_a, extra_b, source, frac, sems,
 ):
     at = 8 * PASSES + 2 * HALO
     copies = [
         pltpu.make_async_copy(far_a.at[at : at + 1, 0:128], extra_a, sems.at[0]),
         pltpu.make_async_copy(far_b.at[at : at + 1, 0:128], extra_b, sems.at[1]),
+        pltpu.make_async_copy(source_all, source, sems.at[2]),
+        pltpu.make_async_copy(frac_all, frac, sems.at[3]),
     ]
     for copy in copies:
         copy.start()
-    lat, last = place[0], place[1] - 1
-    odd = lat % 2
+    lat, odd, last = position()
     lon = own.shape[1]
     rows = source.shape[0]
     n = rows + 2 * HALO
@@ -282,10 +287,14 @@
             else:
                 gather(case % 2 == 0, near_pair, far_pair)
 
-    for copy in copies:
-        copy.wait()
+    copies[2].wait()
+    copies[3].wait()
     origin = (lat - 2) * band
-    for i in range(n):
+    inner = list(range(HALO, HALO + rows))
+    for i in inner + [i for i in range(n) if i not in inner]:
+        if i == 0:
+            copies[0].wait()
+            copies[1].wait()
         k = i - HALO
         if k < 0:
             k += rows
@@ -316,7 +325,7 @@
     def cut(r):
         return slice(r * lon, r * lon + lon)
 
-    def sweep(first, stop):
+    def sweep(first, stop, finish):
         def flux(i, here, there):
             return [north[i, :, cut(r)] * (there[r] - here[r]) for r in range(4)]
 
@@ -334,32 +343,23 @@
                 east[i, :, cut(r)] * ((here[r + 1] if r < 3 else right) - here[r]) for r in range(4)
             ]
             back = [west[i] * (here[0] - left)] + side[:3]
-            for r in range(4):
-                v[i, :, cut(r)] = here[r] + ((high[r] - low[r]) + (side[r] - back[r]))
+            new = [here[r] + ((high[r] - low[r]) + (side[r] - back[r])) for r in range(4)]
+            finish(i, new)
             low, here = high, there
 
-    def first_pass(_, carry):
-        sweep(1, n - 1)
-        return carry
-
-    lax.fori_loop(0, PASSES, first_pass, 0)
-
-    def scale(k, carry):
-        v[PASSES + k] = weight[k] * v[PASSES + k]
-        return carry
-
-    lax.fori_loop(0, rows + 2 * PASSES, scale, 0)
-
-    def second_pass(_, carry):
-        sweep(PASSES + 1, n - PASSES - 1)
-        return carry
-
-    lax.fori_loop(0, PASSES, second_pass, 0)
+    def store(i, new):
+        for r in range(4):
+            v[i, :, cut(r)] = new[r]
+
+    def store_weighted(i, new):
+        for r in range(4):
+            v[i, :, cut(r)] = weight[i - PASSES, :, cut(r)] * new[r]
 
     acc[...] = jnp.zeros(acc.shape, F32)
     base = (lat - 1) * band
-    for k in range(rows):
-        o = [v[HALO + k, :, cut(r)] for r in range(4)]
+
+    def spread(i, o):
+        k = i - HALO
         ahead = pltpu.roll(0.375 * o[0] + 0.125 * o[1], lon - 1, axis=1)
         behind = pltpu.roll(0.125 * o[2] + 0.375 * o[3], 1, axis=1)
         g = 0.625 * (o[0] + o[3]) + 0.875 * (o[1] + o[2]) + (ahead + behind)
@@ -367,6 +367,19 @@
         f = frac[k]
         acc[s] += (1.0 - f) * g
         acc[s + 1] += f * g
+
+    def first_pass(_, carry):
+        sweep(1, n - 1, store)
+        return carry
+
+    def second_pass(_, carry):
+        sweep(PASSES + 1, n - PASSES - 1, store)
+        return carry
+
+    lax.fori_loop(0, PASSES - 1, first_pass, 0)
+    sweep(PASSES, n - PASSES, store_weighted)
+    lax.fori_loop(0, PASSES - 1, second_pass, 0)
+    sweep(HALO, HALO + rows, spread)
     for k in range(band):
         keep[8 * k : 8 * k + 8, :] = acc[band + k]
 
@@ -398,9 +411,8 @@
             out[k, :, lanes] = value
 
 
-def lower_kernel(place, controls, pert, adjoint, mix_t, lon_down, own, send_a, send_b, wide):
-    lat, last = place[0], place[1] - 1
-    odd = lat % 2
+def lower_kernel(controls, pert, adjoint, mix_t, lon_down, own, send_a, send_b, wide):
+    lat, odd, last = position()
     members = pert.shape[0]
     lev = own.shape[0] // members
     field = adjoint[...].reshape(pert.shape[1], pert.shape[2])
@@ -456,9 +468,7 @@
 
 
 def body(controls, perturbations, precision_weight, north_coef, east_coef, fine_source, fine_frac):
-    lat = lax.axis_index("lat")
     count = lax.axis_size("lat")
-    mem = lax.axis_index("mem")
     ranks = lax.axis_size("mem")
     members, clev, _, clon = controls.shape
     lev, band, lon = perturbations.shape[1:]
@@ -470,7 +480,6 @@
     near_chips = [(i, i ^ 2) for i in range(count)]
     far_chips = [(i, (i + 2) % count if i & 2 else (i - 2) % count) for i in range(count)]
 
-    place = jnp.stack([lat, jnp.int32(count), mem]).astype(jnp.int32)
     lon_refine = refine_matrix(clon, True)
     lev_refine = refine_matrix(clev, False)
     mix = np.einsum("vl,rt->vrtl", lev_refine, PHASES).reshape(lev * band, 3 * clev)
@@ -499,7 +508,7 @@
             jax.ShapeDtypeStruct((spots, fine_lon), F32),
             jax.ShapeDtypeStruct((spots, fine_lon), F32),
         ],
-        in_specs=[smem()] * 3 + [anywhere()] * 5,
+        in_specs=[smem()] * 2 + [anywhere()] * 5,
         out_specs=[vmem()] * 4,
         scratch_shapes=[
             pltpu.VMEM((part, rows, fine_lon), BF16),
@@ -512,35 +521,35 @@
         ],
         compiler_params=pltpu.CompilerParams(vmem_limit_bytes=VMEM_LIMIT),
     )(
-        place, fine_source, fine_frac,
+        fine_source, fine_frac,
         *[in_hbm(x) for x in (precision_weight, north_coef, east_coef, pick, order)],
     )
     far_b = lax.ppermute(buf_b, "lat", across)
     far_a = lax.ppermute(buf_a, "lat", mates)
 
-    local_sum, pert = pl.pallas_call(
-        raise_kernel,
-        name="raise",
+    flat_shape = (members * clev, clon)
+    own_copy, lon_copy, mix_copy, pert = pl.pallas_call(
+        arrange_kernel,
+        name="arrange",
         out_shape=[
-            jax.ShapeDtypeStruct((ranks, part * band, lon), F32),
+            jax.ShapeDtypeStruct(flat_shape, F32),
+            jax.ShapeDtypeStruct(lon_up.shape, BF16),
+            jax.ShapeDtypeStruct(mix_up.shape, BF16),
             jax.ShapeDtypeStruct((members, lev * band, lon), BF16),
         ],
-        in_specs=[smem()] + [vmem()] * 2 + [anywhere()] * 4,
-        out_specs=[vmem()] * 2,
+        in_specs=[anywhere()] * 4,
+        out_specs=[vmem()] * 4,
         scratch_shapes=[
-            pltpu.VMEM((3 * members * clev, clon), F32),
-            pltpu.VMEM((lev * band, lon), F32),
             pltpu.VMEM((members, lev, band, lon), BF16),
-            pltpu.VMEM((lev * band, lon), F32),
-            pltpu.VMEM((members * clev, clon), F32),
-            pltpu.VMEM(lon_up.shape, BF16),
-            pltpu.VMEM(mix_up.shape, BF16),
+            pltpu.VMEM((members, lev * band, lon), F32),
             pltpu.SemaphoreType.DMA((members + 3,)),
         ],
         compiler_params=pltpu.CompilerParams(vmem_limit_bytes=VMEM_LIMIT),
-    )(
-        place, low_high[1], low_high[0],
-        *[in_hbm(x) for x in (own, lon_up, mix_up, perturbations)],
+    )(*[in_hbm(x) for x in (own, lon_up, mix_up, perturbations)])
+    local_sum = call(
+        raise_kernel, "raise", (ranks, part * band, lon),
+        [(3 * members * clev, clon), (lev * band, lon)],
+        [], [low_high[1], low_high[0], own_copy, lon_copy, mix_copy, pert],
     )
     parts = lax.all_to_all(local_sum, "mem", 0, 0, tiled=True)
     mine = call(total_kernel, "total", (band * part, lon), [(band * part * lon // 128, 128)], [], [parts])
@@ -553,14 +562,14 @@
     north, east, west, weight = call(
         assemble_kernel, "assemble",
         [(n, 8, fine_lon), (n, 8, fine_lon), (n, 8, lon), (rows + 2 * PASSES, 8, fine_lon)],
-        [], [place], [coef, own_weight, far_a, far_b],
+        [], [], [coef, own_weight, far_a, far_b],
     )
     piece = jax.ShapeDtypeStruct((band * part, lon), F32)
     keep, send_a, send_b = pl.pallas_call(
         fine_kernel,
         name="fine",
         out_shape=[piece] * 3,
-        in_specs=[smem()] * 3 + [anywhere()] * 2 + [vmem()] * 8,
+        in_specs=[anywhere()] * 4 + [vmem()] * 8,
         out_specs=[vmem()] * 3,
         scratch_shapes=[
             pltpu.VMEM((5 * band, 8, lon), F32),
@@ -568,11 +577,13 @@
             pltpu.VMEM((3 * band, 8, lon), F32),
             pltpu.SMEM((1, 128), F32),
             pltpu.SMEM((1, 128), F32),
-            pltpu.SemaphoreType.DMA((2,)),
+            pltpu.SMEM((rows,), jnp.int32),
+            pltpu.SMEM((rows,), F32),
+            pltpu.SemaphoreType.DMA((4,)),
         ],
         compiler_params=pltpu.CompilerParams(vmem_limit_bytes=VMEM_LIMIT),
     )(
-        place, fine_source, fine_frac, far_a, far_b, mine, mate, near_pair, far_pair,
+        fine_source, fine_frac, far_a, far_b, mine, mate, near_pair, far_pair,
         north, east, west, weight,
     )
     got_b = lax.ppermute(send_b, "lat", across)
@@ -585,7 +596,7 @@
     flat = (members * clev, clon)
     result, send_a, send_b = call(
         lower_kernel, "lower", [flat, flat, flat], [(3 * members * clev, lon)],
-        [place], [own, pert, adjoint, mix_down, lon_down],
+        [], [own, pert, adjoint, mix_down, lon_down],
     )
     got_b = lax.ppermute(send_b, "lat", across)
     got_a = lax.ppermute(send_a, "lat", mates)

time: 70.6 us -> 65.5 us (0.928)
  Pallas kernels: 16.8 us -> 13.2 us
  starting transfers between devices: 23.1 us -> 21.3 us
  waiting for transfers between devices: 15.6 us -> 16.6 us
    pallas_call x1, Pallas kernels: 4.03 us -> 1.55 us  [body(): pl.pallas_call(arrange_kernel, name='arrange', out_shape=[jax.ShapeDtypeS...]
    ppermute x1, waiting for transfers between devices: 2.2 us -> 4.46 us  [body(): far_pair = lax.ppermute(pair, 'lat', far_chips)]
    pallas_call x1, Pallas kernels: 7.11 us -> 5.56 us  [body(): pl.pallas_call(fine_kernel, name='fine', out_shape=[piece] * 3, in_specs=...]
    ppermute x1, waiting for transfers between devices: 1.99 us -> 0.51 us  [body(): lax.ppermute(own, 'lat', across)]
    ppermute x1, waiting for transfers between devices: 1.26 us -> 0.01 us  [body(): near_pair = lax.ppermute(pair, 'lat', near_chips)]
    all_to_all x1, waiting for transfers between devices: 2.86 us -> 3.69 us  [body(): parts = lax.all_to_all(local_sum, 'mem', 0, 0, tiled=True)]
    pallas_call x5 -> x6, Pallas kernels: 2.38 us -> 2.81 us  [call(): pl.pallas_call(kernel, name=name, out_shape=shapes if many else shapes[0]...]
  transfers between devices with their start and end apart: 12 -> 12, of which waited for: 7 -> 6; matrix products, arithmetic and copies ran while one was open for 0% -> 0% of each run, Pallas kernels for 6% -> 8%
where the time goes in v4:
time: 65.5 us; the launch traced here: 65.2 us
  starting transfers between devices  21.3 us (33%)
  waiting for transfers between devices  16.6 us (25%)
  blocking collectives  13.4 us (20%)
  Pallas kernels  13.2 us (20%)
    all_to_all x1, blocking collectives, body(): adjoint = lax.all_to_all(copies, 'mem', 0, 0, tiled=True)  13.4 us
    ppermute x2, waiting for transfers between devices, body(): got_b = lax.ppermute(send_b, 'lat', across)  6.71 us
    all_to_all x1, starting transfers between devices, body(): parts = lax.all_to_all(local_sum, 'mem', 0, 0, tiled=True)  6.64 us
    pallas_call x1, Pallas kernels, body(): pl.pallas_call(fine_kernel, name='fine', out_shape=[piece] * 3, in_specs=...  5.56 us
    ppermute x2, starting transfers between devices, body(): got_b = lax.ppermute(send_b, 'lat', across)  4.7 us
    ppermute x1, starting transfers between devices, body(): lax.ppermute(own, 'lat', across)  4.52 us
    ppermute x1, waiting for transfers between devices, body(): far_pair = lax.ppermute(pair, 'lat', far_chips)  4.46 us
    all_to_all x1, waiting for transfers between devices, body(): parts = lax.all_to_all(local_sum, 'mem', 0, 0, tiled=True)  3.69 us
  transfers between devices with their start and end apart: 12, of which 6 were waited for; matrix products, arithmetic and copies ran while one was open for 0% of the time, Pallas kernels for 8%

profile of v4, /device:TPU:0, one launch (start us, length us, event | category | flops | bytes accessed | tf_op | source)
XLA Modules:
  0.0 65.2 jit_solution(6687683149228050252)
XLA Ops:
  0.0 4.5 %collective-permute-start.3 = (f32[96,96]{1,0:T(8,128)}, f32[96,96]{1,0:T(8,128)S(1)}, u32[]{:S(2)}, u32[]{:S(2)}) collective-permute-start(f32[96,96]{1,0:T(8,128)} %bitcast.4), channel_id=1, source_target_pairs={{0,15},{1,2},{2,1},{3,4},{4,3},{5,6},{6,5},{7,8},{8,7},{9,10},{10,... | collective-permute-start | bytes 110600 | tf_op jit(solution)/shard_map/ppermute | solution.py:499
  4.5 1.5 %arrange.1 = (f32[96,96]{1,0:T(8,128)S(1)}, bf16[96,384]{1,0:T(8,128)(2,1)S(1)}, bf16[256,96]{1,0:T(8,128)(2,1)S(1)}, bf16[6,256,384]{2,1,0:T(8,128)(2,1)S(1)}) custom-call(f32[96,96]{1,0:T(8,128)} %bitcast.6, bf16[96,384]{1,0:T(8,128)(2,1)} %constant.12.clone.lon_all, bf16[256,96]{1,0:T(8,128)(2,1)} %constant.14.clone.mix_all, bf16[6,64,4,384]{3,2,1,0:T(4,128)(2,1)} %stored.1), custom_call_target="tpu_custom_call" | custom-call | tf_op jit(solution)/shard_map/arrange/pallas_call | solution.py:531
  6.1 0.5 collective-permute-done.3.got_b
  6.6 1.5 %raise.1 = f32[8,32,384]{2,1,0:T(8,128)} custom-call(f32[96,96]{1,0:T(8,128)S(1)} %collective-permute-done.2.got_a, f32[96,96]{1,0:T(8,128)S(1)} %collective-permute-done.3.got_b, f32[96,96]{1,0:T(8,128)S(1)} %get-tuple-element.26.own, bf16[96,384]{1,0:T(8,128)(2,1)S(1)} %get-tuple-element.27.lon_up, bf16[256,96]{1,0:T(8,128)(2,1)S(1)} %get-tuple-element.28.mix, ...), custom_call_target="tpu_custom_call" | custom-call | tf_op jit(solution)/shard_map/raise/pallas_call | solution.py:459
  8.1 6.6 %all-to-all-start = ((f32[8,32,384]{2,1,0:T(8,128)}), f32[8,32,384]{2,1,0:T(8,128)S(1)}, u32[]{:S(2)}, u32[]{:S(2)}) async-start(f32[8,32,384]{2,1,0:T(8,128)} %raise.1), calls=%async_computation | async-start | bytes 786432 | tf_op jit(solution)/shard_map/all_to_all | solution.py:554
  14.7 3.3 %prepare.1 = (f32[32,1536]{1,0:T(8,128)S(1)}, bf16[16,8,1536]{2,1,0:T(8,128)(2,1)S(1)}, f32[64,1536]{1,0:T(8,128)}, f32[64,1536]{1,0:T(8,128)S(1)}) custom-call(s32[16]{0:T(128)S(1)} %copy-done.3, f32[16]{0:T(128)S(1)} %copy-done.4, bf16[64,16,1536]{2,1,0:T(8,128)(2,1)} %weight.1, f32[16,1536]{1,0:T(8,128)} %north_all.1, f32[16,1536]{1,0:T(8,128)} %east_all.1, ...), custom_call_target="tpu_custom_call" | custom-call | tf_op jit(solution)/shard_map/prepare/pallas_call | solution.py:502
  18.0 0.1 collective-permute-start
  18.1 3.0 %collective-permute-start.1 = (f32[64,1536]{1,0:T(8,128)S(1)}, f32[64,1536]{1,0:T(8,128)S(1)}, u32[]{:S(2)}, u32[]{:S(2)}) collective-permute-start(f32[64,1536]{1,0:T(8,128)S(1)} %get-tuple-element.25), channel_id=1, source_target_pairs={{0,15},{1,2},{2,1},{3,4},{4,3},{5,6},{6,5},{7,8},{8,7},{9,10},{10,... | collective-permute-start | bytes 1179656 | tf_op jit(solution)/shard_map/ppermute | solution.py:527
  21.1 3.7 %all-to-all-done.parts = f32[8,32,384]{2,1,0:T(8,128)S(1)} async-done(((f32[8,32,384]{2,1,0:T(8,128)}), f32[8,32,384]{2,1,0:T(8,128)S(1)}, u32[]{:S(2)}, u32[]{:S(2)}) %all-to-all-start) | async-done | bytes 393248 | tf_op jit(solution)/shard_map/all_to_all | solution.py:554
  24.8 0.1 collective-permute-start.4
  24.9 1.2 %collective-permute-done.4.mate = f32[32,384]{1,0:T(8,128)S(1)} collective-permute-done((f32[32,384]{1,0:T(8,128)S(1)}, f32[32,384]{1,0:T(8,128)S(1)}, u32[]{:S(2)}, u32[]{:S(2)}) %collective-permute-start.4) | collective-permute-done | bytes 49184 | tf_op jit(solution)/shard_map/ppermute | solution.py:556
  26.2 2.1 %collective-permute-start.6 = (f32[64,384]{1,0:T(8,128)S(1)}, f32[64,384]{1,0:T(8,128)S(1)}, u32[]{:S(2)}, u32[]{:S(2)}) collective-permute-start(f32[64,384]{1,0:T(8,128)S(1)} %join.1), channel_id=1, source_target_pairs={{0,14},{1,15},{2,4},{3,5},{4,2},{5,3},{6,8},{7,9},{8,6},{9,7},{10,... | collective-permute-start | bytes 294920 | tf_op jit(solution)/shard_map/ppermute | solution.py:558
  28.3 0.4 assemble.1
  28.7 4.5 %collective-permute-done.6.far_pair = f32[64,384]{1,0:T(8,128)S(1)} collective-permute-done((f32[64,384]{1,0:T(8,128)S(1)}, f32[64,384]{1,0:T(8,128)S(1)}, u32[]{:S(2)}, u32[]{:S(2)}) %collective-permute-start.6) | collective-permute-done | bytes 98336 | tf_op jit(solution)/shard_map/ppermute | solution.py:558
  33.2 5.6 %fine.1 = (f32[32,384]{1,0:T(8,128)S(1)}, f32[32,384]{1,0:T(8,128)S(1)}, f32[32,384]{1,0:T(8,128)S(1)}) custom-call(s32[16]{0:T(128)S(1)} %copy-done.3, f32[16]{0:T(128)S(1)} %copy-done.4, f32[64,1536]{1,0:T(8,128)S(1)} %collective-permute-done.got_a.far_a, f32[64,1536]{1,0:T(8,128)S(1)} %collective-permute-done.1.got_b.far_b, f32[32,384]{1,0:T(8,128)S(1)} %total.1.mine.own, ...), custom_call_target="tpu_custom_call" | custom-call | tf_op jit(solution)/shard_map/fine/pallas_call | solution.py:568
  38.7 0.1 collective-permute-start.7
  38.8 2.4 %collective-permute-start.8 = (f32[32,384]{1,0:T(8,128)S(1)}, f32[32,384]{1,0:T(8,128)S(1)}, u32[]{:S(2)}, u32[]{:S(2)}) collective-permute-start(f32[32,384]{1,0:T(8,128)S(1)} %get-tuple-element.37), channel_id=1, source_target_pairs={{0,15},{1,2},{2,1},{3,4},{4,3},{5,6},{6,5},{7,8},{8,7},{9,10},{10,... | collective-permute-start | bytes 147464 | tf_op jit(solution)/shard_map/ppermute | solution.py:589
  41.3 3.3 %collective-permute-done.8.got_b = f32[32,384]{1,0:T(8,128)S(1)} collective-permute-done((f32[32,384]{1,0:T(8,128)S(1)}, f32[32,384]{1,0:T(8,128)S(1)}, u32[]{:S(2)}, u32[]{:S(2)}) %collective-permute-start.8) | collective-permute-done | bytes 49184 | tf_op jit(solution)/shard_map/ppermute | solution.py:589
  44.6 13.4 %all_to_all.10.adjoint = f32[8,32,384]{2,1,0:T(8,128)S(1)} all-to-all(f32[8,32,384]{2,1,0:T(8,128)S(1)} %copies.1), channel_id=1, replica_groups=mesh['mem'=8,'lat'=16] {'mem'}, dimensions={0} | all-to-all | bytes 786432 | tf_op jit(solution)/shard_map/all_to_all | solution.py:595
  58.0 0.8 %lower.1 = (f32[96,96]{1,0:T(8,128)S(1)}, f32[96,96]{1,0:T(8,128)S(1)}, f32[96,96]{1,0:T(8,128)S(1)}) custom-call(f32[96,96]{1,0:T(8,128)S(1)} %bitcast.7, bf16[6,256,384]{2,1,0:T(8,128)(2,1)S(1)} %get-tuple-element.23.pert, f32[8,32,384]{2,1,0:T(8,128)S(1)} %all_to_all.10.adjoint, bf16[48,256]{1,0:T(8,128)(2,1)S(1)} %copy-done.2, bf16[384,96]{1,0:T(8,128)(2,1)S(1)} %copy-done.1), custom_call_target="tpu_custom_call" | custom-call | tf_op jit(solution)/shard_map/lower/pallas_call | solution.py:459
  58.8 0.1 collective-permute-start.9
  58.9 2.3 %collective-permute-start.10 = (f32[96,96]{1,0:T(8,128)S(1)}, f32[96,96]{1,0:T(8,128)S(1)}, u32[]{:S(2)}, u32[]{:S(2)}) collective-permute-start(f32[96,96]{1,0:T(8,128)S(1)} %get-tuple-element.40), channel_id=1, source_target_pairs={{0,15},{1,2},{2,1},{3,4},{4,3},{5,6},{6,5},{7,8},{8,7},{9,10},{10,... | collective-permute-start | bytes 110600 | tf_op jit(solution)/shard_map/ppermute | solution.py:601
  61.2 3.4 %collective-permute-done.10 = f32[96,96]{1,0:T(8,128)S(1)} collective-permute-done((f32[96,96]{1,0:T(8,128)S(1)}, f32[96,96]{1,0:T(8,128)S(1)}, u32[]{:S(2)}, u32[]{:S(2)}) %collective-permute-start.10) | collective-permute-done | bytes 36896 | tf_op jit(solution)/shard_map/ppermute | solution.py:601
  64.6 0.6 add_add_fusion
  (21 shorter events, 0.1 us)
Async XLA Ops:
  0.0 14.7 %copy-start.3 = (s32[16]{0:T(128)S(1)}, s32[16]{0:T(128)}, u32[]{:S(2)}) copy-start(s32[16]{0:T(128)} %source_all.1) | copy-start | bytes 196
  0.0 14.7 %copy-start.4 = (f32[16]{0:T(128)S(1)}, f32[16]{0:T(128)}, u32[]{:S(2)}) copy-start(f32[16]{0:T(128)} %frac_all.1) | copy-start | bytes 196
  0.0 6.6 %collective-permute-start.3 = (f32[96,96]{1,0:T(8,128)}, f32[96,96]{1,0:T(8,128)S(1)}, u32[]{:S(2)}, u32[]{:S(2)}) collective-permute-start(f32[96,96]{1,0:T(8,128)} %bitcast.4), channel_id=1, source_target_pairs={{0,15},{1,2},{2,1},{3,4},{4,3},{5,6},{6,5},{7,8},{8,7},{9,10},{10,... | collective-permute-start | bytes 110600 | tf_op jit(solution)/shard_map/ppermute | solution.py:499
  4.5 2.1 %collective-permute-start.2 = (f32[96,96]{1,0:T(8,128)}, f32[96,96]{1,0:T(8,128)S(1)}, u32[]{:S(2)}, u32[]{:S(2)}) collective-permute-start(f32[96,96]{1,0:T(8,128)} %bitcast.5), channel_id=1, source_target_pairs={{0,1},{1,0},{2,3},{3,2},{4,5},{5,4},{6,7},{7,6},{8,9},{9,8},{10,11... | collective-permute-start | bytes 110600 | tf_op jit(solution)/shard_map/ppermute | solution.py:499
  8.1 16.7 %all-to-all-start = ((f32[8,32,384]{2,1,0:T(8,128)}), f32[8,32,384]{2,1,0:T(8,128)S(1)}, u32[]{:S(2)}, u32[]{:S(2)}) async-start(f32[8,32,384]{2,1,0:T(8,128)} %raise.1), calls=%async_computation | async-start | bytes 786432 | tf_op jit(solution)/shard_map/all_to_all | solution.py:554
  18.0 10.2 %collective-permute-start = (f32[64,1536]{1,0:T(8,128)}, f32[64,1536]{1,0:T(8,128)S(1)}, u32[]{:S(2)}, u32[]{:S(2)}) collective-permute-start(f32[64,1536]{1,0:T(8,128)} %get-tuple-element.24), channel_id=1, source_target_pairs={{0,1},{1,0},{2,3},{3,2},{4,5},{5,4},{6,7},{7,6},{8,9},{9,8},{10,11... | collective-permute-start | bytes 1179656 | tf_op jit(solution)/shard_map/ppermute | solution.py:528
  18.1 10.1 %collective-permute-start.1 = (f32[64,1536]{1,0:T(8,128)S(1)}, f32[64,1536]{1,0:T(8,128)S(1)}, u32[]{:S(2)}, u32[]{:S(2)}) collective-permute-start(f32[64,1536]{1,0:T(8,128)S(1)} %get-tuple-element.25), channel_id=1, source_target_pairs={{0,15},{1,2},{2,1},{3,4},{4,3},{5,6},{6,5},{7,8},{8,7},{9,10},{10,... | collective-permute-start | bytes 1179656 | tf_op jit(solution)/shard_map/ppermute | solution.py:527
  24.8 1.3 %collective-permute-start.4 = (f32[32,384]{1,0:T(8,128)S(1)}, f32[32,384]{1,0:T(8,128)S(1)}, u32[]{:S(2)}, u32[]{:S(2)}) collective-permute-start(f32[32,384]{1,0:T(8,128)S(1)} %total.1.mine.own), channel_id=1, source_target_pairs={{0,1},{1,0},{2,3},{3,2},{4,5},{5,4},{6,7},{7,6},{8,9},{9,8},{10,11... | collective-permute-start | bytes 147464 | tf_op jit(solution)/shard_map/ppermute | solution.py:556
  26.2 7.0 %collective-permute-start.6 = (f32[64,384]{1,0:T(8,128)S(1)}, f32[64,384]{1,0:T(8,128)S(1)}, u32[]{:S(2)}, u32[]{:S(2)}) collective-permute-start(f32[64,384]{1,0:T(8,128)S(1)} %join.1), channel_id=1, source_target_pairs={{0,14},{1,15},{2,4},{3,5},{4,2},{5,3},{6,8},{7,9},{8,6},{9,7},{10,... | collective-permute-start | bytes 294920 | tf_op jit(solution)/shard_map/ppermute | solution.py:558
  28.3 4.9 %collective-permute-start.5 = (f32[64,384]{1,0:T(8,128)S(1)}, f32[64,384]{1,0:T(8,128)S(1)}, u32[]{:S(2)}, u32[]{:S(2)}) collective-permute-start(f32[64,384]{1,0:T(8,128)S(1)} %join.1), channel_id=1, source_target_pairs={{0,2},{1,3},{2,0},{3,1},{4,6},{5,7},{6,4},{7,5},{8,10},{9,11},{10,... | collective-permute-start | bytes 294920 | tf_op jit(solution)/shard_map/ppermute | solution.py:559
  33.2 24.8 %copy-start = (f32[6,16,1,96]{3,2,1,0:T(1,128)S(1)}, f32[6,16,1,96]{3,2,1,0:T(1,128)}, u32[]{:S(2)}) copy-start(f32[6,16,1,96]{3,2,1,0:T(1,128)} %param.13) | copy-start | bytes 110596
  33.2 24.8 %copy-start.1 = (bf16[384,96]{1,0:T(8,128)(2,1)S(1)}, bf16[384,96]{1,0:T(8,128)(2,1)}, u32[]{:S(2)}) copy-start(bf16[384,96]{1,0:T(8,128)(2,1)} %constant.13.clone.lon_down) | copy-start | bytes 221188
  33.2 24.8 %copy-start.2 = (bf16[48,256]{1,0:T(8,128)(2,1)S(1)}, bf16[48,256]{1,0:T(8,128)(2,1)}, u32[]{:S(2)}) copy-start(bf16[48,256]{1,0:T(8,128)(2,1)} %constant.15.clone.mix_t) | copy-start | bytes 73732
  38.7 2.5 %collective-permute-start.7 = (f32[32,384]{1,0:T(8,128)S(1)}, f32[32,384]{1,0:T(8,128)S(1)}, u32[]{:S(2)}, u32[]{:S(2)}) collective-permute-start(f32[32,384]{1,0:T(8,128)S(1)} %get-tuple-element.36), channel_id=1, source_target_pairs={{0,1},{1,0},{2,3},{3,2},{4,5},{5,4},{6,7},{7,6},{8,9},{9,8},{10,11... | collective-permute-start | bytes 147464 | tf_op jit(solution)/shard_map/ppermute | solution.py:590
  38.8 5.7 %collective-permute-start.8 = (f32[32,384]{1,0:T(8,128)S(1)}, f32[32,384]{1,0:T(8,128)S(1)}, u32[]{:S(2)}, u32[]{:S(2)}) collective-permute-start(f32[32,384]{1,0:T(8,128)S(1)} %get-tuple-element.37), channel_id=1, source_target_pairs={{0,15},{1,2},{2,1},{3,4},{4,3},{5,6},{6,5},{7,8},{8,7},{9,10},{10,... | collective-permute-start | bytes 147464 | tf_op jit(solution)/shard_map/ppermute | solution.py:589
  58.8 2.4 %collective-permute-start.9 = (f32[96,96]{1,0:T(8,128)S(1)}, f32[96,96]{1,0:T(8,128)S(1)}, u32[]{:S(2)}, u32[]{:S(2)}) collective-permute-start(f32[96,96]{1,0:T(8,128)S(1)} %get-tuple-element.39), channel_id=1, source_target_pairs={{0,1},{1,0},{2,3},{3,2},{4,5},{5,4},{6,7},{7,6},{8,9},{9,8},{10,11... | collective-permute-start | bytes 110600 | tf_op jit(solution)/shard_map/ppermute | solution.py:602
  58.9 5.7 %collective-permute-start.10 = (f32[96,96]{1,0:T(8,128)S(1)}, f32[96,96]{1,0:T(8,128)S(1)}, u32[]{:S(2)}, u32[]{:S(2)}) collective-permute-start(f32[96,96]{1,0:T(8,128)S(1)} %get-tuple-element.40), channel_id=1, source_target_pairs={{0,15},{1,2},{2,1},{3,4},{4,3},{5,6},{6,5},{7,8},{8,7},{9,10},{10,... | collective-permute-start | bytes 110600 | tf_op jit(solution)/shard_map/ppermute | solution.py:601

commit v5 on v4

--- a/solution.py
+++ b/solution.py
@@ -45,22 +45,11 @@
 
 
 def prepare_kernel(
-    source, frac, weight, north_all, east_all, select_all, order_all,
-    coef, own_weight, buf_a, buf_b, level_weight, north, east, select, order, extra, sems,
+    source, frac, level_weight, north, east, select, order,
+    coef, own_weight, buf_a, buf_b, extra,
 ):
     _, odd, _ = position()
     levels, rows, lon = level_weight.shape
-    copies = [
-        pltpu.make_async_copy(north_all, north, sems.at[0]),
-        pltpu.make_async_copy(east_all, east, sems.at[1]),
-        pltpu.make_async_copy(
-            weight.at[pl.ds(lax.axis_index("mem") * levels, levels)], level_weight, sems.at[2]
-        ),
-        pltpu.make_async_copy(order_all, order, sems.at[3]),
-        pltpu.make_async_copy(select_all, select, sems.at[4]),
-    ]
-    for copy in copies:
-        copy.start()
     lane = lax.broadcasted_iota(jnp.int32, (4, 128), 1)
     tail = jnp.zeros((4, 128), F32)
     for k in range(rows):
@@ -68,18 +57,13 @@
         tail = jnp.where(lane == rows + k, source[k].astype(F32), tail)
     extra[...] = jnp.zeros(extra.shape, F32)
     extra[:, 0:128] = tail
-    copies[0].wait()
-    copies[1].wait()
     stacked = jnp.concatenate([north[...], east[...]], axis=0)
     hi = stacked.astype(BF16)
     rest = stacked - hi.astype(F32)
     mid = rest.astype(BF16)
     low = (rest - mid.astype(F32)).astype(BF16)
-    copies[2].wait()
-    copies[3].wait()
     values = dot(order[...], level_weight[...].reshape(levels * rows, lon)).astype(BF16)
     everything = jnp.concatenate([values, hi, mid, low], axis=0)
-    copies[4].wait()
     many = levels * rows
     quarter = lon // 4
     for c in range(lon // 512):
@@ -152,7 +136,10 @@
         north[HALO - 1] = jnp.zeros(north.shape[1:], F32)
 
 
-def arrange_kernel(own_all, lon_all, mix_all, stored, own, lon_up, mix, pert, raw, flat, sems):
+def arrange_kernel(
+    own_all, lon_all, mix_all, stored, weight_all, north_all, east_all, select_all, order_all,
+    own, lon_up, mix, pert, weight, north, east, select, order, raw, flat, sems,
+):
     members, levels, band, _ = raw.shape
     small = [
         pltpu.make_async_copy(own_all, own, sems.at[members]),
@@ -160,6 +147,14 @@
         pltpu.make_async_copy(mix_all, mix, sems.at[members + 2]),
     ]
     copies = [pltpu.make_async_copy(stored.at[m], raw.at[m], sems.at[m]) for m in range(members)]
+    levels_here = weight_all.at[pl.ds(lax.axis_index("mem") * weight.shape[0], weight.shape[0])]
+    small += [
+        pltpu.make_async_copy(levels_here, weight, sems.at[members + 3]),
+        pltpu.make_async_copy(north_all, north, sems.at[members + 4]),
+        pltpu.make_async_copy(east_all, east, sems.at[members + 5]),
+        pltpu.make_async_copy(select_all, select, sems.at[members + 6]),
+        pltpu.make_async_copy(order_all, order, sems.at[members + 7]),
+    ]
     for copy in copies + small:
         copy.start()
     for m in range(members):
@@ -498,6 +493,34 @@
     own = controls.reshape(members * clev, clon)
     low_high = [lax.ppermute(own, "lat", across), lax.ppermute(own, "lat", mates)]
 
+    flat_shape = (members * clev, clon)
+    own_copy, lon_copy, mix_copy, pert, *fetched = pl.pallas_call(
+        arrange_kernel,
+        name="arrange",
+        out_shape=[
+            jax.ShapeDtypeStruct(flat_shape, F32),
+            jax.ShapeDtypeStruct(lon_up.shape, BF16),
+            jax.ShapeDtypeStruct(mix_up.shape, BF16),
+            jax.ShapeDtypeStruct((members, lev * band, lon), BF16),
+            jax.ShapeDtypeStruct((part, rows, fine_lon), BF16),
+            jax.ShapeDtypeStruct((rows, fine_lon), F32),
+            jax.ShapeDtypeStruct((rows, fine_lon), F32),
+            jax.ShapeDtypeStruct(pick.shape, BF16),
+            jax.ShapeDtypeStruct(order.shape, BF16),
+        ],
+        in_specs=[anywhere()] * 9,
+        out_specs=[vmem()] * 9,
+        scratch_shapes=[
+            pltpu.VMEM((members, lev, band, lon), BF16),
+            pltpu.VMEM((members, lev * band, lon), F32),
+            pltpu.SemaphoreType.DMA((members + 8,)),
+        ],
+        compiler_params=pltpu.CompilerParams(vmem_limit_bytes=VMEM_LIMIT),
+    )(
+        *[in_hbm(x) for x in (own, lon_up, mix_up, perturbations)],
+        *[in_hbm(x) for x in (precision_weight, north_coef, east_coef, pick, order)],
+    )
+
     spots = 8 * PASSES + 2 * HALO + 4
     coef, own_weight, buf_a, buf_b = pl.pallas_call(
         prepare_kernel,
@@ -508,44 +531,16 @@
             jax.ShapeDtypeStruct((spots, fine_lon), F32),
             jax.ShapeDtypeStruct((spots, fine_lon), F32),
         ],
-        in_specs=[smem()] * 2 + [anywhere()] * 5,
+        in_specs=[smem()] * 2 + [vmem()] * 5,
         out_specs=[vmem()] * 4,
-        scratch_shapes=[
-            pltpu.VMEM((part, rows, fine_lon), BF16),
-            pltpu.VMEM((rows, fine_lon), F32),
-            pltpu.VMEM((rows, fine_lon), F32),
-            pltpu.VMEM((512, 512), BF16),
-            pltpu.VMEM((part * rows, part * rows), BF16),
-            pltpu.VMEM((4, fine_lon), F32),
-            pltpu.SemaphoreType.DMA((5,)),
-        ],
+        scratch_shapes=[pltpu.VMEM((4, fine_lon), F32)],
         compiler_params=pltpu.CompilerParams(vmem_limit_bytes=VMEM_LIMIT),
     )(
-        fine_source, fine_frac,
-        *[in_hbm(x) for x in (precision_weight, north_coef, east_coef, pick, order)],
+        fine_source, fine_frac, *fetched,
     )
     far_b = lax.ppermute(buf_b, "lat", across)
     far_a = lax.ppermute(buf_a, "lat", mates)
 
-    flat_shape = (members * clev, clon)
-    own_copy, lon_copy, mix_copy, pert = pl.pallas_call(
-        arrange_kernel,
-        name="arrange",
-        out_shape=[
-            jax.ShapeDtypeStruct(flat_shape, F32),
-            jax.ShapeDtypeStruct(lon_up.shape, BF16),
-            jax.ShapeDtypeStruct(mix_up.shape, BF16),
-            jax.ShapeDtypeStruct((members, lev * band, lon), BF16),
-        ],
-        in_specs=[anywhere()] * 4,
-        out_specs=[vmem()] * 4,
-        scratch_shapes=[
-            pltpu.VMEM((members, lev, band, lon), BF16),
-            pltpu.VMEM((members, lev * band, lon), F32),
-            pltpu.SemaphoreType.DMA((members + 3,)),
-        ],
-        compiler_params=pltpu.CompilerParams(vmem_limit_bytes=VMEM_LIMIT),
-    )(*[in_hbm(x) for x in (own, lon_up, mix_up, perturbations)])
     local_sum = call(
         raise_kernel, "raise", (ranks, part * band, lon),
         [(3 * members * clev, clon), (lev * band, lon)],

time: 65.5 us -> 64.6 us (0.986)
  starting transfers between devices: 21.3 us -> 23 us
  waiting for transfers between devices: 16.6 us -> 15.5 us
  blocking collectives: 13.4 us -> 12.6 us
  Pallas kernels: 13.2 us -> 12.4 us
    ppermute x1, waiting for transfers between devices: 4.46 us -> 2.2 us  [body(): far_pair = lax.ppermute(pair, 'lat', far_chips)]
    ppermute x1, waiting for transfers between devices: 0.01 us -> 1.81 us  [body(): near_pair = lax.ppermute(pair, 'lat', near_chips)]
    pallas_call x1, Pallas kernels: 3.3 us -> 2.13 us  [body(): pl.pallas_call(prepare_kernel, name='prepare', out_shape=[jax.ShapeDtypeS...]
    ppermute x2, waiting for transfers between devices: 6.71 us -> 5.91 us  [body(): got_b = lax.ppermute(send_b, 'lat', across)]
    ppermute x2, starting transfers between devices: 4.7 us -> 5.5 us  [body(): got_b = lax.ppermute(send_b, 'lat', across)]
    all_to_all x1, blocking collectives: 13.4 us -> 12.6 us  [body(): adjoint = lax.all_to_all(copies, 'mem', 0, 0, tiled=True)]
    ppermute x1, starting transfers between devices: 4.52 us -> 5.19 us  [body(): lax.ppermute(own, 'lat', across)]
  transfers between devices with their start and end apart: 12 -> 12, of which waited for: 6 -> 7; matrix products, arithmetic and copies ran while one was open for 0% -> 0% of each run, Pallas kernels for 8% -> 7%
where the time goes in v5:
time: 64.6 us; the launch traced here: 64.3 us
  starting transfers between devices  23 us (36%)
  waiting for transfers between devices  15.5 us (24%)
  blocking collectives  12.6 us (20%)
  Pallas kernels  12.4 us (19%)
    all_to_all x1, blocking collectives, body(): adjoint = lax.all_to_all(copies, 'mem', 0, 0, tiled=True)  12.6 us
    all_to_all x1, starting transfers between devices, body(): parts = lax.all_to_all(local_sum, 'mem', 0, 0, tiled=True)  6.64 us
    ppermute x2, waiting for transfers between devices, body(): got_b = lax.ppermute(send_b, 'lat', across)  5.91 us
    pallas_call x1, Pallas kernels, body(): pl.pallas_call(fine_kernel, name='fine', out_shape=[piece] * 3, in_specs=...  5.56 us
    ppermute x2, starting transfers between devices, body(): got_b = lax.ppermute(send_b, 'lat', across)  5.5 us
    ppermute x1, starting transfers between devices, body(): lax.ppermute(own, 'lat', across)  5.19 us
    all_to_all x1, waiting for transfers between devices, body(): parts = lax.all_to_all(local_sum, 'mem', 0, 0, tiled=True)  4.21 us
    ppermute x1, starting transfers between devices, body(): far_b = lax.ppermute(buf_b, 'lat', across)  2.89 us
  transfers between devices with their start and end apart: 12, of which 7 were waited for; matrix products, arithmetic and copies ran while one was open for 0% of the time, Pallas kernels for 7%

profile of v5, /device:TPU:0, one launch (start us, length us, event | category | flops | bytes accessed | tf_op | source)
XLA Modules:
  0.0 64.3 jit_solution(10814428517841821592)
XLA Ops:
  0.0 5.2 %collective-permute-start.3 = (f32[96,96]{1,0:T(8,128)}, f32[96,96]{1,0:T(8,128)S(1)}, u32[]{:S(2)}, u32[]{:S(2)}) collective-permute-start(f32[96,96]{1,0:T(8,128)} %bitcast.5), channel_id=1, source_target_pairs={{0,15},{1,2},{2,1},{3,4},{4,3},{5,6},{6,5},{7,8},{8,7},{9,10},{10,... | collective-permute-start | bytes 110600 | tf_op jit(solution)/shard_map/ppermute | solution.py:494
  5.2 1.9 %arrange.1 = (f32[96,96]{1,0:T(8,128)S(1)}, bf16[96,384]{1,0:T(8,128)(2,1)S(1)}, bf16[256,96]{1,0:T(8,128)(2,1)S(1)}, bf16[6,256,384]{2,1,0:T(8,128)(2,1)S(1)}, ...) custom-call(f32[96,96]{1,0:T(8,128)} %bitcast.6, ...), custom_call_target="tpu_custom_call" | custom-call | tf_op jit(solution)/shard_map/arrange/pallas_call | solution.py:497
  7.1 0.2 collective-permute-done.3.got_b
  7.3 1.5 %raise.1 = f32[8,32,384]{2,1,0:T(8,128)} custom-call(f32[96,96]{1,0:T(8,128)S(1)} %collective-permute-done.2.got_a, f32[96,96]{1,0:T(8,128)S(1)} %collective-permute-done.3.got_b, f32[96,96]{1,0:T(8,128)S(1)} %get-tuple-element.36.own, bf16[96,384]{1,0:T(8,128)(2,1)S(1)} %get-tuple-element.37.lon_up, bf16[256,96]{1,0:T(8,128)(2,1)S(1)} %get-tuple-element.38.mix, ...), custom_call_target="tpu_custom_call" | custom-call | tf_op jit(solution)/shard_map/raise/pallas_call | solution.py:454
  8.7 6.6 %all-to-all-start = ((f32[8,32,384]{2,1,0:T(8,128)}), f32[8,32,384]{2,1,0:T(8,128)S(1)}, u32[]{:S(2)}, u32[]{:S(2)}) async-start(f32[8,32,384]{2,1,0:T(8,128)} %raise.1), calls=%async_computation | async-start | bytes 786432 | tf_op jit(solution)/shard_map/all_to_all | solution.py:549
  15.4 2.1 %prepare.1 = (f32[32,1536]{1,0:T(8,128)S(1)}, bf16[16,8,1536]{2,1,0:T(8,128)(2,1)S(1)}, f32[64,1536]{1,0:T(8,128)}, f32[64,1536]{1,0:T(8,128)}) custom-call(s32[16]{0:T(128)S(1)} %copy-done.3, f32[16]{0:T(128)S(1)} %copy-done.4, bf16[8,16,1536]{2,1,0:T(8,128)(2,1)S(1)} %get-tuple-element.29.level_weight, f32[16,1536]{1,0:T(8,128)S(1)} %get-tuple-element.30.north, ...), custom_call_target="tpu_custom_call" | custom-call | tf_op jit(solution)/shard_map/prepare/pallas_call | solution.py:525
  17.5 2.9 %collective-permute-start.1 = (f32[64,1536]{1,0:T(8,128)}, f32[64,1536]{1,0:T(8,128)S(1)}, u32[]{:S(2)}, u32[]{:S(2)}) collective-permute-start(f32[64,1536]{1,0:T(8,128)} %get-tuple-element.35), channel_id=1, source_target_pairs={{0,15},{1,2},{2,1},{3,4},{4,3},{5,6},{6,5},{7,8},{8,7},{9,10},{10,... | collective-permute-start | bytes 1179656 | tf_op jit(solution)/shard_map/ppermute | solution.py:541
  20.4 4.2 %all-to-all-done.parts = f32[8,32,384]{2,1,0:T(8,128)S(1)} async-done(((f32[8,32,384]{2,1,0:T(8,128)}), f32[8,32,384]{2,1,0:T(8,128)S(1)}, u32[]{:S(2)}, u32[]{:S(2)}) %all-to-all-start) | async-done | bytes 393248 | tf_op jit(solution)/shard_map/all_to_all | solution.py:549
  24.7 0.1 collective-permute-start.4
  24.8 1.2 %collective-permute-done.4.mate = f32[32,384]{1,0:T(8,128)S(1)} collective-permute-done((f32[32,384]{1,0:T(8,128)S(1)}, f32[32,384]{1,0:T(8,128)S(1)}, u32[]{:S(2)}, u32[]{:S(2)}) %collective-permute-start.4) | collective-permute-done | bytes 49184 | tf_op jit(solution)/shard_map/ppermute | solution.py:551
  26.0 0.1 collective-permute-start.5
  26.1 2.6 %collective-permute-start.6 = (f32[64,384]{1,0:T(8,128)S(1)}, f32[64,384]{1,0:T(8,128)S(1)}, u32[]{:S(2)}, u32[]{:S(2)}) collective-permute-start(f32[64,384]{1,0:T(8,128)S(1)} %join.1), channel_id=1, source_target_pairs={{0,14},{1,15},{2,4},{3,5},{4,2},{5,3},{6,8},{7,9},{8,6},{9,7},{10,... | collective-permute-start | bytes 294920 | tf_op jit(solution)/shard_map/ppermute | solution.py:553
  28.7 0.4 assemble.1
  29.1 1.8 %collective-permute-done.5.near_pair = f32[64,384]{1,0:T(8,128)S(1)} collective-permute-done((f32[64,384]{1,0:T(8,128)S(1)}, f32[64,384]{1,0:T(8,128)S(1)}, u32[]{:S(2)}, u32[]{:S(2)}) %collective-permute-start.5) | collective-permute-done | bytes 98336 | tf_op jit(solution)/shard_map/ppermute | solution.py:554
  30.9 2.2 %collective-permute-done.6.far_pair = f32[64,384]{1,0:T(8,128)S(1)} collective-permute-done((f32[64,384]{1,0:T(8,128)S(1)}, f32[64,384]{1,0:T(8,128)S(1)}, u32[]{:S(2)}, u32[]{:S(2)}) %collective-permute-start.6) | collective-permute-done | bytes 98336 | tf_op jit(solution)/shard_map/ppermute | solution.py:553
  33.1 5.6 %fine.1 = (f32[32,384]{1,0:T(8,128)S(1)}, f32[32,384]{1,0:T(8,128)S(1)}, f32[32,384]{1,0:T(8,128)S(1)}) custom-call(s32[16]{0:T(128)S(1)} %copy-done.3, f32[16]{0:T(128)S(1)} %copy-done.4, f32[64,1536]{1,0:T(8,128)S(1)} %collective-permute-done.got_a.far_a, f32[64,1536]{1,0:T(8,128)S(1)} %collective-permute-done.1.got_b.far_b, f32[32,384]{1,0:T(8,128)S(1)} %total.1.mine.own, ...), custom_call_target="tpu_custom_call" | custom-call | tf_op jit(solution)/shard_map/fine/pallas_call | solution.py:563
  38.7 0.1 collective-permute-start.7
  38.8 2.9 %collective-permute-start.8 = (f32[32,384]{1,0:T(8,128)S(1)}, f32[32,384]{1,0:T(8,128)S(1)}, u32[]{:S(2)}, u32[]{:S(2)}) collective-permute-start(f32[32,384]{1,0:T(8,128)S(1)} %get-tuple-element.47), channel_id=1, source_target_pairs={{0,15},{1,2},{2,1},{3,4},{4,3},{5,6},{6,5},{7,8},{8,7},{9,10},{10,... | collective-permute-start | bytes 147464 | tf_op jit(solution)/shard_map/ppermute | solution.py:584
  41.6 2.8 %collective-permute-done.8.got_b = f32[32,384]{1,0:T(8,128)S(1)} collective-permute-done((f32[32,384]{1,0:T(8,128)S(1)}, f32[32,384]{1,0:T(8,128)S(1)}, u32[]{:S(2)}, u32[]{:S(2)}) %collective-permute-start.8) | collective-permute-done | bytes 49184 | tf_op jit(solution)/shard_map/ppermute | solution.py:584
  44.5 12.6 %all_to_all.10.adjoint = f32[8,32,384]{2,1,0:T(8,128)S(1)} all-to-all(f32[8,32,384]{2,1,0:T(8,128)S(1)} %copies.1), channel_id=1, replica_groups=mesh['mem'=8,'lat'=16] {'mem'}, dimensions={0} | all-to-all | bytes 786432 | tf_op jit(solution)/shard_map/all_to_all | solution.py:590
  57.1 0.8 %lower.1 = (f32[96,96]{1,0:T(8,128)S(1)}, f32[96,96]{1,0:T(8,128)S(1)}, f32[96,96]{1,0:T(8,128)S(1)}) custom-call(f32[96,96]{1,0:T(8,128)S(1)} %bitcast.7, bf16[6,256,384]{2,1,0:T(8,128)(2,1)S(1)} %get-tuple-element.28.pert, f32[8,32,384]{2,1,0:T(8,128)S(1)} %all_to_all.10.adjoint, bf16[48,256]{1,0:T(8,128)(2,1)S(1)} %copy-done.2, bf16[384,96]{1,0:T(8,128)(2,1)S(1)} %copy-done.1), custom_call_target="tpu_custom_call" | custom-call | tf_op jit(solution)/shard_map/lower/pallas_call | solution.py:454
  58.0 2.6 %collective-permute-start.10 = (f32[96,96]{1,0:T(8,128)S(1)}, f32[96,96]{1,0:T(8,128)S(1)}, u32[]{:S(2)}, u32[]{:S(2)}) collective-permute-start(f32[96,96]{1,0:T(8,128)S(1)} %get-tuple-element.50), channel_id=1, source_target_pairs={{0,15},{1,2},{2,1},{3,4},{4,3},{5,6},{6,5},{7,8},{8,7},{9,10},{10,... | collective-permute-start | bytes 110600 | tf_op jit(solution)/shard_map/ppermute | solution.py:596
  60.6 3.1 %collective-permute-done.10 = f32[96,96]{1,0:T(8,128)S(1)} collective-permute-done((f32[96,96]{1,0:T(8,128)S(1)}, f32[96,96]{1,0:T(8,128)S(1)}, u32[]{:S(2)}, u32[]{:S(2)}) %collective-permute-start.10) | collective-permute-done | bytes 36896 | tf_op jit(solution)/shard_map/ppermute | solution.py:596
  63.7 0.6 add_add_fusion
  (21 shorter events, 0.1 us)
Async XLA Ops:
  0.0 7.1 %collective-permute-start.2 = (f32[96,96]{1,0:T(8,128)}, f32[96,96]{1,0:T(8,128)S(1)}, u32[]{:S(2)}, u32[]{:S(2)}) collective-permute-start(f32[96,96]{1,0:T(8,128)} %bitcast.4), channel_id=1, source_target_pairs={{0,1},{1,0},{2,3},{3,2},{4,5},{5,4},{6,7},{7,6},{8,9},{9,8},{10,11... | collective-permute-start | bytes 110600 | tf_op jit(solution)/shard_map/ppermute | solution.py:494
  0.0 7.3 %collective-permute-start.3 = (f32[96,96]{1,0:T(8,128)}, f32[96,96]{1,0:T(8,128)S(1)}, u32[]{:S(2)}, u32[]{:S(2)}) collective-permute-start(f32[96,96]{1,0:T(8,128)} %bitcast.5), channel_id=1, source_target_pairs={{0,15},{1,2},{2,1},{3,4},{4,3},{5,6},{6,5},{7,8},{8,7},{9,10},{10,... | collective-permute-start | bytes 110600 | tf_op jit(solution)/shard_map/ppermute | solution.py:494
  7.1 8.3 %copy-start.3 = (s32[16]{0:T(128)S(1)}, s32[16]{0:T(128)}, u32[]{:S(2)}) copy-start(s32[16]{0:T(128)} %source_all.1) | copy-start | bytes 196
  7.1 8.3 %copy-start.4 = (f32[16]{0:T(128)S(1)}, f32[16]{0:T(128)}, u32[]{:S(2)}) copy-start(f32[16]{0:T(128)} %frac_all.1) | copy-start | bytes 196
  8.7 15.9 %all-to-all-start = ((f32[8,32,384]{2,1,0:T(8,128)}), f32[8,32,384]{2,1,0:T(8,128)S(1)}, u32[]{:S(2)}, u32[]{:S(2)}) async-start(f32[8,32,384]{2,1,0:T(8,128)} %raise.1), calls=%async_computation | async-start | bytes 786432 | tf_op jit(solution)/shard_map/all_to_all | solution.py:549
  17.5 11.1 %collective-permute-start = (f32[64,1536]{1,0:T(8,128)}, f32[64,1536]{1,0:T(8,128)S(1)}, u32[]{:S(2)}, u32[]{:S(2)}) collective-permute-start(f32[64,1536]{1,0:T(8,128)} %get-tuple-element.34), channel_id=1, source_target_pairs={{0,1},{1,0},{2,3},{3,2},{4,5},{5,4},{6,7},{7,6},{8,9},{9,8},{10,11... | collective-permute-start | bytes 1179656 | tf_op jit(solution)/shard_map/ppermute | solution.py:542
  17.5 11.1 %collective-permute-start.1 = (f32[64,1536]{1,0:T(8,128)}, f32[64,1536]{1,0:T(8,128)S(1)}, u32[]{:S(2)}, u32[]{:S(2)}) collective-permute-start(f32[64,1536]{1,0:T(8,128)} %get-tuple-element.35), channel_id=1, source_target_pairs={{0,15},{1,2},{2,1},{3,4},{4,3},{5,6},{6,5},{7,8},{8,7},{9,10},{10,... | collective-permute-start | bytes 1179656 | tf_op jit(solution)/shard_map/ppermute | solution.py:541
  24.7 1.3 %collective-permute-start.4 = (f32[32,384]{1,0:T(8,128)S(1)}, f32[32,384]{1,0:T(8,128)S(1)}, u32[]{:S(2)}, u32[]{:S(2)}) collective-permute-start(f32[32,384]{1,0:T(8,128)S(1)} %total.1.mine.own), channel_id=1, source_target_pairs={{0,1},{1,0},{2,3},{3,2},{4,5},{5,4},{6,7},{7,6},{8,9},{9,8},{10,11... | collective-permute-start | bytes 147464 | tf_op jit(solution)/shard_map/ppermute | solution.py:551
  26.0 4.9 %collective-permute-start.5 = (f32[64,384]{1,0:T(8,128)S(1)}, f32[64,384]{1,0:T(8,128)S(1)}, u32[]{:S(2)}, u32[]{:S(2)}) collective-permute-start(f32[64,384]{1,0:T(8,128)S(1)} %join.1), channel_id=1, source_target_pairs={{0,2},{1,3},{2,0},{3,1},{4,6},{5,7},{6,4},{7,5},{8,10},{9,11},{10,... | collective-permute-start | bytes 294920 | tf_op jit(solution)/shard_map/ppermute | solution.py:554
  26.1 7.0 %collective-permute-start.6 = (f32[64,384]{1,0:T(8,128)S(1)}, f32[64,384]{1,0:T(8,128)S(1)}, u32[]{:S(2)}, u32[]{:S(2)}) collective-permute-start(f32[64,384]{1,0:T(8,128)S(1)} %join.1), channel_id=1, source_target_pairs={{0,14},{1,15},{2,4},{3,5},{4,2},{5,3},{6,8},{7,9},{8,6},{9,7},{10,... | collective-permute-start | bytes 294920 | tf_op jit(solution)/shard_map/ppermute | solution.py:553
  33.1 24.0 %copy-start = (f32[6,16,1,96]{3,2,1,0:T(1,128)S(1)}, f32[6,16,1,96]{3,2,1,0:T(1,128)}, u32[]{:S(2)}) copy-start(f32[6,16,1,96]{3,2,1,0:T(1,128)} %param.13) | copy-start | bytes 110596
  33.1 24.0 %copy-start.1 = (bf16[384,96]{1,0:T(8,128)(2,1)S(1)}, bf16[384,96]{1,0:T(8,128)(2,1)}, u32[]{:S(2)}) copy-start(bf16[384,96]{1,0:T(8,128)(2,1)} %constant.13.clone.lon_down) | copy-start | bytes 221188
  33.1 24.0 %copy-start.2 = (bf16[48,256]{1,0:T(8,128)(2,1)S(1)}, bf16[48,256]{1,0:T(8,128)(2,1)}, u32[]{:S(2)}) copy-start(bf16[48,256]{1,0:T(8,128)(2,1)} %constant.15.clone.mix_t) | copy-start | bytes 73732
  38.7 3.0 %collective-permute-start.7 = (f32[32,384]{1,0:T(8,128)S(1)}, f32[32,384]{1,0:T(8,128)S(1)}, u32[]{:S(2)}, u32[]{:S(2)}) collective-permute-start(f32[32,384]{1,0:T(8,128)S(1)} %get-tuple-element.46), channel_id=1, source_target_pairs={{0,1},{1,0},{2,3},{3,2},{4,5},{5,4},{6,7},{7,6},{8,9},{9,8},{10,11... | collective-permute-start | bytes 147464 | tf_op jit(solution)/shard_map/ppermute | solution.py:585
  38.8 5.7 %collective-permute-start.8 = (f32[32,384]{1,0:T(8,128)S(1)}, f32[32,384]{1,0:T(8,128)S(1)}, u32[]{:S(2)}, u32[]{:S(2)}) collective-permute-start(f32[32,384]{1,0:T(8,128)S(1)} %get-tuple-element.47), channel_id=1, source_target_pairs={{0,15},{1,2},{2,1},{3,4},{4,3},{5,6},{6,5},{7,8},{8,7},{9,10},{10,... | collective-permute-start | bytes 147464 | tf_op jit(solution)/shard_map/ppermute | solution.py:584
  58.0 5.7 %collective-permute-start.10 = (f32[96,96]{1,0:T(8,128)S(1)}, f32[96,96]{1,0:T(8,128)S(1)}, u32[]{:S(2)}, u32[]{:S(2)}) collective-permute-start(f32[96,96]{1,0:T(8,128)S(1)} %get-tuple-element.50), channel_id=1, source_target_pairs={{0,15},{1,2},{2,1},{3,4},{4,3},{5,6},{6,5},{7,8},{8,7},{9,10},{10,... | collective-permute-start | bytes 110600 | tf_op jit(solution)/shard_map/ppermute | solution.py:596
  60.6 3.1 %collective-permute-start.9 = (f32[96,96]{1,0:T(8,128)S(1)}, f32[96,96]{1,0:T(8,128)S(1)}, u32[]{:S(2)}, u32[]{:S(2)}) collective-permute-start(f32[96,96]{1,0:T(8,128)S(1)} %get-tuple-element.49), channel_id=1, source_target_pairs={{0,1},{1,0},{2,3},{3,2},{4,5},{5,4},{6,7},{7,6},{8,9},{9,8},{10,11... | collective-permute-start | bytes 110600 | tf_op jit(solution)/shard_map/ppermute | solution.py:597

commit v6 on v5

--- a/solution.py
+++ b/solution.py
@@ -363,17 +363,18 @@
         acc[s] += (1.0 - f) * g
         acc[s + 1] += f * g
 
-    def first_pass(_, carry):
-        sweep(1, n - 1, store)
-        return carry
-
-    def second_pass(_, carry):
-        sweep(PASSES + 1, n - PASSES - 1, store)
-        return carry
-
-    lax.fori_loop(0, PASSES - 1, first_pass, 0)
+    def twice(first, stop):
+        def one_pass(_, carry):
+            sweep(first, stop, store)
+            return carry
+
+        lax.fori_loop(0, 2, one_pass, 0)
+
+    twice(1, n - 1)
+    twice(3, n - 3)
     sweep(PASSES, n - PASSES, store_weighted)
-    lax.fori_loop(0, PASSES - 1, second_pass, 0)
+    twice(PASSES + 1, n - PASSES - 1)
+    twice(PASSES + 3, n - PASSES - 3)
     sweep(HALO, HALO + rows, spread)
     for k in range(band):
         keep[8 * k : 8 * k + 8, :] = acc[band + k]

time: 64.6 us -> 64.3 us (level)
  no operation moved by 1% of the time
where the time goes in v6:
time: 64.3 us; the launch traced here: 64.1 us
  starting transfers between devices  23.1 us (36%)
  waiting for transfers between devices  15.5 us (24%)
  blocking collectives  12.6 us (20%)
  Pallas kernels  12.1 us (19%)
    all_to_all x1, blocking collectives, body(): adjoint = lax.all_to_all(copies, 'mem', 0, 0, tiled=True)  12.6 us
    all_to_all x1, starting transfers between devices, body(): parts = lax.all_to_all(local_sum, 'mem', 0, 0, tiled=True)  6.64 us
    ppermute x2, waiting for transfers between devices, body(): got_b = lax.ppermute(send_b, 'lat', across)  5.89 us
    ppermute x2, starting transfers between devices, body(): got_b = lax.ppermute(send_b, 'lat', across)  5.51 us
    pallas_call x1, Pallas kernels, body(): pl.pallas_call(fine_kernel, name='fine', out_shape=[piece] * 3, in_specs=...  5.32 us
    ppermute x1, starting transfers between devices, body(): lax.ppermute(own, 'lat', across)  5.19 us
    all_to_all x1, waiting for transfers between devices, body(): parts = lax.all_to_all(local_sum, 'mem', 0, 0, tiled=True)  4.21 us
    ppermute x1, starting transfers between devices, body(): far_b = lax.ppermute(buf_b, 'lat', across)  2.89 us
  transfers between devices with their start and end apart: 12, of which 7 were waited for; matrix products, arithmetic and copies ran while one was open for 0% of the time, Pallas kernels for 7%

profile of v6, /device:TPU:0, one launch (start us, length us, event | category | flops | bytes accessed | tf_op | source)
XLA Modules:
  0.0 64.1 jit_solution(10655192118787093427)
XLA Ops:
  0.0 5.2 %collective-permute-start.3 = (f32[96,96]{1,0:T(8,128)}, f32[96,96]{1,0:T(8,128)S(1)}, u32[]{:S(2)}, u32[]{:S(2)}) collective-permute-start(f32[96,96]{1,0:T(8,128)} %bitcast.5), channel_id=1, source_target_pairs={{0,15},{1,2},{2,1},{3,4},{4,3},{5,6},{6,5},{7,8},{8,7},{9,10},{10,... | collective-permute-start | bytes 110600 | tf_op jit(solution)/shard_map/ppermute | solution.py:495
  5.2 1.9 %arrange.1 = (f32[96,96]{1,0:T(8,128)S(1)}, bf16[96,384]{1,0:T(8,128)(2,1)S(1)}, bf16[256,96]{1,0:T(8,128)(2,1)S(1)}, bf16[6,256,384]{2,1,0:T(8,128)(2,1)S(1)}, ...) custom-call(f32[96,96]{1,0:T(8,128)} %bitcast.6, ...), custom_call_target="tpu_custom_call" | custom-call | tf_op jit(solution)/shard_map/arrange/pallas_call | solution.py:498
  7.1 0.2 collective-permute-done.3.got_b
  7.3 1.5 %raise.1 = f32[8,32,384]{2,1,0:T(8,128)} custom-call(f32[96,96]{1,0:T(8,128)S(1)} %collective-permute-done.2.got_a, f32[96,96]{1,0:T(8,128)S(1)} %collective-permute-done.3.got_b, f32[96,96]{1,0:T(8,128)S(1)} %get-tuple-element.36.own, bf16[96,384]{1,0:T(8,128)(2,1)S(1)} %get-tuple-element.37.lon_up, bf16[256,96]{1,0:T(8,128)(2,1)S(1)} %get-tuple-element.38.mix, ...), custom_call_target="tpu_custom_call" | custom-call | tf_op jit(solution)/shard_map/raise/pallas_call | solution.py:455
  8.7 6.6 %all-to-all-start = ((f32[8,32,384]{2,1,0:T(8,128)}), f32[8,32,384]{2,1,0:T(8,128)S(1)}, u32[]{:S(2)}, u32[]{:S(2)}) async-start(f32[8,32,384]{2,1,0:T(8,128)} %raise.1), calls=%async_computation | async-start | bytes 786432 | tf_op jit(solution)/shard_map/all_to_all | solution.py:550
  15.4 2.1 %prepare.1 = (f32[32,1536]{1,0:T(8,128)S(1)}, bf16[16,8,1536]{2,1,0:T(8,128)(2,1)S(1)}, f32[64,1536]{1,0:T(8,128)}, f32[64,1536]{1,0:T(8,128)}) custom-call(s32[16]{0:T(128)S(1)} %copy-done.3, f32[16]{0:T(128)S(1)} %copy-done.4, bf16[8,16,1536]{2,1,0:T(8,128)(2,1)S(1)} %get-tuple-element.29.level_weight, f32[16,1536]{1,0:T(8,128)S(1)} %get-tuple-element.30.north, ...), custom_call_target="tpu_custom_call" | custom-call | tf_op jit(solution)/shard_map/prepare/pallas_call | solution.py:526
  17.5 2.9 %collective-permute-start.1 = (f32[64,1536]{1,0:T(8,128)}, f32[64,1536]{1,0:T(8,128)S(1)}, u32[]{:S(2)}, u32[]{:S(2)}) collective-permute-start(f32[64,1536]{1,0:T(8,128)} %get-tuple-element.35), channel_id=1, source_target_pairs={{0,15},{1,2},{2,1},{3,4},{4,3},{5,6},{6,5},{7,8},{8,7},{9,10},{10,... | collective-permute-start | bytes 1179656 | tf_op jit(solution)/shard_map/ppermute | solution.py:542
  20.4 4.2 %all-to-all-done.parts = f32[8,32,384]{2,1,0:T(8,128)S(1)} async-done(((f32[8,32,384]{2,1,0:T(8,128)}), f32[8,32,384]{2,1,0:T(8,128)S(1)}, u32[]{:S(2)}, u32[]{:S(2)}) %all-to-all-start) | async-done | bytes 393248 | tf_op jit(solution)/shard_map/all_to_all | solution.py:550
  24.7 0.1 collective-permute-start.4
  24.8 1.2 %collective-permute-done.4.mate = f32[32,384]{1,0:T(8,128)S(1)} collective-permute-done((f32[32,384]{1,0:T(8,128)S(1)}, f32[32,384]{1,0:T(8,128)S(1)}, u32[]{:S(2)}, u32[]{:S(2)}) %collective-permute-start.4) | collective-permute-done | bytes 49184 | tf_op jit(solution)/shard_map/ppermute | solution.py:552
  26.0 0.1 collective-permute-start.5
  26.1 2.6 %collective-permute-start.6 = (f32[64,384]{1,0:T(8,128)S(1)}, f32[64,384]{1,0:T(8,128)S(1)}, u32[]{:S(2)}, u32[]{:S(2)}) collective-permute-start(f32[64,384]{1,0:T(8,128)S(1)} %join.1), channel_id=1, source_target_pairs={{0,14},{1,15},{2,4},{3,5},{4,2},{5,3},{6,8},{7,9},{8,6},{9,7},{10,... | collective-permute-start | bytes 294920 | tf_op jit(solution)/shard_map/ppermute | solution.py:554
  28.7 0.4 assemble.1
  29.1 1.8 %collective-permute-done.5.near_pair = f32[64,384]{1,0:T(8,128)S(1)} collective-permute-done((f32[64,384]{1,0:T(8,128)S(1)}, f32[64,384]{1,0:T(8,128)S(1)}, u32[]{:S(2)}, u32[]{:S(2)}) %collective-permute-start.5) | collective-permute-done | bytes 98336 | tf_op jit(solution)/shard_map/ppermute | solution.py:555
  30.9 2.2 %collective-permute-done.6.far_pair = f32[64,384]{1,0:T(8,128)S(1)} collective-permute-done((f32[64,384]{1,0:T(8,128)S(1)}, f32[64,384]{1,0:T(8,128)S(1)}, u32[]{:S(2)}, u32[]{:S(2)}) %collective-permute-start.6) | collective-permute-done | bytes 98336 | tf_op jit(solution)/shard_map/ppermute | solution.py:554
  33.1 5.3 %fine.1 = (f32[32,384]{1,0:T(8,128)S(1)}, f32[32,384]{1,0:T(8,128)S(1)}, f32[32,384]{1,0:T(8,128)S(1)}) custom-call(s32[16]{0:T(128)S(1)} %copy-done.3, f32[16]{0:T(128)S(1)} %copy-done.4, f32[64,1536]{1,0:T(8,128)S(1)} %collective-permute-done.got_a.far_a, f32[64,1536]{1,0:T(8,128)S(1)} %collective-permute-done.1.got_b.far_b, f32[32,384]{1,0:T(8,128)S(1)} %total.1.mine.own, ...), custom_call_target="tpu_custom_call" | custom-call | tf_op jit(solution)/shard_map/fine/pallas_call | solution.py:564
  38.4 0.1 collective-permute-start.7
  38.5 2.9 %collective-permute-start.8 = (f32[32,384]{1,0:T(8,128)S(1)}, f32[32,384]{1,0:T(8,128)S(1)}, u32[]{:S(2)}, u32[]{:S(2)}) collective-permute-start(f32[32,384]{1,0:T(8,128)S(1)} %get-tuple-element.47), channel_id=1, source_target_pairs={{0,15},{1,2},{2,1},{3,4},{4,3},{5,6},{6,5},{7,8},{8,7},{9,10},{10,... | collective-permute-start | bytes 147464 | tf_op jit(solution)/shard_map/ppermute | solution.py:585
  41.4 2.8 %collective-permute-done.8.got_b = f32[32,384]{1,0:T(8,128)S(1)} collective-permute-done((f32[32,384]{1,0:T(8,128)S(1)}, f32[32,384]{1,0:T(8,128)S(1)}, u32[]{:S(2)}, u32[]{:S(2)}) %collective-permute-start.8) | collective-permute-done | bytes 49184 | tf_op jit(solution)/shard_map/ppermute | solution.py:585
  44.3 12.6 %all_to_all.10.adjoint = f32[8,32,384]{2,1,0:T(8,128)S(1)} all-to-all(f32[8,32,384]{2,1,0:T(8,128)S(1)} %copies.1), channel_id=1, replica_groups=mesh['mem'=8,'lat'=16] {'mem'}, dimensions={0} | all-to-all | bytes 786432 | tf_op jit(solution)/shard_map/all_to_all | solution.py:591
  56.9 0.8 %lower.1 = (f32[96,96]{1,0:T(8,128)S(1)}, f32[96,96]{1,0:T(8,128)S(1)}, f32[96,96]{1,0:T(8,128)S(1)}) custom-call(f32[96,96]{1,0:T(8,128)S(1)} %bitcast.7, bf16[6,256,384]{2,1,0:T(8,128)(2,1)S(1)} %get-tuple-element.28.pert, f32[8,32,384]{2,1,0:T(8,128)S(1)} %all_to_all.10.adjoint, bf16[48,256]{1,0:T(8,128)(2,1)S(1)} %copy-done.2, bf16[384,96]{1,0:T(8,128)(2,1)S(1)} %copy-done.1), custom_call_target="tpu_custom_call" | custom-call | tf_op jit(solution)/shard_map/lower/pallas_call | solution.py:455
  57.7 2.6 %collective-permute-start.10 = (f32[96,96]{1,0:T(8,128)S(1)}, f32[96,96]{1,0:T(8,128)S(1)}, u32[]{:S(2)}, u32[]{:S(2)}) collective-permute-start(f32[96,96]{1,0:T(8,128)S(1)} %get-tuple-element.50), channel_id=1, source_target_pairs={{0,15},{1,2},{2,1},{3,4},{4,3},{5,6},{6,5},{7,8},{8,7},{9,10},{10,... | collective-permute-start | bytes 110600 | tf_op jit(solution)/shard_map/ppermute | solution.py:597
  60.4 3.1 %collective-permute-done.10 = f32[96,96]{1,0:T(8,128)S(1)} collective-permute-done((f32[96,96]{1,0:T(8,128)S(1)}, f32[96,96]{1,0:T(8,128)S(1)}, u32[]{:S(2)}, u32[]{:S(2)}) %collective-permute-start.10) | collective-permute-done | bytes 36896 | tf_op jit(solution)/shard_map/ppermute | solution.py:597
  63.4 0.6 add_add_fusion
  (21 shorter events, 0.1 us)
Async XLA Ops:
  0.0 7.1 %collective-permute-start.2 = (f32[96,96]{1,0:T(8,128)}, f32[96,96]{1,0:T(8,128)S(1)}, u32[]{:S(2)}, u32[]{:S(2)}) collective-permute-start(f32[96,96]{1,0:T(8,128)} %bitcast.4), channel_id=1, source_target_pairs={{0,1},{1,0},{2,3},{3,2},{4,5},{5,4},{6,7},{7,6},{8,9},{9,8},{10,11... | collective-permute-start | bytes 110600 | tf_op jit(solution)/shard_map/ppermute | solution.py:495
  0.0 7.3 %collective-permute-start.3 = (f32[96,96]{1,0:T(8,128)}, f32[96,96]{1,0:T(8,128)S(1)}, u32[]{:S(2)}, u32[]{:S(2)}) collective-permute-start(f32[96,96]{1,0:T(8,128)} %bitcast.5), channel_id=1, source_target_pairs={{0,15},{1,2},{2,1},{3,4},{4,3},{5,6},{6,5},{7,8},{8,7},{9,10},{10,... | collective-permute-start | bytes 110600 | tf_op jit(solution)/shard_map/ppermute | solution.py:495
  7.1 8.3 %copy-start.3 = (s32[16]{0:T(128)S(1)}, s32[16]{0:T(128)}, u32[]{:S(2)}) copy-start(s32[16]{0:T(128)} %source_all.1) | copy-start | bytes 196
  7.1 8.3 %copy-start.4 = (f32[16]{0:T(128)S(1)}, f32[16]{0:T(128)}, u32[]{:S(2)}) copy-start(f32[16]{0:T(128)} %frac_all.1) | copy-start | bytes 196
  8.7 15.9 %all-to-all-start = ((f32[8,32,384]{2,1,0:T(8,128)}), f32[8,32,384]{2,1,0:T(8,128)S(1)}, u32[]{:S(2)}, u32[]{:S(2)}) async-start(f32[8,32,384]{2,1,0:T(8,128)} %raise.1), calls=%async_computation | async-start | bytes 786432 | tf_op jit(solution)/shard_map/all_to_all | solution.py:550
  17.5 11.1 %collective-permute-start = (f32[64,1536]{1,0:T(8,128)}, f32[64,1536]{1,0:T(8,128)S(1)}, u32[]{:S(2)}, u32[]{:S(2)}) collective-permute-start(f32[64,1536]{1,0:T(8,128)} %get-tuple-element.34), channel_id=1, source_target_pairs={{0,1},{1,0},{2,3},{3,2},{4,5},{5,4},{6,7},{7,6},{8,9},{9,8},{10,11... | collective-permute-start | bytes 1179656 | tf_op jit(solution)/shard_map/ppermute | solution.py:543
  17.5 11.1 %collective-permute-start.1 = (f32[64,1536]{1,0:T(8,128)}, f32[64,1536]{1,0:T(8,128)S(1)}, u32[]{:S(2)}, u32[]{:S(2)}) collective-permute-start(f32[64,1536]{1,0:T(8,128)} %get-tuple-element.35), channel_id=1, source_target_pairs={{0,15},{1,2},{2,1},{3,4},{4,3},{5,6},{6,5},{7,8},{8,7},{9,10},{10,... | collective-permute-start | bytes 1179656 | tf_op jit(solution)/shard_map/ppermute | solution.py:542
  24.7 1.3 %collective-permute-start.4 = (f32[32,384]{1,0:T(8,128)S(1)}, f32[32,384]{1,0:T(8,128)S(1)}, u32[]{:S(2)}, u32[]{:S(2)}) collective-permute-start(f32[32,384]{1,0:T(8,128)S(1)} %total.1.mine.own), channel_id=1, source_target_pairs={{0,1},{1,0},{2,3},{3,2},{4,5},{5,4},{6,7},{7,6},{8,9},{9,8},{10,11... | collective-permute-start | bytes 147464 | tf_op jit(solution)/shard_map/ppermute | solution.py:552
  26.0 4.9 %collective-permute-start.5 = (f32[64,384]{1,0:T(8,128)S(1)}, f32[64,384]{1,0:T(8,128)S(1)}, u32[]{:S(2)}, u32[]{:S(2)}) collective-permute-start(f32[64,384]{1,0:T(8,128)S(1)} %join.1), channel_id=1, source_target_pairs={{0,2},{1,3},{2,0},{3,1},{4,6},{5,7},{6,4},{7,5},{8,10},{9,11},{10,... | collective-permute-start | bytes 294920 | tf_op jit(solution)/shard_map/ppermute | solution.py:555
  26.1 7.0 %collective-permute-start.6 = (f32[64,384]{1,0:T(8,128)S(1)}, f32[64,384]{1,0:T(8,128)S(1)}, u32[]{:S(2)}, u32[]{:S(2)}) collective-permute-start(f32[64,384]{1,0:T(8,128)S(1)} %join.1), channel_id=1, source_target_pairs={{0,14},{1,15},{2,4},{3,5},{4,2},{5,3},{6,8},{7,9},{8,6},{9,7},{10,... | collective-permute-start | bytes 294920 | tf_op jit(solution)/shard_map/ppermute | solution.py:554
  33.1 23.8 %copy-start = (f32[6,16,1,96]{3,2,1,0:T(1,128)S(1)}, f32[6,16,1,96]{3,2,1,0:T(1,128)}, u32[]{:S(2)}) copy-start(f32[6,16,1,96]{3,2,1,0:T(1,128)} %param.13) | copy-start | bytes 110596
  33.1 23.8 %copy-start.1 = (bf16[384,96]{1,0:T(8,128)(2,1)S(1)}, bf16[384,96]{1,0:T(8,128)(2,1)}, u32[]{:S(2)}) copy-start(bf16[384,96]{1,0:T(8,128)(2,1)} %constant.13.clone.lon_down) | copy-start | bytes 221188
  33.1 23.8 %copy-start.2 = (bf16[48,256]{1,0:T(8,128)(2,1)S(1)}, bf16[48,256]{1,0:T(8,128)(2,1)}, u32[]{:S(2)}) copy-start(bf16[48,256]{1,0:T(8,128)(2,1)} %constant.15.clone.mix_t) | copy-start | bytes 73732
  38.4 3.0 %collective-permute-start.7 = (f32[32,384]{1,0:T(8,128)S(1)}, f32[32,384]{1,0:T(8,128)S(1)}, u32[]{:S(2)}, u32[]{:S(2)}) collective-permute-start(f32[32,384]{1,0:T(8,128)S(1)} %get-tuple-element.46), channel_id=1, source_target_pairs={{0,1},{1,0},{2,3},{3,2},{4,5},{5,4},{6,7},{7,6},{8,9},{9,8},{10,11... | collective-permute-start | bytes 147464 | tf_op jit(solution)/shard_map/ppermute | solution.py:586
  38.5 5.7 %collective-permute-start.8 = (f32[32,384]{1,0:T(8,128)S(1)}, f32[32,384]{1,0:T(8,128)S(1)}, u32[]{:S(2)}, u32[]{:S(2)}) collective-permute-start(f32[32,384]{1,0:T(8,128)S(1)} %get-tuple-element.47), channel_id=1, source_target_pairs={{0,15},{1,2},{2,1},{3,4},{4,3},{5,6},{6,5},{7,8},{8,7},{9,10},{10,... | collective-permute-start | bytes 147464 | tf_op jit(solution)/shard_map/ppermute | solution.py:585
  57.7 5.7 %collective-permute-start.10 = (f32[96,96]{1,0:T(8,128)S(1)}, f32[96,96]{1,0:T(8,128)S(1)}, u32[]{:S(2)}, u32[]{:S(2)}) collective-permute-start(f32[96,96]{1,0:T(8,128)S(1)} %get-tuple-element.50), channel_id=1, source_target_pairs={{0,15},{1,2},{2,1},{3,4},{4,3},{5,6},{6,5},{7,8},{8,7},{9,10},{10,... | collective-permute-start | bytes 110600 | tf_op jit(solution)/shard_map/ppermute | solution.py:597
  60.4 3.1 %collective-permute-start.9 = (f32[96,96]{1,0:T(8,128)S(1)}, f32[96,96]{1,0:T(8,128)S(1)}, u32[]{:S(2)}, u32[]{:S(2)}) collective-permute-start(f32[96,96]{1,0:T(8,128)S(1)} %get-tuple-element.49), channel_id=1, source_target_pairs={{0,1},{1,0},{2,3},{3,2},{4,5},{5,4},{6,7},{7,6},{8,9},{9,8},{10,11... | collective-permute-start | bytes 110600 | tf_op jit(solution)/shard_map/ppermute | solution.py:598

commit v7 on v6

--- a/solution.py
+++ b/solution.py
@@ -45,7 +45,7 @@
 
 
 def prepare_kernel(
-    source, frac, level_weight, north, east, select, order,
+    source, frac, level_weight, north, east, order,
     coef, own_weight, buf_a, buf_b, extra,
 ):
     _, odd, _ = position()
@@ -65,9 +65,12 @@
     values = dot(order[...], level_weight[...].reshape(levels * rows, lon)).astype(BF16)
     everything = jnp.concatenate([values, hi, mid, low], axis=0)
     many = levels * rows
+    entry = lax.broadcasted_iota(jnp.int32, (512, 512), 0)
+    place = lax.broadcasted_iota(jnp.int32, (512, 512), 1)
+    select = jnp.where(entry == 4 * (place & 127) + (place >> 7), 1.0, 0.0).astype(BF16)
     quarter = lon // 4
     for c in range(lon // 512):
-        moved = dot(everything[:, 512 * c : 512 * c + 512], select[...])
+        moved = dot(everything[:, 512 * c : 512 * c + 512], select)
         wpart = moved[:many]
         cpart = moved[many : many + 2 * rows] + moved[many + 2 * rows : many + 4 * rows]
         cpart = cpart + moved[many + 4 * rows :]
@@ -137,8 +140,8 @@
 
 
 def arrange_kernel(
-    own_all, lon_all, mix_all, stored, weight_all, north_all, east_all, select_all, order_all,
-    own, lon_up, mix, pert, weight, north, east, select, order, raw, flat, sems,
+    own_all, lon_all, mix_all, stored, weight_all, north_all, east_all, order_all,
+    own, lon_up, mix, pert, weight, north, east, order, raw, flat, sems,
 ):
     members, levels, band, _ = raw.shape
     small = [
@@ -152,8 +155,7 @@
         pltpu.make_async_copy(levels_here, weight, sems.at[members + 3]),
         pltpu.make_async_copy(north_all, north, sems.at[members + 4]),
         pltpu.make_async_copy(east_all, east, sems.at[members + 5]),
-        pltpu.make_async_copy(select_all, select, sems.at[members + 6]),
-        pltpu.make_async_copy(order_all, order, sems.at[members + 7]),
+        pltpu.make_async_copy(order_all, order, sems.at[members + 6]),
     ]
     for copy in copies + small:
         copy.start()
@@ -483,11 +485,6 @@
     lon_down = jnp.asarray(lon_refine, BF16)
     mix_up = jnp.asarray(np.concatenate([mix, mix], axis=1), BF16)
     mix_down = jnp.asarray(mix.T, BF16)
-    pick = np.zeros((512, 512), np.float32)
-    for r in range(4):
-        for q in range(128):
-            pick[4 * q + r, 128 * r + q] = 1.0
-    pick = jnp.asarray(pick, BF16)
     order = np.eye(part * rows).reshape(part, rows, part, rows).transpose(1, 0, 2, 3)
     order = jnp.asarray(order.reshape(part * rows, part * rows), BF16)
 
@@ -506,20 +503,19 @@
             jax.ShapeDtypeStruct((part, rows, fine_lon), BF16),
             jax.ShapeDtypeStruct((rows, fine_lon), F32),
             jax.ShapeDtypeStruct((rows, fine_lon), F32),
-            jax.ShapeDtypeStruct(pick.shape, BF16),
             jax.ShapeDtypeStruct(order.shape, BF16),
         ],
-        in_specs=[anywhere()] * 9,
-        out_specs=[vmem()] * 9,
+        in_specs=[anywhere()] * 8,
+        out_specs=[vmem()] * 8,
         scratch_shapes=[
             pltpu.VMEM((members, lev, band, lon), BF16),
             pltpu.VMEM((members, lev * band, lon), F32),
-            pltpu.SemaphoreType.DMA((members + 8,)),
+            pltpu.SemaphoreType.DMA((members + 7,)),
         ],
         compiler_params=pltpu.CompilerParams(vmem_limit_bytes=VMEM_LIMIT),
     )(
         *[in_hbm(x) for x in (own, lon_up, mix_up, perturbations)],
-        *[in_hbm(x) for x in (precision_weight, north_coef, east_coef, pick, order)],
+        *[in_hbm(x) for x in (precision_weight, north_coef, east_coef, order)],
     )
 
     spots = 8 * PASSES + 2 * HALO + 4
@@ -532,7 +528,7 @@
             jax.ShapeDtypeStruct((spots, fine_lon), F32),
             jax.ShapeDtypeStruct((spots, fine_lon), F32),
         ],
-        in_specs=[smem()] * 2 + [vmem()] * 5,
+        in_specs=[smem()] * 2 + [vmem()] * 4,
         out_specs=[vmem()] * 4,
         scratch_shapes=[pltpu.VMEM((4, fine_lon), F32)],
         compiler_params=pltpu.CompilerParams(vmem_limit_bytes=VMEM_LIMIT),

time: 64.3 us -> 64.3 us (level)
  transfers between devices with their start and end apart: 12 -> 12, of which waited for: 7 -> 7; matrix products, arithmetic and copies ran while one was open for 0% -> 0% of each run, Pallas kernels for 7% -> 6%
where the time goes in v7:
time: 64.3 us; the launch traced here: 64.1 us
  starting transfers between devices  22.7 us (35%)
  waiting for transfers between devices  16.1 us (25%)
  blocking collectives  12.6 us (20%)
  Pallas kernels  11.8 us (18%)
    all_to_all x1, blocking collectives, body(): adjoint = lax.all_to_all(copies, 'mem', 0, 0, tiled=True)  12.6 us
    all_to_all x1, starting transfers between devices, body(): parts = lax.all_to_all(local_sum, 'mem', 0, 0, tiled=True)  6.64 us
    ppermute x2, waiting for transfers between devices, body(): got_b = lax.ppermute(send_b, 'lat', across)  6.24 us
    pallas_call x1, Pallas kernels, body(): pl.pallas_call(fine_kernel, name='fine', out_shape=[piece] * 3, in_specs=...  5.33 us
    ppermute x1, starting transfers between devices, body(): lax.ppermute(own, 'lat', across)  5.19 us
    ppermute x2, starting transfers between devices, body(): got_b = lax.ppermute(send_b, 'lat', across)  5.16 us
    all_to_all x1, waiting for transfers between devices, body(): parts = lax.all_to_all(local_sum, 'mem', 0, 0, tiled=True)  4.32 us
    ppermute x1, starting transfers between devices, body(): far_b = lax.ppermute(buf_b, 'lat', across)  2.9 us
  transfers between devices with their start and end apart: 12, of which 7 were waited for; matrix products, arithmetic and copies ran while one was open for 0% of the time, Pallas kernels for 6%

profile of v7, /device:TPU:0, one launch (start us, length us, event | category | flops | bytes accessed | tf_op | source)
XLA Modules:
  0.0 64.1 jit_solution(9858208238798675108)
XLA Ops:
  0.0 5.2 %collective-permute-start.3 = (f32[96,96]{1,0:T(8,128)}, f32[96,96]{1,0:T(8,128)S(1)}, u32[]{:S(2)}, u32[]{:S(2)}) collective-permute-start(f32[96,96]{1,0:T(8,128)} %bitcast.5), channel_id=1, source_target_pairs={{0,15},{1,2},{2,1},{3,4},{4,3},{5,6},{6,5},{7,8},{8,7},{9,10},{10,... | collective-permute-start | bytes 110600 | tf_op jit(solution)/shard_map/ppermute | solution.py:492
  5.2 1.7 %arrange.1 = (f32[96,96]{1,0:T(8,128)S(1)}, bf16[96,384]{1,0:T(8,128)(2,1)S(1)}, bf16[256,96]{1,0:T(8,128)(2,1)S(1)}, bf16[6,256,384]{2,1,0:T(8,128)(2,1)S(1)}, ...) custom-call(f32[96,96]{1,0:T(8,128)} %bitcast.6, ...), custom_call_target="tpu_custom_call" | custom-call | tf_op jit(solution)/shard_map/arrange/pallas_call | solution.py:495
  6.9 0.3 collective-permute-done.3.got_b
  7.3 1.5 %raise.1 = f32[8,32,384]{2,1,0:T(8,128)} custom-call(f32[96,96]{1,0:T(8,128)S(1)} %collective-permute-done.2.got_a, f32[96,96]{1,0:T(8,128)S(1)} %collective-permute-done.3.got_b, f32[96,96]{1,0:T(8,128)S(1)} %get-tuple-element.34.own, bf16[96,384]{1,0:T(8,128)(2,1)S(1)} %get-tuple-element.35.lon_up, bf16[256,96]{1,0:T(8,128)(2,1)S(1)} %get-tuple-element.36.mix, ...), custom_call_target="tpu_custom_call" | custom-call | tf_op jit(solution)/shard_map/raise/pallas_call | solution.py:457
  8.7 6.6 %all-to-all-start = ((f32[8,32,384]{2,1,0:T(8,128)}), f32[8,32,384]{2,1,0:T(8,128)S(1)}, u32[]{:S(2)}, u32[]{:S(2)}) async-start(f32[8,32,384]{2,1,0:T(8,128)} %raise.1), calls=%async_computation | async-start | bytes 786432 | tf_op jit(solution)/shard_map/all_to_all | solution.py:546
  15.4 2.0 %prepare.1 = (f32[32,1536]{1,0:T(8,128)S(1)}, bf16[16,8,1536]{2,1,0:T(8,128)(2,1)S(1)}, f32[64,1536]{1,0:T(8,128)}, f32[64,1536]{1,0:T(8,128)S(1)}) custom-call(s32[16]{0:T(128)S(1)} %copy-done.3, f32[16]{0:T(128)S(1)} %copy-done.4, bf16[8,16,1536]{2,1,0:T(8,128)(2,1)S(1)} %get-tuple-element.28.level_weight, f32[16,1536]{1,0:T(8,128)S(1)} %get-tuple-element.29.north, ...), custom_call_target="tpu_custom_call" | custom-call | tf_op jit(solution)/shard_map/prepare/pallas_call | solution.py:522
  17.4 2.9 %collective-permute-start.1 = (f32[64,1536]{1,0:T(8,128)S(1)}, f32[64,1536]{1,0:T(8,128)S(1)}, u32[]{:S(2)}, u32[]{:S(2)}) collective-permute-start(f32[64,1536]{1,0:T(8,128)S(1)} %get-tuple-element.33), channel_id=1, source_target_pairs={{0,15},{1,2},{2,1},{3,4},{4,3},{5,6},{6,5},{7,8},{8,7},{9,10},{10,... | collective-permute-start | bytes 1179656 | tf_op jit(solution)/shard_map/ppermute | solution.py:538
  20.3 4.3 %all-to-all-done.parts = f32[8,32,384]{2,1,0:T(8,128)S(1)} async-done(((f32[8,32,384]{2,1,0:T(8,128)}), f32[8,32,384]{2,1,0:T(8,128)S(1)}, u32[]{:S(2)}, u32[]{:S(2)}) %all-to-all-start) | async-done | bytes 393248 | tf_op jit(solution)/shard_map/all_to_all | solution.py:546
  24.7 0.1 collective-permute-start.4
  24.8 1.2 %collective-permute-done.4.mate = f32[32,384]{1,0:T(8,128)S(1)} collective-permute-done((f32[32,384]{1,0:T(8,128)S(1)}, f32[32,384]{1,0:T(8,128)S(1)}, u32[]{:S(2)}, u32[]{:S(2)}) %collective-permute-start.4) | collective-permute-done | bytes 49184 | tf_op jit(solution)/shard_map/ppermute | solution.py:548
  26.0 0.1 collective-permute-start.5
  26.1 2.6 %collective-permute-start.6 = (f32[64,384]{1,0:T(8,128)S(1)}, f32[64,384]{1,0:T(8,128)S(1)}, u32[]{:S(2)}, u32[]{:S(2)}) collective-permute-start(f32[64,384]{1,0:T(8,128)S(1)} %join.1), channel_id=1, source_target_pairs={{0,14},{1,15},{2,4},{3,5},{4,2},{5,3},{6,8},{7,9},{8,6},{9,7},{10,... | collective-permute-start | bytes 294920 | tf_op jit(solution)/shard_map/ppermute | solution.py:550
  28.7 0.4 assemble.1
  29.1 1.8 %collective-permute-done.5.near_pair = f32[64,384]{1,0:T(8,128)S(1)} collective-permute-done((f32[64,384]{1,0:T(8,128)S(1)}, f32[64,384]{1,0:T(8,128)S(1)}, u32[]{:S(2)}, u32[]{:S(2)}) %collective-permute-start.5) | collective-permute-done | bytes 98336 | tf_op jit(solution)/shard_map/ppermute | solution.py:551
  30.9 2.2 %collective-permute-done.6.far_pair = f32[64,384]{1,0:T(8,128)S(1)} collective-permute-done((f32[64,384]{1,0:T(8,128)S(1)}, f32[64,384]{1,0:T(8,128)S(1)}, u32[]{:S(2)}, u32[]{:S(2)}) %collective-permute-start.6) | collective-permute-done | bytes 98336 | tf_op jit(solution)/shard_map/ppermute | solution.py:550
  33.1 5.3 %fine.1 = (f32[32,384]{1,0:T(8,128)S(1)}, f32[32,384]{1,0:T(8,128)S(1)}, f32[32,384]{1,0:T(8,128)S(1)}) custom-call(s32[16]{0:T(128)S(1)} %copy-done.3, f32[16]{0:T(128)S(1)} %copy-done.4, f32[64,1536]{1,0:T(8,128)S(1)} %collective-permute-done.got_a.far_a, f32[64,1536]{1,0:T(8,128)S(1)} %collective-permute-done.1.got_b.far_b, f32[32,384]{1,0:T(8,128)S(1)} %total.1.mine.own, ...), custom_call_target="tpu_custom_call" | custom-call | tf_op jit(solution)/shard_map/fine/pallas_call | solution.py:560
  38.4 0.1 collective-permute-start.7
  38.5 2.9 %collective-permute-start.8 = (f32[32,384]{1,0:T(8,128)S(1)}, f32[32,384]{1,0:T(8,128)S(1)}, u32[]{:S(2)}, u32[]{:S(2)}) collective-permute-start(f32[32,384]{1,0:T(8,128)S(1)} %get-tuple-element.45), channel_id=1, source_target_pairs={{0,15},{1,2},{2,1},{3,4},{4,3},{5,6},{6,5},{7,8},{8,7},{9,10},{10,... | collective-permute-start | bytes 147464 | tf_op jit(solution)/shard_map/ppermute | solution.py:581
  41.4 2.8 %collective-permute-done.8.got_b = f32[32,384]{1,0:T(8,128)S(1)} collective-permute-done((f32[32,384]{1,0:T(8,128)S(1)}, f32[32,384]{1,0:T(8,128)S(1)}, u32[]{:S(2)}, u32[]{:S(2)}) %collective-permute-start.8) | collective-permute-done | bytes 49184 | tf_op jit(solution)/shard_map/ppermute | solution.py:581
  44.3 12.6 %all_to_all.10.adjoint = f32[8,32,384]{2,1,0:T(8,128)S(1)} all-to-all(f32[8,32,384]{2,1,0:T(8,128)S(1)} %copies.1), channel_id=1, replica_groups=mesh['mem'=8,'lat'=16] {'mem'}, dimensions={0} | all-to-all | bytes 786432 | tf_op jit(solution)/shard_map/all_to_all | solution.py:587
  56.9 0.8 %lower.1 = (f32[96,96]{1,0:T(8,128)S(1)}, f32[96,96]{1,0:T(8,128)S(1)}, f32[96,96]{1,0:T(8,128)S(1)}) custom-call(f32[96,96]{1,0:T(8,128)S(1)} %bitcast.7, bf16[6,256,384]{2,1,0:T(8,128)(2,1)S(1)} %get-tuple-element.27.pert, f32[8,32,384]{2,1,0:T(8,128)S(1)} %all_to_all.10.adjoint, bf16[48,256]{1,0:T(8,128)(2,1)S(1)} %copy-done.2, bf16[384,96]{1,0:T(8,128)(2,1)S(1)} %copy-done.1), custom_call_target="tpu_custom_call" | custom-call | tf_op jit(solution)/shard_map/lower/pallas_call | solution.py:457
  57.7 2.3 %collective-permute-start.10 = (f32[96,96]{1,0:T(8,128)S(1)}, f32[96,96]{1,0:T(8,128)S(1)}, u32[]{:S(2)}, u32[]{:S(2)}) collective-permute-start(f32[96,96]{1,0:T(8,128)S(1)} %get-tuple-element.48), channel_id=1, source_target_pairs={{0,15},{1,2},{2,1},{3,4},{4,3},{5,6},{6,5},{7,8},{8,7},{9,10},{10,... | collective-permute-start | bytes 110600 | tf_op jit(solution)/shard_map/ppermute | solution.py:593
  60.0 3.4 %collective-permute-done.10 = f32[96,96]{1,0:T(8,128)S(1)} collective-permute-done((f32[96,96]{1,0:T(8,128)S(1)}, f32[96,96]{1,0:T(8,128)S(1)}, u32[]{:S(2)}, u32[]{:S(2)}) %collective-permute-start.10) | collective-permute-done | bytes 36896 | tf_op jit(solution)/shard_map/ppermute | solution.py:593
  63.5 0.6 add_add_fusion
  (21 shorter events, 0.1 us)
Async XLA Ops:
  0.0 6.9 %collective-permute-start.2 = (f32[96,96]{1,0:T(8,128)}, f32[96,96]{1,0:T(8,128)S(1)}, u32[]{:S(2)}, u32[]{:S(2)}) collective-permute-start(f32[96,96]{1,0:T(8,128)} %bitcast.4), channel_id=1, source_target_pairs={{0,1},{1,0},{2,3},{3,2},{4,5},{5,4},{6,7},{7,6},{8,9},{9,8},{10,11... | collective-permute-start | bytes 110600 | tf_op jit(solution)/shard_map/ppermute | solution.py:492
  0.0 7.3 %collective-permute-start.3 = (f32[96,96]{1,0:T(8,128)}, f32[96,96]{1,0:T(8,128)S(1)}, u32[]{:S(2)}, u32[]{:S(2)}) collective-permute-start(f32[96,96]{1,0:T(8,128)} %bitcast.5), channel_id=1, source_target_pairs={{0,15},{1,2},{2,1},{3,4},{4,3},{5,6},{6,5},{7,8},{8,7},{9,10},{10,... | collective-permute-start | bytes 110600 | tf_op jit(solution)/shard_map/ppermute | solution.py:492
  6.9 8.5 %copy-start.3 = (s32[16]{0:T(128)S(1)}, s32[16]{0:T(128)}, u32[]{:S(2)}) copy-start(s32[16]{0:T(128)} %source_all.1) | copy-start | bytes 196
  6.9 8.5 %copy-start.4 = (f32[16]{0:T(128)S(1)}, f32[16]{0:T(128)}, u32[]{:S(2)}) copy-start(f32[16]{0:T(128)} %frac_all.1) | copy-start | bytes 196
  8.7 15.9 %all-to-all-start = ((f32[8,32,384]{2,1,0:T(8,128)}), f32[8,32,384]{2,1,0:T(8,128)S(1)}, u32[]{:S(2)}, u32[]{:S(2)}) async-start(f32[8,32,384]{2,1,0:T(8,128)} %raise.1), calls=%async_computation | async-start | bytes 786432 | tf_op jit(solution)/shard_map/all_to_all | solution.py:546
  17.4 11.2 %collective-permute-start = (f32[64,1536]{1,0:T(8,128)}, f32[64,1536]{1,0:T(8,128)S(1)}, u32[]{:S(2)}, u32[]{:S(2)}) collective-permute-start(f32[64,1536]{1,0:T(8,128)} %get-tuple-element.32), channel_id=1, source_target_pairs={{0,1},{1,0},{2,3},{3,2},{4,5},{5,4},{6,7},{7,6},{8,9},{9,8},{10,11... | collective-permute-start | bytes 1179656 | tf_op jit(solution)/shard_map/ppermute | solution.py:539
  17.4 11.2 %collective-permute-start.1 = (f32[64,1536]{1,0:T(8,128)S(1)}, f32[64,1536]{1,0:T(8,128)S(1)}, u32[]{:S(2)}, u32[]{:S(2)}) collective-permute-start(f32[64,1536]{1,0:T(8,128)S(1)} %get-tuple-element.33), channel_id=1, source_target_pairs={{0,15},{1,2},{2,1},{3,4},{4,3},{5,6},{6,5},{7,8},{8,7},{9,10},{10,... | collective-permute-start | bytes 1179656 | tf_op jit(solution)/shard_map/ppermute | solution.py:538
  24.7 1.3 %collective-permute-start.4 = (f32[32,384]{1,0:T(8,128)S(1)}, f32[32,384]{1,0:T(8,128)S(1)}, u32[]{:S(2)}, u32[]{:S(2)}) collective-permute-start(f32[32,384]{1,0:T(8,128)S(1)} %total.1.mine.own), channel_id=1, source_target_pairs={{0,1},{1,0},{2,3},{3,2},{4,5},{5,4},{6,7},{7,6},{8,9},{9,8},{10,11... | collective-permute-start | bytes 147464 | tf_op jit(solution)/shard_map/ppermute | solution.py:548
  26.0 4.9 %collective-permute-start.5 = (f32[64,384]{1,0:T(8,128)S(1)}, f32[64,384]{1,0:T(8,128)S(1)}, u32[]{:S(2)}, u32[]{:S(2)}) collective-permute-start(f32[64,384]{1,0:T(8,128)S(1)} %join.1), channel_id=1, source_target_pairs={{0,2},{1,3},{2,0},{3,1},{4,6},{5,7},{6,4},{7,5},{8,10},{9,11},{10,... | collective-permute-start | bytes 294920 | tf_op jit(solution)/shard_map/ppermute | solution.py:551
  26.1 7.0 %collective-permute-start.6 = (f32[64,384]{1,0:T(8,128)S(1)}, f32[64,384]{1,0:T(8,128)S(1)}, u32[]{:S(2)}, u32[]{:S(2)}) collective-permute-start(f32[64,384]{1,0:T(8,128)S(1)} %join.1), channel_id=1, source_target_pairs={{0,14},{1,15},{2,4},{3,5},{4,2},{5,3},{6,8},{7,9},{8,6},{9,7},{10,... | collective-permute-start | bytes 294920 | tf_op jit(solution)/shard_map/ppermute | solution.py:550
  33.1 23.8 %copy-start = (f32[6,16,1,96]{3,2,1,0:T(1,128)S(1)}, f32[6,16,1,96]{3,2,1,0:T(1,128)}, u32[]{:S(2)}) copy-start(f32[6,16,1,96]{3,2,1,0:T(1,128)} %param.12) | copy-start | bytes 110596
  33.1 23.8 %copy-start.1 = (bf16[384,96]{1,0:T(8,128)(2,1)S(1)}, bf16[384,96]{1,0:T(8,128)(2,1)}, u32[]{:S(2)}) copy-start(bf16[384,96]{1,0:T(8,128)(2,1)} %constant.11.clone.lon_down) | copy-start | bytes 221188
  33.1 23.8 %copy-start.2 = (bf16[48,256]{1,0:T(8,128)(2,1)S(1)}, bf16[48,256]{1,0:T(8,128)(2,1)}, u32[]{:S(2)}) copy-start(bf16[48,256]{1,0:T(8,128)(2,1)} %constant.13.clone.mix_t) | copy-start | bytes 73732
  38.4 3.0 %collective-permute-start.7 = (f32[32,384]{1,0:T(8,128)S(1)}, f32[32,384]{1,0:T(8,128)S(1)}, u32[]{:S(2)}, u32[]{:S(2)}) collective-permute-start(f32[32,384]{1,0:T(8,128)S(1)} %get-tuple-element.44), channel_id=1, source_target_pairs={{0,1},{1,0},{2,3},{3,2},{4,5},{5,4},{6,7},{7,6},{8,9},{9,8},{10,11... | collective-permute-start | bytes 147464 | tf_op jit(solution)/shard_map/ppermute | solution.py:582
  38.5 5.7 %collective-permute-start.8 = (f32[32,384]{1,0:T(8,128)S(1)}, f32[32,384]{1,0:T(8,128)S(1)}, u32[]{:S(2)}, u32[]{:S(2)}) collective-permute-start(f32[32,384]{1,0:T(8,128)S(1)} %get-tuple-element.45), channel_id=1, source_target_pairs={{0,15},{1,2},{2,1},{3,4},{4,3},{5,6},{6,5},{7,8},{8,7},{9,10},{10,... | collective-permute-start | bytes 147464 | tf_op jit(solution)/shard_map/ppermute | solution.py:581
  57.7 5.7 %collective-permute-start.10 = (f32[96,96]{1,0:T(8,128)S(1)}, f32[96,96]{1,0:T(8,128)S(1)}, u32[]{:S(2)}, u32[]{:S(2)}) collective-permute-start(f32[96,96]{1,0:T(8,128)S(1)} %get-tuple-element.48), channel_id=1, source_target_pairs={{0,15},{1,2},{2,1},{3,4},{4,3},{5,6},{6,5},{7,8},{8,7},{9,10},{10,... | collective-permute-start | bytes 110600 | tf_op jit(solution)/shard_map/ppermute | solution.py:593
  60.0 3.4 %collective-permute-start.9 = (f32[96,96]{1,0:T(8,128)S(1)}, f32[96,96]{1,0:T(8,128)S(1)}, u32[]{:S(2)}, u32[]{:S(2)}) collective-permute-start(f32[96,96]{1,0:T(8,128)S(1)} %get-tuple-element.47), channel_id=1, source_target_pairs={{0,1},{1,0},{2,3},{3,2},{4,5},{5,4},{6,7},{7,6},{8,9},{9,8},{10,11... | collective-permute-start | bytes 110600 | tf_op jit(solution)/shard_map/ppermute | solution.py:594
